TPU v7x, 8 devices: a whole 2x2x1 slice. The times are simulated.
8 devices in a mesh: dp: 2 (over z, y), sp: 4 (over x, core).
Axes of the slice: x: 2, y: 2, z: 1, core: 2. Of those that a mesh axis runs over, the one named last changes fastest.
Arguments:
- hidden: bfloat16 [8192, 3072], P(('dp', 'sp')), parts along dimension 0
- positions: int32 [8192], P(('dp', 'sp')), parts along dimension 0
- d_attn: bfloat16 [8192, 3072], P(('dp', 'sp')), parts along dimension 0
- ln_weight: bfloat16 [3072], replicated
- w_q: bfloat16 [3072, 3072], replicated
- w_k: bfloat16 [3072, 1024], replicated
- w_v: bfloat16 [3072, 1024], replicated
- w_o: bfloat16 [3072, 3072], replicated
Outputs:
- output 1: bfloat16 [8192, 3072], P(('dp', 'sp')), parts along dimension 0
- output 2: bfloat16 [8192, 3072], P(('dp', 'sp')), parts along dimension 0
- output 3: bfloat16 [6144], P('dp'), parts along dimension 0
- output 4: bfloat16 [6144, 3072], P('dp'), parts along dimension 0
- output 5: bfloat16 [6144, 1024], P('dp'), parts along dimension 0
- output 6: bfloat16 [6144, 1024], P('dp'), parts along dimension 0
- output 7: bfloat16 [6144, 3072], P('dp'), parts along dimension 0
There are 2 independent parts. A program takes and returns all parts, laid end to end along the dimension named above; an argument that names none is the same for every part.
All inputs are finite; a program needn't handle non-finite values.
Results may differ from a plain program's by a relative error of at most 0.0121207.
Values are sent between devices in bfloat16 or wider.
A program may use at most 1 GiB of HBM per device.

v0:
```python
import math
import jax
import jax.numpy as jnp
from jax import lax
from jax.sharding import PartitionSpec as P

HEAD_DIM = 128
LN_EPS = 1e-5
ROPE_BASE = 10000.0


def norm_f32(hid_f32, weight_f32):
    mean_val = jnp.mean(hid_f32, axis=-1, keepdims=True)
    centered = hid_f32 - mean_val
    var_val = jnp.mean(centered * centered, axis=-1, keepdims=True)
    return centered * lax.rsqrt(var_val + LN_EPS) * weight_f32


def rope_tables(positions):
    inv_freq = ROPE_BASE ** (-jnp.arange(0, HEAD_DIM, 2, dtype=jnp.float32) / HEAD_DIM)
    angles = positions.astype(jnp.float32)[:, None] * inv_freq[None, :]
    return jnp.cos(angles)[:, None, :], jnp.sin(angles)[:, None, :]


def apply_rope(values, cos_t, sin_t):
    rot_pairs = values.reshape(values.shape[:-1] + (HEAD_DIM // 2, 2))
    even_part = rot_pairs[..., 0]
    odd_part = rot_pairs[..., 1]
    new_even = even_part * cos_t - odd_part * sin_t
    new_odd = odd_part * cos_t + even_part * sin_t
    return jnp.stack([new_even, new_odd], axis=-1).reshape(values.shape)


def block_probs(q_block, row_start, k_all):
    scores = jnp.einsum('qgrd,kgd->grqk', q_block, k_all, preferred_element_type=jnp.float32) * (HEAD_DIM ** -0.5)
    row_ids = row_start + jnp.arange(q_block.shape[0])
    col_ids = jnp.arange(k_all.shape[0])
    scores = jnp.where(row_ids[:, None] >= col_ids[None, :], scores, -jnp.inf)
    return jax.nn.softmax(scores, axis=-1)


def attn_forward(q_grp, k_all, v_all, row_offset):
    n_rows = q_grp.shape[0]
    block_rows = math.gcd(n_rows, 128)
    q_blocks = q_grp.reshape((n_rows // block_rows, block_rows) + q_grp.shape[1:])

    def one_block(block_in):
        q_block, block_idx = block_in
        attn_prob = block_probs(q_block, row_offset + block_idx * block_rows, k_all)
        return jnp.einsum('grqk,kgd->qgrd', attn_prob.astype(jnp.bfloat16), v_all, preferred_element_type=jnp.float32).astype(jnp.bfloat16)

    o_blocks = lax.map(one_block, (q_blocks, jnp.arange(n_rows // block_rows)))
    return o_blocks.reshape(q_grp.shape)


def attn_backward(q_grp, k_all, v_all, do_grp, row_offset):
    n_rows = q_grp.shape[0]
    block_rows = math.gcd(n_rows, 128)
    block_shape = (n_rows // block_rows, block_rows) + q_grp.shape[1:]

    def one_block(carry, block_in):
        dk_acc, dv_acc = carry
        q_block, do_block, block_idx = block_in
        attn_prob = block_probs(q_block, row_offset + block_idx * block_rows, k_all)
        d_prob = jnp.einsum('qgrd,kgd->grqk', do_block, v_all, preferred_element_type=jnp.float32)
        row_dot = jnp.sum(attn_prob * d_prob, axis=-1, keepdims=True)
        d_score = (attn_prob * (d_prob - row_dot) * (HEAD_DIM ** -0.5)).astype(jnp.bfloat16)
        dq_block = jnp.einsum('grqk,kgd->qgrd', d_score, k_all, preferred_element_type=jnp.float32).astype(jnp.bfloat16)
        dk_acc = dk_acc + jnp.einsum('grqk,qgrd->kgd', d_score, q_block, preferred_element_type=jnp.float32)
        dv_acc = dv_acc + jnp.einsum('grqk,qgrd->kgd', attn_prob.astype(jnp.bfloat16), do_block, preferred_element_type=jnp.float32)
        return (dk_acc, dv_acc), dq_block

    zero_acc = jnp.zeros(k_all.shape, jnp.float32)
    kv_sums, dq_blocks = lax.scan(one_block, (zero_acc, zero_acc), (q_grp.reshape(block_shape), do_grp.reshape(block_shape), jnp.arange(block_shape[0])))
    return dq_blocks.reshape(q_grp.shape), kv_sums[0], kv_sums[1]


def solution(mesh):
    sp_size = mesh.shape['sp']
    row_spec = P(('dp', 'sp'), None)
    pos_spec = P(('dp', 'sp'))
    full_spec = P(None, None)
    grad_spec = P('dp', None)

    def local_step(hidden, positions, d_attn, ln_weight, w_q, w_k, w_v, w_o):
        local_rows = hidden.shape[0]
        n_heads = w_q.shape[1] // HEAD_DIM
        kv_heads = w_k.shape[1] // HEAD_DIM
        copies = max(sp_size // kv_heads, 1)
        normed32, norm_vjp = jax.vjp(norm_f32, hidden.astype(jnp.float32), ln_weight.astype(jnp.float32))
        normed = normed32.astype(jnp.bfloat16)
        cos_t, sin_t = rope_tables(positions)
        q_rot = apply_rope(jnp.dot(normed, w_q, preferred_element_type=jnp.float32).reshape(local_rows, n_heads, HEAD_DIM), cos_t, sin_t).astype(jnp.bfloat16)
        k_rot = apply_rope(jnp.dot(normed, w_k, preferred_element_type=jnp.float32).reshape(local_rows, kv_heads, HEAD_DIM), cos_t, sin_t).astype(jnp.bfloat16)
        v_loc = jnp.dot(normed, w_v, preferred_element_type=jnp.float32).astype(jnp.bfloat16).reshape(local_rows, kv_heads, HEAD_DIM)
        if copies > 1:
            k_rot = jnp.repeat(k_rot, copies, axis=1)
            v_loc = jnp.repeat(v_loc, copies, axis=1)
        q_heads = lax.all_to_all(q_rot, 'sp', 1, 0, tiled=True)
        k_heads = lax.all_to_all(k_rot, 'sp', 1, 0, tiled=True)
        v_heads = lax.all_to_all(v_loc, 'sp', 1, 0, tiled=True)
        seq_rows, heads_local = q_heads.shape[0], q_heads.shape[1]
        kv_local = k_heads.shape[1]
        q_grp = q_heads.reshape(seq_rows, kv_local, heads_local // kv_local, HEAD_DIM)
        o_grp = attn_forward(q_grp, k_heads, v_heads, 0)
        o_tok = lax.all_to_all(o_grp.reshape(q_heads.shape), 'sp', 0, 1, tiled=True).reshape(local_rows, n_heads * HEAD_DIM)
        attn_out = jnp.dot(o_tok, w_o, preferred_element_type=jnp.float32).astype(jnp.bfloat16)
        d_o = jnp.einsum('td,ed->te', d_attn, w_o, preferred_element_type=jnp.float32).astype(jnp.bfloat16)
        dw_o = jnp.einsum('te,td->ed', o_tok, d_attn, preferred_element_type=jnp.float32)
        do_heads = lax.all_to_all(d_o.reshape(local_rows, n_heads, HEAD_DIM), 'sp', 1, 0, tiled=True)
        dq_grp, dk_acc, dv_acc = attn_backward(q_grp, k_heads, v_heads, do_heads.reshape(q_grp.shape), 0)
        dq_tok = lax.all_to_all(dq_grp.reshape(q_heads.shape), 'sp', 0, 1, tiled=True)
        dk_tok = lax.all_to_all(dk_acc.astype(jnp.bfloat16), 'sp', 0, 1, tiled=True)
        dv_tok = lax.all_to_all(dv_acc.astype(jnp.bfloat16), 'sp', 0, 1, tiled=True)
        if copies > 1:
            dk_tok = dk_tok.reshape(local_rows, kv_heads, copies, HEAD_DIM).astype(jnp.float32).sum(axis=2).astype(jnp.bfloat16)
            dv_tok = dv_tok.reshape(local_rows, kv_heads, copies, HEAD_DIM).astype(jnp.float32).sum(axis=2).astype(jnp.bfloat16)
        g_q = apply_rope(dq_tok.astype(jnp.float32), cos_t, -sin_t).astype(jnp.bfloat16).reshape(local_rows, n_heads * HEAD_DIM)
        g_k = apply_rope(dk_tok.astype(jnp.float32), cos_t, -sin_t).astype(jnp.bfloat16).reshape(local_rows, kv_heads * HEAD_DIM)
        g_v = dv_tok.reshape(local_rows, kv_heads * HEAD_DIM)
        d_normed = (jnp.einsum('te,de->td', g_q, w_q, preferred_element_type=jnp.float32)
                    + jnp.einsum('te,de->td', g_k, w_k, preferred_element_type=jnp.float32)
                    + jnp.einsum('te,de->td', g_v, w_v, preferred_element_type=jnp.float32))
        dw_q = jnp.einsum('td,te->de', normed, g_q, preferred_element_type=jnp.float32)
        dw_k = jnp.einsum('td,te->de', normed, g_k, preferred_element_type=jnp.float32)
        dw_v = jnp.einsum('td,te->de', normed, g_v, preferred_element_type=jnp.float32)
        d_hid, d_lnw = norm_vjp(d_normed)
        grad_sums = lax.psum((d_lnw, dw_q, dw_k, dw_v, dw_o), 'sp')
        return (attn_out, d_hid.astype(jnp.bfloat16), grad_sums[0].astype(jnp.bfloat16), grad_sums[1].astype(jnp.bfloat16),
                grad_sums[2].astype(jnp.bfloat16), grad_sums[3].astype(jnp.bfloat16), grad_sums[4].astype(jnp.bfloat16))

    return jax.shard_map(local_step, mesh=mesh,
                         in_specs=(row_spec, pos_spec, row_spec, P(None), full_spec, full_spec, full_spec, full_spec),
                         out_specs=(row_spec, row_spec, P('dp'), grad_spec, grad_spec, grad_spec, grad_spec),
                         check_vma=False)
```

profile of v0, /device:TPU:0, one launch (start us, length us, event | category | flops | bytes accessed | tf_op | source)
XLA Modules:
  0.0 5292.7 jit_solution(7611136409954293480)
XLA Ops:
  66.0 24.6 convert_bitcast_fusion.1
  100.4 26.4 fusion.145
  142.1 19.2 subtract_convert_fusion.1
  207.3 57.3 %all-to-all-done = bf16[1024,24,128]{0,2,1:T(8,128)(2,1)} async-done(((bf16[1024,24,128]{0,2,1:T(8,128)(2,1)}), bf16[1024,24,128]{0,2,1:T(8,128)(2,1)}, u32[]{:S(2)}, u32[]{:S(2)}) %all-to-all-start) | async-done | bytes 6291488 | tf_op jit(solution)/shard_map/all_to_all | solution.py:99
  285.6 2231.1 %while.26 = (s32[]{:T(128)}, f32[4096,2,128]{0,2,1:T(8,128)}, f32[4096,2,128]{0,2,1:T(8,128)}, bf16[32,128,2,3,128]{4,1,0,3,2:T(8,128)(2,1)}, bf16[32,128,2,3,12...) while((s32[]{:T(128)}, f32[4096,2,128]{0,2,1:T(8,128)}, ...), condition=%wide.region_10.11_spmd.clone, body=%wide.region_6.10_spmd.clone.sunk | while | flops 4094277376 | bytes 163536048 | solution.py:74
  314.2 20.5 fusion.210
  334.6 18.8 fusion.212
  382.8 21.7 fusion.210
  452.5 21.7 fusion.210
  522.3 21.7 fusion.210
  592.1 21.7 fusion.210
  661.9 21.7 fusion.210
  731.7 21.7 fusion.210
  801.4 21.7 fusion.210
  871.2 21.7 fusion.210
  941.0 21.7 fusion.210
  1010.8 21.7 fusion.210
  1080.5 21.7 fusion.210
  1150.3 21.7 fusion.210
  1220.1 21.7 fusion.210
  1289.9 21.7 fusion.210
  1359.7 21.7 fusion.210
  1429.4 21.7 fusion.210
  1499.2 21.7 fusion.210
  1569.0 21.7 fusion.210
  1638.8 21.7 fusion.210
  1708.5 21.7 fusion.210
  1778.3 21.7 fusion.210
  1848.1 21.7 fusion.210
  1917.9 21.7 fusion.210
  1987.6 21.7 fusion.210
  2057.4 21.7 fusion.210
  2127.2 21.7 fusion.210
  2197.0 21.7 fusion.210
  2266.8 21.7 fusion.210
  2336.5 21.7 fusion.210
  2406.3 21.7 fusion.210
  2476.1 21.7 fusion.210
  2562.3 619.8 %while.25 = (s32[]{:T(128)}, bf16[32,128,2,3,128]{4,1,0,3,2:T(8,128)(2,1)}, s32[32]{0:T(128)S(1)}, bf16[32,128,2,3,128]{4,1,3,2,0:T(8,128)(2,1)}, bf16[4096,2,12...) while((s32[]{:T(128)}, bf16[32,128,2,3,128]{4,1,0,3,2:T(8,128)(2,1)}, ...), condition=%wide.region_5.6_spmd, body=%wide.region_2.5_spmd.sunk | while | flops 1630113920 | bytes 30809216 | solution.py:52
  3191.3 25.4 copy.132
  3293.7 44.3 all-to-all-done.3
  3355.4 26.3 convolution_convert_fusion
  3381.7 24.1 fusion.152
  3405.8 30.8 all-to-all-done.5
  3474.8 19.1 subtract_convert_fusion
  3519.5 28.4 fusion.149
  3548.0 34.8 fusion.120
  3602.8 1689.4 %all-reduce.2 = (bf16[3072]{0:T(1024)(128)(2,1)}, bf16[3072,3072]{1,0:T(8,128)(2,1)}, bf16[3072,1024]{1,0:T(8,128)(2,1)}, bf16[3072,1024]{1,0:T(8,128)(2,1)}, bf16[3072,3072]{1,0:T(8,128)(2,1)}) all-reduce(f32[3072]{0:T(1024)S(1)} %get-tuple-element.197, f32[3072,3072]{1,0:T(8,128)} %fusion.149, ...), channel_id=1, replica_groups=mesh['dp'=2,'sp'=4] {'sp'}, use_global_device_ids=true, to_apply=%region_14.15 | all-reduce | flops 25168896 | bytes 151013376 | tf_op jit(solution)/shard_map/psum | solution.py:128
  (514 shorter events, 2487.1 us)
Async XLA Ops:
  0.6 4.6 copy-start
  0.6 6.9 copy-start.18
  5.2 6.0 copy-start.12
  7.0 0.6 copy-start.16
  7.6 3.7 copy-start.14
  7.6 3.7 copy-start.10
  11.3 12.3 copy-start.6
  11.3 17.1 copy-start.19
  23.6 37.5 all-to-all-start.2
  48.2 93.9 %copy-start.3 = (f32[1024,64]{0,1:T(8,128)}, f32[1024,64]{0,1:T(8,128)S(1)}, u32[]{:S(2)}) copy-start(f32[1024,64]{0,1:T(8,128)S(1)} %get-tuple-element.252) | copy-start | bytes 786436
  61.1 29.4 copy-start.2
  61.1 33.8 all-to-all-start.1
  94.9 94.0 %all-to-all-start.4 = ((bf16[1024,24,128]{2,0,1:T(8,128)(2,1)}), bf16[1024,24,128]{2,0,1:T(8,128)(2,1)}, u32[]{:S(2)}, u32[]{:S(2)}) async-start(bf16[1024,24,128]{2,0,1:T(8,128)(2,1)} %bitcast.297), calls=%async_computation.4 | async-start | bytes 12582912 | tf_op jit(solution)/shard_map/all_to_all | solution.py:110
  189.0 75.6 %all-to-all-start = ((bf16[1024,24,128]{0,2,1:T(8,128)(2,1)}), bf16[1024,24,128]{0,2,1:T(8,128)(2,1)}, u32[]{:S(2)}, u32[]{:S(2)}) async-start(bf16[1024,24,128]{0,2,1:T(8,128)(2,1)} %copy.121), calls=%async_computation | async-start | bytes 12582912 | tf_op jit(solution)/shard_map/all_to_all | solution.py:99
  2523.6 29.9 all-to-all-start.6
  2553.4 685.7 %all-to-all-start.7 = ((bf16[4096,2,128]{2,1,0:T(2,128)(2,1)}), bf16[4096,2,128]{2,1,0:T(2,128)(2,1)}, u32[]{:S(2)}, u32[]{:S(2)}) async-start(bf16[4096,2,128]{2,1,0:T(2,128)(2,1)} %copy.146), calls=%async_computation.7 | async-start | bytes 4194304 | tf_op jit(solution)/shard_map/all_to_all | solution.py:114
  3182.1 9.3 copy-start.1
  3216.7 14.8 copy-start.4
  3216.7 14.8 copy-start.7
  3239.1 98.8 %all-to-all-start.3 = ((bf16[4096,6,128]{2,1,0:T(8,128)(2,1)}), bf16[4096,6,128]{2,1,0:T(8,128)(2,1)}, u32[]{:S(2)}, u32[]{:S(2)}) async-start(bf16[4096,6,128]{2,1,0:T(8,128)(2,1)} %copy.132), calls=%async_computation.3 | async-start | bytes 16777216 | tf_op jit(solution)/shard_map/all_to_all | solution.py:106
  3249.6 13.0 copy-start.8
  3249.6 25.6 slice-start.2
  3262.6 12.7 copy-start.9
  3262.6 12.7 slice-start.3
  3262.6 21.9 slice-start.4
  3275.3 9.2 slice-start.5
  3338.0 98.6 %all-to-all-start.5 = ((bf16[4096,6,128]{2,1,0:T(8,128)(2,1)}), bf16[4096,6,128]{2,1,0:T(8,128)(2,1)}, u32[]{:S(2)}, u32[]{:S(2)}) async-start(bf16[4096,6,128]{2,1,0:T(8,128)(2,1)} %copy.140), calls=%async_computation.5 | async-start | bytes 16777216 | tf_op jit(solution)/shard_map/all_to_all | solution.py:112
  3343.8 37.9 slice-start.6
  3355.4 26.3 copy-start.5
  3355.4 26.3 slice-start.7
  3509.2 38.7 slice-start
  3519.5 28.4 slice-start.1
  3519.5 28.4 copy-start.11
  3519.5 28.4 copy-start.13
  3519.5 28.5 copy-start.15
  3548.0 34.8 copy-start.17
where the time goes:
time: 5310 us; the launch traced here: 5290 us
  matrix products  2980 us (56%)
  blocking collectives  1690 us (32%)
  local copies, waits for them, and re-layouts  252 us (5%)
  waiting for transfers between devices  151 us (3%)
  other arithmetic  135 us (3%)
    psum x1, blocking collectives, local_step(): grad_sums = lax.psum((d_lnw, dw_q, dw_k, dw_v, dw_o), 'sp')  1690 us
    dot_general x32, matrix products, one_block(): jnp.einsum('grqk,qgrd->kgd', d_score, q_block, preferred_element_type=jnp...  692 us
    sub x64, matrix products, block_probs(): return jax.nn.softmax(scores, axis=-1)  682 us
    dot_general x32, matrix products, one_block(): jnp.einsum('grqk,kgd->qgrd', d_score, k_all, preferred_element_type=jnp.f...  603 us
    dot_general x32, matrix products, one_block(): jnp.einsum('grqk,qgrd->kgd', attn_prob.astype(jnp.bfloat16), do_block, pr...  303 us
    dot_general x32, matrix products, one_block(): jnp.einsum('qgrd,kgd->grqk', do_block, v_all, preferred_element_type=jnp....  240 us
    dot_general x32, matrix products, one_block(): jnp.einsum('grqk,kgd->qgrd', attn_prob.astype(jnp.bfloat16), v_all, prefe...  227 us
  transfers between devices with their start and end apart: 8, of which 4 were waited for; matrix products, arithmetic and copies ran while one was open for 18% of the time, Pallas kernels for 0%

commit v1 on v0

v1 whole, which is shorter than its diff:
```python
import math
import jax
import jax.numpy as jnp
from jax import lax
from jax.experimental import pallas as pl
from jax.experimental.pallas import tpu as pltpu
from jax.sharding import PartitionSpec as P

HEAD_DIM = 128
LN_EPS = 1e-5
ROPE_BASE = 10000.0
REP = 3
BQ = 256
BK = 512
LOG2E = math.log2(math.e)
SCALE = HEAD_DIM ** -0.5
VMEM_BYTES = 60 * 1024 * 1024
F32 = jnp.float32
BF16 = jnp.bfloat16


def cost(flops, nbytes):
    return pl.CostEstimate(flops=int(flops), bytes_accessed=int(nbytes), transcendentals=0)


def mm(lhs, rhs, dims):
    return lax.dot_general(lhs, rhs, (dims, ((), ())), preferred_element_type=F32)


def rotate(val, cos_t, sin_t):
    lane = lax.broadcasted_iota(jnp.int32, val.shape, 1)
    swapped = jnp.where(lane % 2 == 0, pltpu.roll(val, HEAD_DIM - 1, 1), pltpu.roll(val, 1, 1))
    return val * cos_t + swapped * sin_t


def qkv_kernel(idx, x_ref, lnw_ref, wq_ref, wk_ref, wv_ref, cos_ref, sin_ref, *rest):
    h_ref, qkv_ref = rest[-2:]
    xf = x_ref[...].astype(F32)
    mean = jnp.mean(xf, axis=-1, keepdims=True)
    cen = xf - mean
    var = jnp.mean(cen * cen, axis=-1, keepdims=True)
    h = (cen * lax.rsqrt(var + LN_EPS) * lnw_ref[...].astype(F32)).astype(BF16)
    h_ref[...] = h
    cos_t = cos_ref[...]
    sin_t = sin_ref[...]
    nq = wq_ref.shape[1]
    nk = wk_ref.shape[1]
    q = mm(h, wq_ref[...], ((1,), (0,)))
    for n in range(nq // HEAD_DIM):
        sl = slice(n * HEAD_DIM, (n + 1) * HEAD_DIM)
        qkv_ref[:, sl] = rotate(q[:, sl], cos_t, sin_t).astype(BF16)
    k = mm(h, wk_ref[...], ((1,), (0,)))
    for n in range(nk // HEAD_DIM):
        sl = slice(n * HEAD_DIM, (n + 1) * HEAD_DIM)
        qkv_ref[:, nq + n * HEAD_DIM:nq + (n + 1) * HEAD_DIM] = rotate(k[:, sl], cos_t, sin_t).astype(BF16)
    qkv_ref[:, nq + nk:] = mm(h, wv_ref[...], ((1,), (0,))).astype(BF16)


def qkv_block(idx, x, ln_w, w_q, w_k, w_v, cos_t, sin_t, seq, n_dev, prev):
    rows, dim = x.shape
    cq, ck = w_q.shape[1] // n_dev, w_k.shape[1] // n_dev
    per = rows // BQ
    const = lambda i, ix: (0, 0)
    head = lambda i, ix: (0, ix[0])
    here = lambda i, ix: (ix[1] * per + i, 0)
    in_specs = [
        pl.BlockSpec((BQ, dim), lambda i, ix: (i, 0)),
        pl.BlockSpec((1, dim), const),
        pl.BlockSpec((dim, cq), head),
        pl.BlockSpec((dim, ck), head),
        pl.BlockSpec((dim, ck), head),
        pl.BlockSpec((BQ, HEAD_DIM), here),
        pl.BlockSpec((BQ, HEAD_DIM), here),
    ]
    args = [idx, x, ln_w, w_q, w_k, w_v, cos_t, sin_t]
    aliases = {}
    if prev is not None:
        in_specs += [pl.BlockSpec(memory_space=pl.ANY)] * 2
        args += list(prev)
        aliases = {8: 0, 9: 1}
    cols = cq + 2 * ck
    return pl.pallas_call(
        qkv_kernel,
        out_shape=(jax.ShapeDtypeStruct((seq, dim), BF16), jax.ShapeDtypeStruct((seq, cols), BF16)),
        grid_spec=pltpu.PrefetchScalarGridSpec(
            num_scalar_prefetch=1, grid=(per,), in_specs=in_specs,
            out_specs=(pl.BlockSpec((BQ, dim), here), pl.BlockSpec((BQ, cols), here))),
        input_output_aliases=aliases,
        compiler_params=pltpu.CompilerParams(dimension_semantics=("arbitrary",), vmem_limit_bytes=VMEM_BYTES),
        cost_estimate=cost(2 * rows * dim * cols, 2 * (2 * rows * dim + dim * cols + rows * cols)),
        name="ln_qkv",
    )(*args)


def do_kernel(idx, g_ref, wo_ref, *rest):
    gall_ref, do_ref = rest[-2:]
    g = g_ref[...]
    gall_ref[...] = g
    do_ref[...] = mm(g, wo_ref[...], ((1,), (1,))).astype(BF16)


def do_block(idx, g, w_o, seq, n_dev, prev):
    rows, dim = g.shape
    ce = w_o.shape[0] // n_dev
    per = rows // BQ
    here = lambda i, ix: (ix[1] * per + i, 0)
    in_specs = [
        pl.BlockSpec((BQ, dim), lambda i, ix: (i, 0)),
        pl.BlockSpec((ce, dim), lambda i, ix: (ix[0], 0)),
    ]
    args = [idx, g, w_o]
    aliases = {}
    if prev is not None:
        in_specs += [pl.BlockSpec(memory_space=pl.ANY)] * 2
        args += list(prev)
        aliases = {3: 0, 4: 1}
    return pl.pallas_call(
        do_kernel,
        out_shape=(jax.ShapeDtypeStruct((seq, dim), BF16), jax.ShapeDtypeStruct((seq, ce), BF16)),
        grid_spec=pltpu.PrefetchScalarGridSpec(
            num_scalar_prefetch=1, grid=(per,), in_specs=in_specs,
            out_specs=(pl.BlockSpec((BQ, dim), here), pl.BlockSpec((BQ, ce), here))),
        input_output_aliases=aliases,
        compiler_params=pltpu.CompilerParams(dimension_semantics=("arbitrary",), vmem_limit_bytes=VMEM_BYTES),
        cost_estimate=cost(2 * rows * dim * ce, 2 * (2 * rows * dim + dim * ce + rows * ce)),
        name="d_o",
    )(*args)


def stack_heads(val):
    return jnp.concatenate([val[:, n * HEAD_DIM:(n + 1) * HEAD_DIM] for n in range(REP)], axis=0)


def flip(val):
    return val.astype(F32).T.astype(BF16)


def causal(row_start, key_start, shape):
    key = key_start + lax.broadcasted_iota(jnp.int32, shape, 0)
    query = row_start + lax.broadcasted_iota(jnp.int32, shape, 1) % BQ
    return key <= query


def fwd_kernel(q_ref, k_ref, v_ref, o_ref, ot_ref, lse_ref, qt_sc, vt_sc, acc_sc, ml_sc):
    blk = pl.program_id(1)
    width = REP * BQ
    n_chunks = k_ref.shape[0] // BK

    @pl.when(blk == 0)
    def _():
        def one(j, _):
            vt_sc[j] = flip(v_ref[pl.ds(j * BK, BK), :])
            return 0

        lax.fori_loop(0, n_chunks, one, 0)

    qt_sc[...] = flip(stack_heads(q_ref[...]))
    acc_sc[...] = jnp.zeros_like(acc_sc)
    ml_sc[0:1, :] = jnp.full((1, width), -jnp.inf, F32)
    ml_sc[1:2, :] = jnp.zeros((1, width), F32)

    def chunk(j, masked):
        s = mm(k_ref[pl.ds(j * BK, BK), :], qt_sc[...], ((1,), (0,))) * (SCALE * LOG2E)
        if masked:
            s = jnp.where(causal(blk * BQ, j * BK, s.shape), s, -jnp.inf)
        m_old = ml_sc[0:1, :]
        m_new = jnp.maximum(m_old, jnp.max(s, axis=0, keepdims=True))
        alpha = jnp.exp2(m_old - m_new)
        p = jnp.exp2(s - m_new)
        ml_sc[0:1, :] = m_new
        ml_sc[1:2, :] = ml_sc[1:2, :] * alpha + jnp.sum(p, axis=0, keepdims=True)
        acc_sc[...] = acc_sc[...] * alpha + mm(vt_sc[j], p.astype(BF16), ((1,), (0,)))

    n_full = (blk * BQ) // BK

    def body(j, _):
        chunk(j, False)
        return 0

    lax.fori_loop(0, n_full, body, 0)
    chunk(n_full, True)
    total = ml_sc[1:2, :]
    out_t = acc_sc[...] / total
    ot_ref[0, 0] = out_t
    lse_ref[0, 0] = ml_sc[0:1, :] + jnp.log2(total)
    for n in range(REP):
        o_ref[:, n * HEAD_DIM:(n + 1) * HEAD_DIM] = out_t[:, n * BQ:(n + 1) * BQ].T.astype(BF16)


def attn_forward(qkv, kv_local):
    seq = qkv.shape[0]
    nq = seq // BQ
    wide = REP * HEAD_DIM
    first_k = kv_local * REP
    flops = 2 * 2 * kv_local * REP * seq * seq // 2 * HEAD_DIM * 2
    return pl.pallas_call(
        fwd_kernel,
        grid=(kv_local, nq),
        in_specs=[
            pl.BlockSpec((BQ, wide), lambda t, i: (i, t)),
            pl.BlockSpec((seq, HEAD_DIM), lambda t, i: (0, first_k + t)),
            pl.BlockSpec((seq, HEAD_DIM), lambda t, i: (0, first_k + kv_local + t)),
        ],
        out_specs=(
            pl.BlockSpec((BQ, wide), lambda t, i: (i, t)),
            pl.BlockSpec((1, 1, HEAD_DIM, REP * BQ), lambda t, i: (t, i, 0, 0)),
            pl.BlockSpec((1, 1, 1, REP * BQ), lambda t, i: (t, i, 0, 0)),
        ),
        out_shape=(
            jax.ShapeDtypeStruct((seq, kv_local * wide), BF16),
            jax.ShapeDtypeStruct((kv_local, nq, HEAD_DIM, REP * BQ), F32),
            jax.ShapeDtypeStruct((kv_local, nq, 1, REP * BQ), F32),
        ),
        scratch_shapes=[
            pltpu.VMEM((HEAD_DIM, REP * BQ), BF16),
            pltpu.VMEM((seq // BK, HEAD_DIM, BK), BF16),
            pltpu.VMEM((HEAD_DIM, REP * BQ), F32),
            pltpu.VMEM((8, REP * BQ), F32),
        ],
        compiler_params=pltpu.CompilerParams(dimension_semantics=("arbitrary", "arbitrary"), vmem_limit_bytes=VMEM_BYTES),
        cost_estimate=cost(flops, 4 * seq * wide * kv_local * 2),
        name="attn_fwd",
    )(qkv, qkv, qkv)


def bwd_kernel(q_ref, k_ref, v_ref, do_ref, ot_ref, lse_ref, cos_ref, sin_ref, out_ref,
               qs_sc, qt_sc, ds_sc, dt_sc, kt_sc, dk_sc, dv_sc, dq_sc, row_sc):
    blk = pl.program_id(0)
    wide = REP * HEAD_DIM
    n_chunks = k_ref.shape[0] // BK

    @pl.when(blk == 0)
    def _():
        def one(j, _):
            rows = pl.ds(j * BK, BK)
            kt_sc[j] = flip(k_ref[rows, :])
            dk_sc[rows, :] = jnp.zeros((BK, HEAD_DIM), F32)
            dv_sc[rows, :] = jnp.zeros((BK, HEAD_DIM), F32)
            return 0

        lax.fori_loop(0, n_chunks, one, 0)

    q_all = stack_heads(q_ref[...])
    do_all = stack_heads(do_ref[...])
    qs_sc[...] = q_all
    qt_sc[...] = flip(q_all)
    ds_sc[...] = do_all
    do_t = do_all.astype(F32).T
    dt_sc[...] = do_t.astype(BF16)
    row_sc[0:1, :] = lse_ref[0, 0]
    row_sc[1:2, :] = jnp.sum(ot_ref[0, 0] * do_t, axis=0, keepdims=True)
    dq_sc[...] = jnp.zeros_like(dq_sc)

    def chunk(j, masked):
        rows = pl.ds(j * BK, BK)
        s = mm(k_ref[rows, :], qt_sc[...], ((1,), (0,))) * (SCALE * LOG2E)
        p = jnp.exp2(s - row_sc[0:1, :])
        if masked:
            p = jnp.where(causal(blk * BQ, j * BK, s.shape), p, 0.0)
        dp = mm(v_ref[rows, :], dt_sc[...], ((1,), (0,)))
        dv_sc[rows, :] += mm(p.astype(BF16), ds_sc[...], ((1,), (0,)))
        d_s = (p * (dp - row_sc[1:2, :]) * SCALE).astype(BF16)
        dk_sc[rows, :] += mm(d_s, qs_sc[...], ((1,), (0,)))
        dq_sc[...] += mm(kt_sc[j], d_s, ((1,), (0,)))

    n_full = (blk * BQ) // BK

    def body(j, _):
        chunk(j, False)
        return 0

    lax.fori_loop(0, n_full, body, 0)
    chunk(n_full, True)

    rows = pl.ds(blk * BQ, BQ)
    cos_t = cos_ref[rows, :]
    sin_t = -sin_ref[rows, :]
    for n in range(REP):
        dq = dq_sc[:, n * BQ:(n + 1) * BQ].T.astype(BF16).astype(F32)
        out_ref[rows, n * HEAD_DIM:(n + 1) * HEAD_DIM] = rotate(dq, cos_t, sin_t).astype(BF16)

    @pl.when(blk == pl.num_programs(0) - 1)
    def _():
        def one(j, _):
            kr = pl.ds(j * BK, BK)
            dk = dk_sc[kr, :].astype(BF16).astype(F32)
            out_ref[kr, wide:wide + HEAD_DIM] = rotate(dk, cos_ref[kr, :], -sin_ref[kr, :]).astype(BF16)
            out_ref[kr, wide + HEAD_DIM:wide + 2 * HEAD_DIM] = dv_sc[kr, :].astype(BF16)
            return 0

        lax.fori_loop(0, n_chunks, one, 0)


def attn_backward(qkv, d_o, o_t, lse, cos_t, sin_t, kv_local, t):
    seq = qkv.shape[0]
    nq = seq // BQ
    wide = REP * HEAD_DIM
    first_k = kv_local * REP
    flops = 5 * 2 * REP * seq * seq // 2 * HEAD_DIM * 2
    whole = lambda i: (0, 0)
    return pl.pallas_call(
        bwd_kernel,
        grid=(nq,),
        in_specs=[
            pl.BlockSpec((BQ, wide), lambda i: (i, t)),
            pl.BlockSpec((seq, HEAD_DIM), lambda i: (0, first_k + t)),
            pl.BlockSpec((seq, HEAD_DIM), lambda i: (0, first_k + kv_local + t)),
            pl.BlockSpec((BQ, wide), lambda i: (i, t)),
            pl.BlockSpec((1, 1, HEAD_DIM, REP * BQ), lambda i: (t, i, 0, 0)),
            pl.BlockSpec((1, 1, 1, REP * BQ), lambda i: (t, i, 0, 0)),
            pl.BlockSpec((seq, HEAD_DIM), whole),
            pl.BlockSpec((seq, HEAD_DIM), whole),
        ],
        out_specs=pl.BlockSpec((seq, wide + 2 * HEAD_DIM), whole),
        out_shape=jax.ShapeDtypeStruct((seq, wide + 2 * HEAD_DIM), BF16),
        scratch_shapes=[
            pltpu.VMEM((REP * BQ, HEAD_DIM), BF16),
            pltpu.VMEM((HEAD_DIM, REP * BQ), BF16),
            pltpu.VMEM((REP * BQ, HEAD_DIM), BF16),
            pltpu.VMEM((HEAD_DIM, REP * BQ), BF16),
            pltpu.VMEM((seq // BK, HEAD_DIM, BK), BF16),
            pltpu.VMEM((seq, HEAD_DIM), F32),
            pltpu.VMEM((seq, HEAD_DIM), F32),
            pltpu.VMEM((HEAD_DIM, REP * BQ), F32),
            pltpu.VMEM((8, REP * BQ), F32),
        ],
        compiler_params=pltpu.CompilerParams(dimension_semantics=("arbitrary",), vmem_limit_bytes=VMEM_BYTES),
        cost_estimate=cost(flops, 8 * seq * wide * 2),
        name="attn_bwd",
    )(qkv, qkv, qkv, d_o, o_t, lse, cos_t, sin_t)


def ln_bwd_kernel(dh0_ref, dh1_ref, x_ref, lnw_ref, dx_ref, dw_ref):
    @pl.when(pl.program_id(0) == 0)
    def _():
        dw_ref[...] = jnp.zeros_like(dw_ref)

    xf = x_ref[...].astype(F32)
    mean = jnp.mean(xf, axis=-1, keepdims=True)
    cen = xf - mean
    var = jnp.mean(cen * cen, axis=-1, keepdims=True)
    rstd = lax.rsqrt(var + LN_EPS)
    xhat = cen * rstd
    dh = dh0_ref[...] + dh1_ref[...]
    dw_ref[...] += jnp.sum(dh * xhat, axis=0, keepdims=True)
    dxh = dh * lnw_ref[...].astype(F32)
    mean_d = jnp.mean(dxh, axis=-1, keepdims=True)
    mean_dx = jnp.mean(dxh * xhat, axis=-1, keepdims=True)
    dx_ref[...] = (rstd * (dxh - mean_d - xhat * mean_dx)).astype(BF16)


def ln_backward(dh0, dh1, x, ln_w):
    rows, dim = x.shape
    blk = 128
    row = lambda i: (i, 0)
    const = lambda i: (0, 0)
    return pl.pallas_call(
        ln_bwd_kernel,
        grid=(rows // blk,),
        in_specs=[pl.BlockSpec((blk, dim), row), pl.BlockSpec((blk, dim), row),
                  pl.BlockSpec((blk, dim), row), pl.BlockSpec((1, dim), const)],
        out_specs=(pl.BlockSpec((blk, dim), row), pl.BlockSpec((1, dim), const)),
        out_shape=(jax.ShapeDtypeStruct((rows, dim), BF16), jax.ShapeDtypeStruct((1, dim), F32)),
        compiler_params=pltpu.CompilerParams(dimension_semantics=("arbitrary",), vmem_limit_bytes=VMEM_BYTES),
        cost_estimate=cost(20 * rows * dim, 12 * rows * dim),
        name="ln_bwd",
    )(dh0, dh1, x, ln_w)


def solution(mesh):
    n_dev = mesh.shape['sp']
    row_spec = P(('dp', 'sp'), None)
    pos_spec = P(('dp', 'sp'))
    full_spec = P(None, None)
    grad_spec = P('dp', None)

    def over_chip(val):
        return lax.ppermute(val, 'sp', [(i, i ^ 2) for i in range(n_dev)])

    def over_core(val):
        return lax.ppermute(val, 'sp', [(i, i ^ 1) for i in range(n_dev)])

    def layer(hidden, positions, d_attn, ln_weight, w_q, w_k, w_v, w_o):
        rows, dim = hidden.shape
        seq = rows * n_dev
        kv_local = w_k.shape[1] // HEAD_DIM // n_dev
        wide = REP * HEAD_DIM
        cq = w_q.shape[1] // n_dev
        ck = w_k.shape[1] // n_dev
        me = lax.axis_index('sp')
        chip, core = me // 2, me % 2
        hb = 2 * core + chip
        hbs = [hb, hb ^ 1, hb ^ 2, hb ^ 3]
        toks = [me, me ^ 2, me ^ 1, me ^ 3]

        x_par = over_chip(hidden)
        g_par = over_chip(d_attn)
        x_sib = over_core(hidden)
        g_sib = over_core(d_attn)
        pos = lax.all_gather(positions, 'sp', tiled=True)

        inv_freq = ROPE_BASE ** (-jnp.arange(0, HEAD_DIM, 2, dtype=F32) / HEAD_DIM)
        angles = pos.astype(F32)[:, None] * jnp.repeat(inv_freq, 2)[None, :]
        cos_t = jnp.cos(angles)
        sin_t = jnp.sin(angles) * jnp.where(jnp.arange(HEAD_DIM) % 2 == 0, -1.0, 1.0)[None, :]
        ln_row = ln_weight.reshape(1, dim)

        x_sp = over_core(x_par)
        g_sp = over_core(g_par)

        hq = None
        for tok, x in ((toks[0], hidden), (toks[2], x_sib), (toks[1], x_par), (toks[3], x_sp)):
            idx = jnp.stack([hb, tok]).astype(jnp.int32)
            hq = qkv_block(idx, x, ln_row, w_q, w_k, w_v, cos_t, sin_t, seq, n_dev, hq)
        h_all, qkv = hq
        o_own, o_t, lse = attn_forward(qkv, kv_local)

        gd = None
        for tok, g in ((toks[0], d_attn), (toks[2], g_sib), (toks[1], g_par), (toks[3], g_sp)):
            idx = jnp.stack([hb, tok]).astype(jnp.int32)
            gd = do_block(idx, g, w_o, seq, n_dev, gd)
        g_all, d_o = gd

        def own_rows(val, dev):
            return lax.dynamic_slice_in_dim(val, dev * rows, rows, 0)

        o_par = over_chip(o_own)
        o_tok = [own_rows(o_own, me), own_rows(o_par, me),
                 over_core(own_rows(o_own, me ^ 1)), over_core(own_rows(o_par, me ^ 1))]
        wo_perm = jnp.concatenate([lax.dynamic_slice_in_dim(w_o, b * cq, cq, 0) for b in hbs], axis=0)
        attn_out = jnp.dot(jnp.concatenate(o_tok, axis=1), wo_perm, preferred_element_type=F32).astype(BF16)

        def token_dot(lhs, rhs):
            return mm(lhs, rhs, ((0,), (0,))).astype(BF16)

        dwo_own = token_dot(o_own, g_all)
        dwo_par = token_dot(o_par, g_all)
        d_w_o = jnp.zeros(w_o.shape, BF16)
        for b, piece in zip(hbs, (dwo_own, dwo_par, over_core(dwo_own), over_core(dwo_par))):
            d_w_o = lax.dynamic_update_slice_in_dim(d_w_o, piece, b * cq, 0)

        d_w_q = jnp.zeros(w_q.shape, BF16)
        d_w_k = jnp.zeros(w_k.shape, BF16)
        d_w_v = jnp.zeros(w_v.shape, BF16)
        dhs = []
        for t in range(kv_local):
            gr_own = attn_backward(qkv, d_o, o_t, lse, cos_t, sin_t, kv_local, t)
            gr_par = over_chip(gr_own)
            gr_tok = [own_rows(gr_own, me), own_rows(gr_par, me),
                      over_core(own_rows(gr_own, me ^ 1)), over_core(own_rows(gr_par, me ^ 1))]
            parts = []
            for b in hbs:
                parts.append(lax.dynamic_slice_in_dim(w_q, b * cq + t * wide, wide, 1))
                parts.append(lax.dynamic_slice_in_dim(w_k, b * ck + t * HEAD_DIM, HEAD_DIM, 1))
                parts.append(lax.dynamic_slice_in_dim(w_v, b * ck + t * HEAD_DIM, HEAD_DIM, 1))
            w_perm = jnp.concatenate(parts, axis=1)
            dhs.append(mm(jnp.concatenate(gr_tok, axis=1), w_perm, ((1,), (1,))))
            dw_own = token_dot(h_all, gr_own)
            dw_par = token_dot(h_all, gr_par)
            for b, piece in zip(hbs, (dw_own, dw_par, over_core(dw_own), over_core(dw_par))):
                d_w_q = lax.dynamic_update_slice_in_dim(d_w_q, piece[:, :wide], b * cq + t * wide, 1)
                d_w_k = lax.dynamic_update_slice_in_dim(d_w_k, piece[:, wide:wide + HEAD_DIM], b * ck + t * HEAD_DIM, 1)
                d_w_v = lax.dynamic_update_slice_in_dim(d_w_v, piece[:, wide + HEAD_DIM:], b * ck + t * HEAD_DIM, 1)

        d_hid, d_lnw = ln_backward(dhs[0], dhs[1], hidden, ln_row)
        d_lnw = d_lnw + over_core(d_lnw)
        d_lnw = d_lnw + over_chip(d_lnw)
        return (attn_out, d_hid, d_lnw.reshape(dim).astype(BF16), d_w_q, d_w_k, d_w_v, d_w_o)

    return jax.shard_map(layer, mesh=mesh,
                         in_specs=(row_spec, pos_spec, row_spec, P(None), full_spec, full_spec, full_spec, full_spec),
                         out_specs=(row_spec, row_spec, P('dp'), grad_spec, grad_spec, grad_spec, grad_spec),
                         check_vma=False)
```

time: 5310 us -> 1330 us (0.25)
  matrix products: 2980 us -> 227 us
  blocking collectives: 1690 us -> 272 us
  Pallas kernels: 0 us -> 485 us
  other arithmetic: 135 us -> 12.4 us
  local copies, waits for them, and re-layouts: 252 us -> 150 us
    dot_general x172 -> x9, matrix products: 2300 us -> 227 us  [the longest x8 202 us: mm(): lax.dot_general(lhs, rhs, (dims, ((), ())), preferred_element_type=F32)]
    psum x1 -> x0, blocking collectives: 1690 us -> none  [local_step(): grad_sums = lax.psum((d_lnw, dw_q, dw_k, dw_v, dw_o), 'sp')]
    sub x64 -> x0, matrix products: 682 us -> none  [block_probs(): return jax.nn.softmax(scores, axis=-1)]
    pallas_call x0 -> x12, Pallas kernels: none -> 485 us  [the longest x2 199 us: attn_backward(): pl.pallas_call(bwd_kernel, grid=(nq,), in_specs=[pl.BlockSpec((BQ, wide),...]
    all_gather x0 -> x1, blocking collectives: none -> 272 us  [layer(): pos = lax.all_gather(positions, 'sp', tiled=True)]
    ppermute x0 -> x23, waiting for transfers between devices: none -> 168 us  [the longest x6 168 us: over_chip(): return lax.ppermute(val, 'sp', [(i, i ^ 2) for i in range(n_dev)])]
    all_to_all x8 -> x0, waiting for transfers between devices: 151 us -> none  [the longest x1 57.3 us: local_step(): q_heads = lax.all_to_all(q_rot, 'sp', 1, 0, tiled=True)]
    another operation x8 -> x4, other arithmetic: 74.4 us -> 2.36 us  [layer(): idx = jnp.stack([hb, tok]).astype(jnp.int32)]
  transfers between devices with their start and end apart: 8 -> 23, of which waited for: 4 -> 2; matrix products, arithmetic and copies ran while one was open for 18% -> 29% of each run, Pallas kernels for 0% -> 21%
where the time goes in v1:
time: 1330 us
  Pallas kernels  485 us (36%)
  blocking collectives  272 us (20%)
  matrix products  227 us (17%)
  waiting for transfers between devices  168 us (13%)
  local copies, waits for them, and re-layouts  150 us (11%)
    all_gather x1, blocking collectives, layer(): pos = lax.all_gather(positions, 'sp', tiled=True)  272 us
    dot_general x8, matrix products, mm(): lax.dot_general(lhs, rhs, (dims, ((), ())), preferred_element_type=F32)  202 us
    pallas_call x2, Pallas kernels, attn_backward(): pl.pallas_call(bwd_kernel, grid=(nq,), in_specs=[pl.BlockSpec((BQ, wide),...  199 us
    ppermute x6, waiting for transfers between devices, over_chip(): return lax.ppermute(val, 'sp', [(i, i ^ 2) for i in range(n_dev)])  168 us
    pallas_call x1, Pallas kernels, attn_forward(): pl.pallas_call(fwd_kernel, grid=(kv_local, nq), in_specs=[pl.BlockSpec((B...  153 us
    pallas_call x4, Pallas kernels, qkv_block(): pl.pallas_call(qkv_kernel, out_shape=(jax.ShapeDtypeStruct((seq, dim), BF...  73.4 us
    pallas_call x4, Pallas kernels, do_block(): pl.pallas_call(do_kernel, out_shape=(jax.ShapeDtypeStruct((seq, dim), BF1...  42.3 us
    unnamed x47, local copies, waits for them, and re-layouts  33.6 us
  transfers between devices with their start and end apart: 23, of which 2 were waited for; matrix products, arithmetic and copies ran while one was open for 29% of the time, Pallas kernels for 21%

profile of v1, /device:TPU:0, one launch (start us, length us, event | category | flops | bytes accessed | tf_op | source)
XLA Modules:
  0.0 1326.7 jit_solution(8821802039191875236)
XLA Ops:
  0.6 3.3 collective-permute-start
  4.7 271.8 %all_gather.3 = s32[4096]{0:T(1024)S(1)} all-gather(s32[1024]{0:T(1024)} %param.9), channel_id=1, replica_groups=mesh['dp'=2,'sp'=4] {'sp'}, dimensions={0}, use_global_device_ids=true | all-gather | bytes 20480 | tf_op jit(solution)/shard_map/all_gather | solution.py:400
  279.6 5.3 dynamic-slice_dynamic-update-slice_fusion.3
  288.3 6.0 dynamic-slice_dynamic-update-slice_fusion.2
  311.0 10.7 d_o.4
  321.7 9.3 fusion.36
  331.1 18.3 %ln_qkv.4 = (bf16[4096,3072]{1,0:T(8,128)(2,1)}, bf16[4096,1280]{1,0:T(8,128)(2,1)}) custom-call(s32[2]{0:T(128)} %pad_add_fusion.3.idx, bf16[1024,3072]{1,0:T(8,128)(2,1)} %x_ref.3, bf16[1,3072]{1,0:T(2,128)(2,1)} %reshape.32.lnw_ref, bf16[3072,3072]{1,0:T(8,128)(2,1)} %wq_ref.7, bf16[3072,1024]{1,0:T(8,128)(2,1)} %wk_ref.7, bf16[3072,1024]{1,0:T(8,128)(2,1)} %wv_ref.7, ...), custom_call_target="tpu_custom_call" | custom-call | flops 8053063680 | bytes 23068672 | tf_op jit(solution)/shard_map/ln_qkv/pallas_call | solution.py:82
  349.4 13.8 %constant_dynamic-slice_fusion.11 = (bf16[768,3072]{1,0:T(8,128)(2,1)}, bf16[768,3072]{1,0:T(8,128)(2,1)}, bf16[768,3072]{1,0:T(8,128)(2,1)}, bf16[768,3072]{1,0:T(8,128)(2,1)}) fusion(bf16[3072,3072]{1,0:T(8,128)(2,1)} %wo_ref.7, s32[]{:T(128)S(6)} %select_n.71, s32[]{:T(128)S(6)} %select_n.74, s32[]{:T(128)S(6)} %select_n.73, s32[]{:T(128)S(6)} %select_n.72), kind=kLoop, calls=%fused_computation.104 | loop fusion | bytes 37748752 | tf_op jit(solution)/shard_map/dynamic_slice | solution.py:430
  363.7 10.5 d_o.5
  374.2 10.5 d_o.6
  384.7 18.3 %ln_qkv.5 = (bf16[4096,3072]{1,0:T(8,128)(2,1)}, bf16[4096,1280]{1,0:T(8,128)(2,1)}) custom-call(s32[2]{0:T(128)} %pad_add_fusion.2.idx, bf16[1024,3072]{1,0:T(8,128)(2,1)} %collective-permute-done.2.x_ref, bf16[1,3072]{1,0:T(2,128)(2,1)} %reshape.32.lnw_ref, bf16[3072,3072]{1,0:T(8,128)(2,1)} %wq_ref.7, ...), custom_call_target="tpu_custom_call", output_to_operand_aliasing={{0}: (8, {}), {1}: (9, {})} | custom-call | flops 8053063680 | bytes 23068672 | tf_op jit(solution)/shard_map/ln_qkv/pallas_call | solution.py:82
  403.0 18.5 %ln_qkv.6 = (bf16[4096,3072]{1,0:T(8,128)(2,1)}, bf16[4096,1280]{1,0:T(8,128)(2,1)}) custom-call(s32[2]{0:T(128)} %pad_add_fusion.1.idx, bf16[1024,3072]{1,0:T(8,128)(2,1)} %collective-permute-done.x_ref, bf16[1,3072]{1,0:T(2,128)(2,1)} %reshape.32.lnw_ref, bf16[3072,3072]{1,0:T(8,128)(2,1)} %wq_ref.7, ...), custom_call_target="tpu_custom_call", output_to_operand_aliasing={{0}: (8, {}), {1}: (9, {})} | custom-call | flops 8053063680 | bytes 23068672 | tf_op jit(solution)/shard_map/ln_qkv/pallas_call | solution.py:82
  421.5 18.3 %ln_qkv.7 = (bf16[4096,3072]{1,0:T(8,128)(2,1)}, bf16[4096,1280]{1,0:T(8,128)(2,1)}) custom-call(s32[2]{0:T(128)} %pad_add_fusion.idx, bf16[1024,3072]{1,0:T(8,128)(2,1)} %collective-permute-done.1.x_ref, bf16[1,3072]{1,0:T(2,128)(2,1)} %reshape.32.lnw_ref, bf16[3072,3072]{1,0:T(8,128)(2,1)} %wq_ref.7, ...), custom_call_target="tpu_custom_call", output_to_operand_aliasing={{0}: (8, {}), {1}: (9, {})} | custom-call | flops 8053063680 | bytes 23068672 | tf_op jit(solution)/shard_map/ln_qkv/pallas_call | solution.py:82
  439.8 153.1 %attn_fwd.1 = (bf16[4096,768]{1,0:T(8,128)(2,1)}, f32[2,16,128,768]{3,2,1,0:T(8,128)}, f32[2,16,1,768]{3,2,1,0:T(1,128)}) custom-call(bf16[4096,1280]{1,0:T(8,128)(2,1)} %get-tuple-element.34.q_ref.k_ref.v_ref, bf16[4096,1280]{1,0:T(8,128)(2,1)} %get-tuple-element.34.q_ref.k_ref.v_ref, bf16[4096,1280]{1,0:T(8,128)(2,1)} %get-tuple-element.34.q_ref.k_ref.v_ref), custom_call_target="tpu_custom_call" | custom-call | flops 51539607552 | bytes 25165824 | tf_op jit(solution)/shard_map/attn_fwd/pallas_call | solution.py:196
  592.9 10.5 d_o.7
  603.4 99.2 %attn_bwd.2 = bf16[4096,640]{1,0:T(8,128)(2,1)} custom-call(bf16[4096,1280]{1,0:T(8,128)(2,1)} %get-tuple-element.34.q_ref.k_ref.v_ref, bf16[4096,1280]{1,0:T(8,128)(2,1)} %get-tuple-element.34.q_ref.k_ref.v_ref, bf16[4096,1280]{1,0:T(8,128)(2,1)} %get-tuple-element.34.q_ref.k_ref.v_ref, bf16[4096,768]{1,0:T(8,128)(2,1)} %get-tuple-element.42.do_ref, ...), custom_call_target="tpu_custom_call" | custom-call | flops 64424509440 | bytes 25165824 | tf_op jit(solution)/shard_map/attn_bwd/pallas_call | solution.py:301
  702.6 99.6 %attn_bwd.3 = bf16[4096,640]{1,0:T(8,128)(2,1)} custom-call(bf16[4096,1280]{1,0:T(8,128)(2,1)} %get-tuple-element.34.q_ref.k_ref.v_ref, bf16[4096,1280]{1,0:T(8,128)(2,1)} %get-tuple-element.34.q_ref.k_ref.v_ref, bf16[4096,1280]{1,0:T(8,128)(2,1)} %get-tuple-element.34.q_ref.k_ref.v_ref, bf16[4096,768]{1,0:T(8,128)(2,1)} %get-tuple-element.42.do_ref, ...), custom_call_target="tpu_custom_call" | custom-call | flops 64424509440 | bytes 25165824 | tf_op jit(solution)/shard_map/attn_bwd/pallas_call | solution.py:301
  804.3 3.5 constant_dynamic-slice_fusion.3
  810.3 3.9 constant_dynamic-slice_fusion.15
  814.1 9.4 broadcast.43.clone.1
  823.5 3.4 copy-done.1
  826.9 23.7 %constant_dynamic-update-slice_fusion.3 = (bf16[3072,3072]{1,0:T(8,128)(2,1)}, bf16[768,3072]{1,0:T(8,128)(2,1)}) fusion(bf16[3072,3072]{1,0:T(8,128)(2,1)} %broadcast.43.clone.1, s32[]{:T(128)S(6)} %select_n.71, bf16[4096,768]{1,0:T(8,128)(2,1)} %get-tuple-element.35, bf16[4096,3072]{1,0:T(8,128)(2,1)S(1)} %copy-done.1), kind=kOutput, calls=%fused_computation.92 | convolution fusion | flops 19329712128 | bytes 40894468 | tf_op jit(solution)/shard_map/dot_general | solution.py:27
  850.6 25.9 %convolution_convert_fusion.5 = bf16[3072,640]{1,0:T(8,128)(2,1)} fusion(bf16[4096,3072]{1,0:T(8,128)(2,1)} %get-tuple-element.47, bf16[4096,640]{1,0:T(8,128)(2,1)} %attn_bwd.2), kind=kOutput, calls=%fused_computation.37 | convolution fusion | flops 16108093440 | bytes 34340864 | tf_op jit(solution)/shard_map/dot_general | solution.py:27
  877.0 26.0 %convolution_convert_fusion.3 = bf16[3072,640]{1,0:T(8,128)(2,1)} fusion(bf16[4096,3072]{1,0:T(8,128)(2,1)} %get-tuple-element.47, bf16[4096,640]{1,0:T(8,128)(2,1)} %attn_bwd.3), kind=kOutput, calls=%fused_computation.35 | convolution fusion | flops 16108093440 | bytes 34340864 | tf_op jit(solution)/shard_map/dot_general | solution.py:27
  903.0 3.5 broadcast.44.clone
  910.8 7.3 broadcast.43.clone
  918.0 3.3 slice_dynamic-update-slice_fusion.7
  921.4 27.4 %convolution_convert_fusion.4 = bf16[3072,640]{1,0:T(8,128)(2,1)} fusion(bf16[4096,3072]{1,0:T(8,128)(2,1)S(1)} %bitcast.20, bf16[4096,640]{1,0:T(8,128)(2,1)} %collective-permute-done.9), kind=kOutput, calls=%fused_computation.36 | convolution fusion | flops 16108093440 | bytes 34340864 | tf_op jit(solution)/shard_map/dot_general | solution.py:27
  948.8 82.0 %collective-permute-done.12 = bf16[4096,640]{1,0:T(8,128)(2,1)} collective-permute-done((bf16[4096,640]{1,0:T(8,128)(2,1)}, bf16[4096,640]{1,0:T(8,128)(2,1)}, u32[]{:S(2)}, u32[]{:S(2)}) %collective-permute-start.12) | collective-permute-done | bytes 5242912 | tf_op jit(solution)/shard_map/ppermute | solution.py:378
  1030.9 3.4 constant_dynamic-slice_fusion.2
  1034.3 3.3 slice_dynamic-update-slice_fusion.6
  1039.9 27.6 %convolution_convert_fusion.2 = bf16[3072,640]{1,0:T(8,128)(2,1)} fusion(bf16[4096,3072]{1,0:T(8,128)(2,1)S(1)} %bitcast.20, bf16[4096,640]{1,0:T(8,128)(2,1)} %collective-permute-done.12), kind=kOutput, calls=%fused_computation.34 | convolution fusion | flops 16108093440 | bytes 34340864 | tf_op jit(solution)/shard_map/dot_general | solution.py:27
  1070.4 5.3 constant_dynamic-slice_fusion.6
  1075.8 3.3 slice_dynamic-update-slice_fusion.5
  1079.1 85.9 %collective-permute-done.3 = bf16[4096,768]{1,0:T(8,128)(2,1)} collective-permute-done((bf16[4096,768]{1,0:T(8,128)(2,1)}, bf16[4096,768]{1,0:T(8,128)(2,1)}, u32[]{:S(2)}, u32[]{:S(2)}) %collective-permute-start.3) | collective-permute-done | bytes 6291488 | tf_op jit(solution)/shard_map/ppermute | solution.py:378
  1164.9 3.8 constant_dynamic-slice_fusion.14
  1170.3 23.1 %fusion.28.dh1_ref = f32[1024,3072]{1,0:T(8,128)} fusion(bf16[3072,2560]{1,0:T(8,128)(2,1)} %get-tuple-element.61, bf16[1024,640]{1,0:T(8,128)(2,1)} %copy-done.11, bf16[1024,640]{1,0:T(8,128)(2,1)} %collective-permute-done.13, bf16[1024,640]{1,0:T(8,128)(2,1)} %get-tuple-element.83, bf16[1024,640]{1,0:T(8,128)(2,1)} %get-tuple-element.81), kind=kOutput, calls=%fused_computation.24 | convolution fusion | flops 16127098880 | bytes 33554432 | tf_op jit(solution)/shard_map/dot_general | solution.py:27
  1193.5 21.7 %fusion.20.dh0_ref = f32[1024,3072]{1,0:T(8,128)} fusion(bf16[3072,2560]{1,0:T(8,128)(2,1)} %get-tuple-element.62, bf16[1024,640]{1,0:T(8,128)(2,1)S(1)} %collective-permute-done.11, bf16[1024,640]{1,0:T(8,128)(2,1)} %collective-permute-done.10, bf16[1024,640]{1,0:T(8,128)(2,1)S(1)} %copy-done.9, bf16[1024,640]{1,0:T(8,128)(2,1)S(1)} %copy-done.8), kind=kOutput, calls=%fused_computation.16 | convolution fusion | flops 16127098880 | bytes 33554432 | tf_op jit(solution)/shard_map/dot_general | solution.py:27
  1215.2 17.6 %ln_bwd.1 = (bf16[1024,3072]{1,0:T(8,128)(2,1)}, f32[1,3072]{1,0:T(1,128)}) custom-call(f32[1024,3072]{1,0:T(8,128)} %fusion.20.dh0_ref, f32[1024,3072]{1,0:T(8,128)} %fusion.28.dh1_ref, bf16[1024,3072]{1,0:T(8,128)(2,1)} %x_ref.3, bf16[1,3072]{1,0:T(2,128)(2,1)} %reshape.32.lnw_ref), custom_call_target="tpu_custom_call" | custom-call | flops 62914560 | bytes 37748736 | tf_op jit(solution)/shard_map/ln_bwd/pallas_call | solution.py:357
  1233.3 26.6 %constant_dynamic-update-slice_fusion.2 = (bf16[3072,3072]{1,0:T(8,128)(2,1)}, bf16[768,3072]{1,0:T(8,128)(2,1)}) fusion(bf16[3072,3072]{1,0:T(8,128)(2,1)} %get-tuple-element.105, s32[]{:T(128)S(6)} %select_n.72, bf16[4096,768]{1,0:T(8,128)(2,1)} %collective-permute-done.3, bf16[4096,3072]{1,0:T(8,128)(2,1)} %get-tuple-element.48), kind=kOutput, calls=%fused_computation.91 | convolution fusion | flops 19329712128 | bytes 40894468 | tf_op jit(solution)/shard_map/dot_general | solution.py:27
  1261.0 4.8 constant_dynamic-update-slice_fusion.1
  1267.0 25.0 %fusion.15 = bf16[1024,3072]{1,0:T(8,128)(2,1)} fusion(bf16[768,3072]{1,0:T(8,128)(2,1)} %get-tuple-element.58, bf16[768,3072]{1,0:T(8,128)(2,1)} %get-tuple-element.59, bf16[768,3072]{1,0:T(8,128)(2,1)} %get-tuple-element.60, bf16[768,3072]{1,0:T(8,128)(2,1)} %get-tuple-element.57, bf16[1024,768]{1,0:T(8,128)(2,1)} %collective-permute-done.5, ...), kind=kOutput, calls=%fused_computation.15 | convolution fusion | flops 19431161856 | bytes 31457280 | tf_op jit(solution)/shard_map/dot_general | solution.py:431
  1305.1 3.3 slice_dynamic-update-slice_fusion.4
  1308.4 3.3 slice_dynamic-update-slice_fusion.3
  1311.7 3.3 slice_dynamic-update-slice_fusion.2
  1315.0 3.3 slice_dynamic-update-slice_fusion.1
  1318.3 3.3 slice_dynamic-update-slice_fusion
  1321.6 4.8 constant_dynamic-update-slice_fusion
  (112 shorter events, 56.5 us)
Async XLA Ops:
  0.6 306.5 %collective-permute-start = (bf16[1024,3072]{1,0:T(8,128)(2,1)}, bf16[1024,3072]{1,0:T(8,128)(2,1)}, u32[]{:S(2)}, u32[]{:S(2)}) collective-permute-start(bf16[1024,3072]{1,0:T(8,128)(2,1)} %x_ref.3), channel_id=1, source_target_pairs={{0,2},{1,3},{2,0},{3,1},{4,6},{5,7},{6,4},{7,5}} | collective-permute-start | bytes 18874376 | tf_op jit(solution)/shard_map/ppermute | solution.py:378
  4.0 359.7 %collective-permute-start.8 = (bf16[1024,3072]{1,0:T(8,128)(2,1)}, bf16[1024,3072]{1,0:T(8,128)(2,1)}, u32[]{:S(2)}, u32[]{:S(2)}) collective-permute-start(bf16[1024,3072]{1,0:T(8,128)(2,1)} %g_ref.1), channel_id=1, source_target_pairs={{0,1},{1,0},{2,3},{3,2},{4,5},{5,4},{6,7},{7,6}} | collective-permute-start | bytes 18874376 | tf_op jit(solution)/shard_map/ppermute | solution.py:381
  4.0 359.2 %collective-permute-start.6 = (bf16[1024,3072]{1,0:T(8,128)(2,1)}, bf16[1024,3072]{1,0:T(8,128)(2,1)}, u32[]{:S(2)}, u32[]{:S(2)}) collective-permute-start(bf16[1024,3072]{1,0:T(8,128)(2,1)} %g_ref.1), channel_id=1, source_target_pairs={{0,2},{1,3},{2,0},{3,1},{4,6},{5,7},{6,4},{7,5}} | collective-permute-start | bytes 18874376 | tf_op jit(solution)/shard_map/ppermute | solution.py:378
  4.0 380.7 %collective-permute-start.2 = (bf16[1024,3072]{1,0:T(8,128)(2,1)}, bf16[1024,3072]{1,0:T(8,128)(2,1)}, u32[]{:S(2)}, u32[]{:S(2)}) collective-permute-start(bf16[1024,3072]{1,0:T(8,128)(2,1)} %x_ref.3), channel_id=1, source_target_pairs={{0,1},{1,0},{2,3},{3,2},{4,5},{5,4},{6,7},{7,6}} | collective-permute-start | bytes 18874376 | tf_op jit(solution)/shard_map/ppermute | solution.py:381
  277.8 7.1 copy-start.2
  279.6 6.9 copy-start.3
  286.5 11.0 copy-start
  307.1 114.4 %collective-permute-start.1 = (bf16[1024,3072]{1,0:T(8,128)(2,1)}, bf16[1024,3072]{1,0:T(8,128)(2,1)}, u32[]{:S(2)}, u32[]{:S(2)}) collective-permute-start(bf16[1024,3072]{1,0:T(8,128)(2,1)} %collective-permute-done.x_ref), channel_id=1, source_target_pairs={{0,1},{1,0},{2,3},{3,2},{4,5},{5,4},{6,7},{7,6}} | collective-permute-start | bytes 18874376 | tf_op jit(solution)/shard_map/ppermute | solution.py:381
  363.2 229.7 %collective-permute-start.7 = (bf16[1024,3072]{1,0:T(8,128)(2,1)}, bf16[1024,3072]{1,0:T(8,128)(2,1)}, u32[]{:S(2)}, u32[]{:S(2)}) collective-permute-start(bf16[1024,3072]{1,0:T(8,128)(2,1)} %collective-permute-done.6.g_ref), channel_id=1, source_target_pairs={{0,1},{1,0},{2,3},{3,2},{4,5},{5,4},{6,7},{7,6}} | collective-permute-start | bytes 18874376 | tf_op jit(solution)/shard_map/ppermute | solution.py:381
  802.3 5.5 copy-start.7
  802.3 119.1 %collective-permute-start.9 = (bf16[4096,640]{1,0:T(8,128)(2,1)}, bf16[4096,640]{1,0:T(8,128)(2,1)}, u32[]{:S(2)}, u32[]{:S(2)}) collective-permute-start(bf16[4096,640]{1,0:T(8,128)(2,1)} %attn_bwd.2), channel_id=1, source_target_pairs={{0,2},{1,3},{2,0},{3,1},{4,6},{5,7},{6,4},{7,5}} | collective-permute-start | bytes 15728648 | tf_op jit(solution)/shard_map/ppermute | solution.py:378
  803.1 227.8 %collective-permute-start.12 = (bf16[4096,640]{1,0:T(8,128)(2,1)}, bf16[4096,640]{1,0:T(8,128)(2,1)}, u32[]{:S(2)}, u32[]{:S(2)}) collective-permute-start(bf16[4096,640]{1,0:T(8,128)(2,1)} %attn_bwd.3), channel_id=1, source_target_pairs={{0,2},{1,3},{2,0},{3,1},{4,6},{5,7},{6,4},{7,5}} | collective-permute-start | bytes 15728648 | tf_op jit(solution)/shard_map/ppermute | solution.py:378
  809.5 355.4 %collective-permute-start.3 = (bf16[4096,768]{1,0:T(8,128)(2,1)}, bf16[4096,768]{1,0:T(8,128)(2,1)}, u32[]{:S(2)}, u32[]{:S(2)}) collective-permute-start(bf16[4096,768]{1,0:T(8,128)(2,1)} %get-tuple-element.35), channel_id=1, source_target_pairs={{0,2},{1,3},{2,0},{3,1},{4,6},{5,7},{6,4},{7,5}} | collective-permute-start | bytes 18874376 | tf_op jit(solution)/shard_map/ppermute | solution.py:378
  810.3 16.6 %copy-start.1 = (bf16[4096,3072]{1,0:T(8,128)(2,1)S(1)}, bf16[4096,3072]{1,0:T(8,128)(2,1)}, u32[]{:S(2)}) copy-start(bf16[4096,3072]{1,0:T(8,128)(2,1)} %get-tuple-element.48) | copy-start | bytes 75497472
  850.6 409.4 %collective-permute-start.21 = (bf16[768,3072]{1,0:T(8,128)(2,1)}, bf16[768,3072]{1,0:T(8,128)(2,1)}, u32[]{:S(2)}, u32[]{:S(2)}) collective-permute-start(bf16[768,3072]{1,0:T(8,128)(2,1)} %get-tuple-element.106), channel_id=1, source_target_pairs={{0,1},{1,0},{2,3},{3,2},{4,5},{5,4},{6,7},{7,6}} | collective-permute-start | bytes 14155784 | tf_op jit(solution)/shard_map/ppermute | solution.py:381
  876.5 191.0 %collective-permute-start.17 = (bf16[3072,640]{1,0:T(8,128)(2,1)}, bf16[3072,640]{1,0:T(8,128)(2,1)}, u32[]{:S(2)}, u32[]{:S(2)}) collective-permute-start(bf16[3072,640]{1,0:T(8,128)(2,1)} %convolution_convert_fusion.5), channel_id=1, source_target_pairs={{0,1},{1,0},{2,3},{3,2},{4,5},{5,4},{6,7},{7,6}} | collective-permute-start | bytes 11796488 | tf_op jit(solution)/shard_map/ppermute | solution.py:381
  877.0 44.4 %slice-start = ((s8[25165824]{0:T(1024)(128)(4,1)}), s8[4194304]{0:T(1024)(128)(4,1)S(1)}, s32[]{:S(2)}) async-start(s8[25165824]{0:T(1024)(128)(4,1)} %bitcast.19), calls=%async_computation | async-start | bytes 8388608
  877.0 44.4 %slice-start.1 = ((s8[25165824]{0:T(1024)(128)(4,1)}), s8[4194304]{0:T(1024)(128)(4,1)S(1)}, s32[]{:S(2)}) async-start(s8[25165824]{0:T(1024)(128)(4,1)} %bitcast.19), calls=%async_computation.1 | async-start | bytes 8388608
  877.0 44.4 %slice-start.2 = ((s8[25165824]{0:T(1024)(128)(4,1)}), s8[4194304]{0:T(1024)(128)(4,1)S(1)}, s32[]{:S(2)}) async-start(s8[25165824]{0:T(1024)(128)(4,1)} %bitcast.19), calls=%async_computation.2 | async-start | bytes 8388608
  877.0 44.4 %slice-start.3 = ((s8[25165824]{0:T(1024)(128)(4,1)}), s8[4194304]{0:T(1024)(128)(4,1)S(1)}, s32[]{:S(2)}) async-start(s8[25165824]{0:T(1024)(128)(4,1)} %bitcast.19), calls=%async_computation.3 | async-start | bytes 8388608
  903.0 18.4 %slice-start.4 = ((s8[25165824]{0:T(1024)(128)(4,1)}), s8[4194304]{0:T(1024)(128)(4,1)S(1)}, s32[]{:S(2)}) async-start(s8[25165824]{0:T(1024)(128)(4,1)} %bitcast.19), calls=%async_computation.4 | async-start | bytes 8388608
  910.8 10.6 slice-start.5
  921.3 378.5 %collective-permute-start.19 = (bf16[3072,640]{1,0:T(8,128)(2,1)}, bf16[3072,640]{1,0:T(8,128)(2,1)}, u32[]{:S(2)}, u32[]{:S(2)}) collective-permute-start(bf16[3072,640]{1,0:T(8,128)(2,1)} %convolution_convert_fusion.3), channel_id=1, source_target_pairs={{0,1},{1,0},{2,3},{3,2},{4,5},{5,4},{6,7},{7,6}} | collective-permute-start | bytes 11796488 | tf_op jit(solution)/shard_map/ppermute | solution.py:381
  1030.9 137.8 %collective-permute-start.13 = (bf16[1024,640]{1,0:T(8,128)(2,1)}, bf16[1024,640]{1,0:T(8,128)(2,1)}, u32[]{:S(2)}, u32[]{:S(2)}) collective-permute-start(bf16[1024,640]{1,0:T(8,128)(2,1)} %get-tuple-element.82), channel_id=1, source_target_pairs={{0,1},{1,0},{2,3},{3,2},{4,5},{5,4},{6,7},{7,6}} | collective-permute-start | bytes 3932168 | tf_op jit(solution)/shard_map/ppermute | solution.py:381
  1067.5 101.7 %collective-permute-start.14 = (bf16[1024,640]{1,0:T(8,128)(2,1)}, bf16[1024,640]{1,0:T(8,128)(2,1)S(1)}, u32[]{:S(2)}, u32[]{:S(2)}) collective-permute-start(bf16[1024,640]{1,0:T(8,128)(2,1)} %get-tuple-element.84), channel_id=1, source_target_pairs={{0,1},{1,0},{2,3},{3,2},{4,5},{5,4},{6,7},{7,6}} | collective-permute-start | bytes 3932168 | tf_op jit(solution)/shard_map/ppermute | solution.py:381
  1070.4 98.3 %copy-start.4 = (bf16[3072,1024]{1,0:T(8,128)(2,1)}, bf16[3072,1024]{1,0:T(8,128)(2,1)S(1)}, u32[]{:S(2)}) copy-start(bf16[3072,1024]{1,0:T(8,128)(2,1)S(1)} %get-tuple-element.100) | copy-start | bytes 18874372
  1164.9 28.5 %collective-permute-start.10 = (bf16[1024,640]{1,0:T(8,128)(2,1)}, bf16[1024,640]{1,0:T(8,128)(2,1)}, u32[]{:S(2)}, u32[]{:S(2)}) collective-permute-start(bf16[1024,640]{1,0:T(8,128)(2,1)} %get-tuple-element.86), channel_id=1, source_target_pairs={{0,1},{1,0},{2,3},{3,2},{4,5},{5,4},{6,7},{7,6}} | collective-permute-start | bytes 3932168 | tf_op jit(solution)/shard_map/ppermute | solution.py:381
  1168.7 97.9 %collective-permute-start.4 = (bf16[1024,768]{1,0:T(8,128)(2,1)}, bf16[1024,768]{1,0:T(8,128)(2,1)}, u32[]{:S(2)}, u32[]{:S(2)}) collective-permute-start(bf16[1024,768]{1,0:T(8,128)(2,1)} %get-tuple-element.78), channel_id=1, source_target_pairs={{0,1},{1,0},{2,3},{3,2},{4,5},{5,4},{6,7},{7,6}} | collective-permute-start | bytes 4718600 | tf_op jit(solution)/shard_map/ppermute | solution.py:381
  1169.2 1.1 copy-start.11
  1169.2 24.3 %collective-permute-start.11 = (bf16[1024,640]{1,0:T(8,128)(2,1)}, bf16[1024,640]{1,0:T(8,128)(2,1)S(1)}, u32[]{:S(2)}, u32[]{:S(2)}) collective-permute-start(bf16[1024,640]{1,0:T(8,128)(2,1)} %get-tuple-element.88), channel_id=1, source_target_pairs={{0,1},{1,0},{2,3},{3,2},{4,5},{5,4},{6,7},{7,6}} | collective-permute-start | bytes 3932168 | tf_op jit(solution)/shard_map/ppermute | solution.py:381
  1170.3 23.2 %copy-start.8 = (bf16[1024,640]{1,0:T(8,128)(2,1)S(1)}, bf16[1024,640]{1,0:T(8,128)(2,1)}, u32[]{:S(2)}) copy-start(bf16[1024,640]{1,0:T(8,128)(2,1)} %get-tuple-element.85) | copy-start | bytes 3932164
  1170.3 23.2 %copy-start.9 = (bf16[1024,640]{1,0:T(8,128)(2,1)S(1)}, bf16[1024,640]{1,0:T(8,128)(2,1)}, u32[]{:S(2)}) copy-start(bf16[1024,640]{1,0:T(8,128)(2,1)} %get-tuple-element.87) | copy-start | bytes 3932164
  1193.4 73.5 %collective-permute-start.5 = (bf16[1024,768]{1,0:T(8,128)(2,1)}, bf16[1024,768]{1,0:T(8,128)(2,1)}, u32[]{:S(2)}, u32[]{:S(2)}) collective-permute-start(bf16[1024,768]{1,0:T(8,128)(2,1)} %get-tuple-element.80), channel_id=1, source_target_pairs={{0,1},{1,0},{2,3},{3,2},{4,5},{5,4},{6,7},{7,6}} | collective-permute-start | bytes 4718600 | tf_op jit(solution)/shard_map/ppermute | solution.py:381
  1232.8 27.1 %collective-permute-start.15 = (f32[1,3072]{1,0:T(1,128)}, f32[1,3072]{1,0:T(1,128)S(1)}, u32[]{:S(2)}, u32[]{:S(2)}) collective-permute-start(f32[1,3072]{1,0:T(1,128)} %get-tuple-element.46), channel_id=1, source_target_pairs={{0,1},{1,0},{2,3},{3,2},{4,5},{5,4},{6,7},{7,6}} | collective-permute-start | bytes 36872 | tf_op jit(solution)/shard_map/ppermute | solution.py:381
  1233.3 26.7 %copy-start.10 = (f32[1,3072]{1,0:T(1,128)S(1)}, f32[1,3072]{1,0:T(1,128)}, u32[]{:S(2)}) copy-start(f32[1,3072]{1,0:T(1,128)} %get-tuple-element.46) | copy-start | bytes 36868
  1259.9 7.1 copy-start.5
  1259.9 7.1 copy-start.6
  1259.9 32.1 %collective-permute-start.18 = (bf16[3072,640]{1,0:T(8,128)(2,1)}, bf16[3072,640]{1,0:T(8,128)(2,1)}, u32[]{:S(2)}, u32[]{:S(2)}) collective-permute-start(bf16[3072,640]{1,0:T(8,128)(2,1)} %convolution_convert_fusion.4), channel_id=1, source_target_pairs={{0,1},{1,0},{2,3},{3,2},{4,5},{5,4},{6,7},{7,6}} | collective-permute-start | bytes 11796488 | tf_op jit(solution)/shard_map/ppermute | solution.py:381
  1260.0 5.8 collective-permute-start.16
  1265.8 36.7 %collective-permute-start.20 = (bf16[3072,640]{1,0:T(8,128)(2,1)}, bf16[3072,640]{1,0:T(8,128)(2,1)}, u32[]{:S(2)}, u32[]{:S(2)}) collective-permute-start(bf16[3072,640]{1,0:T(8,128)(2,1)} %convolution_convert_fusion.2), channel_id=1, source_target_pairs={{0,1},{1,0},{2,3},{3,2},{4,5},{5,4},{6,7},{7,6}} | collective-permute-start | bytes 11796488 | tf_op jit(solution)/shard_map/ppermute | solution.py:381
  1266.6 55.0 %collective-permute-start.22 = (bf16[768,3072]{1,0:T(8,128)(2,1)}, bf16[768,3072]{1,0:T(8,128)(2,1)}, u32[]{:S(2)}, u32[]{:S(2)}) collective-permute-start(bf16[768,3072]{1,0:T(8,128)(2,1)} %get-tuple-element.108), channel_id=1, source_target_pairs={{0,1},{1,0},{2,3},{3,2},{4,5},{5,4},{6,7},{7,6}} | collective-permute-start | bytes 14155784 | tf_op jit(solution)/shard_map/ppermute | solution.py:381

commit v2 on v1

--- a/solution.py
+++ b/solution.py
@@ -11,7 +11,8 @@
 ROPE_BASE = 10000.0
 REP = 3
 BQ = 256
-BK = 512
+BK = 256
+ROWS = 512
 LOG2E = math.log2(math.e)
 SCALE = HEAD_DIM ** -0.5
 VMEM_BYTES = 60 * 1024 * 1024
@@ -33,62 +34,78 @@
     return val * cos_t + swapped * sin_t
 
 
-def qkv_kernel(idx, x_ref, lnw_ref, wq_ref, wk_ref, wv_ref, cos_ref, sin_ref, *rest):
-    h_ref, qkv_ref = rest[-2:]
+def ln_kernel(x_ref, lnw_ref, h_ref):
     xf = x_ref[...].astype(F32)
     mean = jnp.mean(xf, axis=-1, keepdims=True)
     cen = xf - mean
     var = jnp.mean(cen * cen, axis=-1, keepdims=True)
-    h = (cen * lax.rsqrt(var + LN_EPS) * lnw_ref[...].astype(F32)).astype(BF16)
-    h_ref[...] = h
+    h_ref[...] = (cen * lax.rsqrt(var + LN_EPS) * lnw_ref[...].astype(F32)).astype(BF16)
+
+
+def ln_forward(x, ln_w):
+    rows, dim = x.shape
+    blk = 128
+    return pl.pallas_call(
+        ln_kernel,
+        grid=(rows // blk,),
+        in_specs=[pl.BlockSpec((blk, dim), lambda i: (i, 0)), pl.BlockSpec((1, dim), lambda i: (0, 0))],
+        out_specs=pl.BlockSpec((blk, dim), lambda i: (i, 0)),
+        out_shape=jax.ShapeDtypeStruct((rows, dim), BF16),
+        compiler_params=pltpu.CompilerParams(dimension_semantics=("arbitrary",)),
+        cost_estimate=cost(10 * rows * dim, 4 * rows * dim),
+        name="ln_fwd",
+    )(x, ln_w)
+
+
+def qkv_kernel(idx, h_ref, wq_ref, wk_ref, wv_ref, cos_ref, sin_ref, *rest):
+    hall_ref, qkv_ref = rest[-2:]
+    h = h_ref[...]
+    hall_ref[...] = h
     cos_t = cos_ref[...]
     sin_t = sin_ref[...]
     nq = wq_ref.shape[1]
     nk = wk_ref.shape[1]
-    q = mm(h, wq_ref[...], ((1,), (0,)))
-    for n in range(nq // HEAD_DIM):
-        sl = slice(n * HEAD_DIM, (n + 1) * HEAD_DIM)
-        qkv_ref[:, sl] = rotate(q[:, sl], cos_t, sin_t).astype(BF16)
-    k = mm(h, wk_ref[...], ((1,), (0,)))
-    for n in range(nk // HEAD_DIM):
-        sl = slice(n * HEAD_DIM, (n + 1) * HEAD_DIM)
-        qkv_ref[:, nq + n * HEAD_DIM:nq + (n + 1) * HEAD_DIM] = rotate(k[:, sl], cos_t, sin_t).astype(BF16)
+    step = 2 * HEAD_DIM
+    for start in range(0, nq + nk, step):
+        w = wq_ref[:, start:start + step] if start < nq else wk_ref[:, start - nq:start - nq + step]
+        val = mm(h, w, ((1,), (0,)))
+        for n in range(2):
+            sl = slice(n * HEAD_DIM, (n + 1) * HEAD_DIM)
+            qkv_ref[:, start + n * HEAD_DIM:start + (n + 1) * HEAD_DIM] = rotate(val[:, sl], cos_t, sin_t).astype(BF16)
     qkv_ref[:, nq + nk:] = mm(h, wv_ref[...], ((1,), (0,))).astype(BF16)
 
 
-def qkv_block(idx, x, ln_w, w_q, w_k, w_v, cos_t, sin_t, seq, n_dev, prev):
-    rows, dim = x.shape
+def qkv_block(idx, h, w_q, w_k, w_v, cos_t, sin_t, seq, n_dev, prev):
+    rows, dim = h.shape
     cq, ck = w_q.shape[1] // n_dev, w_k.shape[1] // n_dev
-    per = rows // BQ
-    const = lambda i, ix: (0, 0)
+    per = rows // ROWS
     head = lambda i, ix: (0, ix[0])
     here = lambda i, ix: (ix[1] * per + i, 0)
     in_specs = [
-        pl.BlockSpec((BQ, dim), lambda i, ix: (i, 0)),
-        pl.BlockSpec((1, dim), const),
+        pl.BlockSpec((ROWS, dim), lambda i, ix: (i, 0)),
         pl.BlockSpec((dim, cq), head),
         pl.BlockSpec((dim, ck), head),
         pl.BlockSpec((dim, ck), head),
-        pl.BlockSpec((BQ, HEAD_DIM), here),
-        pl.BlockSpec((BQ, HEAD_DIM), here),
+        pl.BlockSpec((ROWS, HEAD_DIM), here),
+        pl.BlockSpec((ROWS, HEAD_DIM), here),
     ]
-    args = [idx, x, ln_w, w_q, w_k, w_v, cos_t, sin_t]
+    args = [idx, h, w_q, w_k, w_v, cos_t, sin_t]
     aliases = {}
     if prev is not None:
         in_specs += [pl.BlockSpec(memory_space=pl.ANY)] * 2
         args += list(prev)
-        aliases = {8: 0, 9: 1}
+        aliases = {7: 0, 8: 1}
     cols = cq + 2 * ck
     return pl.pallas_call(
         qkv_kernel,
         out_shape=(jax.ShapeDtypeStruct((seq, dim), BF16), jax.ShapeDtypeStruct((seq, cols), BF16)),
         grid_spec=pltpu.PrefetchScalarGridSpec(
             num_scalar_prefetch=1, grid=(per,), in_specs=in_specs,
-            out_specs=(pl.BlockSpec((BQ, dim), here), pl.BlockSpec((BQ, cols), here))),
+            out_specs=(pl.BlockSpec((ROWS, dim), here), pl.BlockSpec((ROWS, cols), here))),
         input_output_aliases=aliases,
         compiler_params=pltpu.CompilerParams(dimension_semantics=("arbitrary",), vmem_limit_bytes=VMEM_BYTES),
         cost_estimate=cost(2 * rows * dim * cols, 2 * (2 * rows * dim + dim * cols + rows * cols)),
-        name="ln_qkv",
+        name="qkv",
     )(*args)
 
 
@@ -102,10 +119,10 @@
 def do_block(idx, g, w_o, seq, n_dev, prev):
     rows, dim = g.shape
     ce = w_o.shape[0] // n_dev
-    per = rows // BQ
+    per = rows // ROWS
     here = lambda i, ix: (ix[1] * per + i, 0)
     in_specs = [
-        pl.BlockSpec((BQ, dim), lambda i, ix: (i, 0)),
+        pl.BlockSpec((ROWS, dim), lambda i, ix: (i, 0)),
         pl.BlockSpec((ce, dim), lambda i, ix: (ix[0], 0)),
     ]
     args = [idx, g, w_o]
@@ -119,7 +136,7 @@
         out_shape=(jax.ShapeDtypeStruct((seq, dim), BF16), jax.ShapeDtypeStruct((seq, ce), BF16)),
         grid_spec=pltpu.PrefetchScalarGridSpec(
             num_scalar_prefetch=1, grid=(per,), in_specs=in_specs,
-            out_specs=(pl.BlockSpec((BQ, dim), here), pl.BlockSpec((BQ, ce), here))),
+            out_specs=(pl.BlockSpec((ROWS, dim), here), pl.BlockSpec((ROWS, ce), here))),
         input_output_aliases=aliases,
         compiler_params=pltpu.CompilerParams(dimension_semantics=("arbitrary",), vmem_limit_bytes=VMEM_BYTES),
         cost_estimate=cost(2 * rows * dim * ce, 2 * (2 * rows * dim + dim * ce + rows * ce)),
@@ -135,10 +152,8 @@
     return val.astype(F32).T.astype(BF16)
 
 
-def causal(row_start, key_start, shape):
-    key = key_start + lax.broadcasted_iota(jnp.int32, shape, 0)
-    query = row_start + lax.broadcasted_iota(jnp.int32, shape, 1) % BQ
-    return key <= query
+def causal(shape):
+    return lax.broadcasted_iota(jnp.int32, shape, 0) <= lax.broadcasted_iota(jnp.int32, shape, 1) % BQ
 
 
 def fwd_kernel(q_ref, k_ref, v_ref, o_ref, ot_ref, lse_ref, qt_sc, vt_sc, acc_sc, ml_sc):
@@ -159,26 +174,38 @@
     ml_sc[0:1, :] = jnp.full((1, width), -jnp.inf, F32)
     ml_sc[1:2, :] = jnp.zeros((1, width), F32)
 
-    def chunk(j, masked):
-        s = mm(k_ref[pl.ds(j * BK, BK), :], qt_sc[...], ((1,), (0,))) * (SCALE * LOG2E)
+    def chunks(js, masked):
+        scores = [mm(k_ref[pl.ds(j * BK, BK), :], qt_sc[...], ((1,), (0,))) * (SCALE * LOG2E) for j in js]
         if masked:
-            s = jnp.where(causal(blk * BQ, j * BK, s.shape), s, -jnp.inf)
-        m_old = ml_sc[0:1, :]
-        m_new = jnp.maximum(m_old, jnp.max(s, axis=0, keepdims=True))
-        alpha = jnp.exp2(m_old - m_new)
-        p = jnp.exp2(s - m_new)
-        ml_sc[0:1, :] = m_new
-        ml_sc[1:2, :] = ml_sc[1:2, :] * alpha + jnp.sum(p, axis=0, keepdims=True)
-        acc_sc[...] = acc_sc[...] * alpha + mm(vt_sc[j], p.astype(BF16), ((1,), (0,)))
-
-    n_full = (blk * BQ) // BK
+            scores[-1] = jnp.where(causal(scores[-1].shape), scores[-1], -jnp.inf)
+        m = ml_sc[0:1, :]
+        total = ml_sc[1:2, :]
+        acc = acc_sc[...]
+        for j, s in zip(js, scores):
+            m_new = jnp.maximum(m, jnp.max(s, axis=0, keepdims=True))
+            alpha = jnp.exp2(m - m_new)
+            p = jnp.exp2(s - m_new)
+            total = total * alpha + jnp.sum(p, axis=0, keepdims=True)
+            acc = acc * alpha + mm(vt_sc[j], p.astype(BF16), ((1,), (0,)))
+            m = m_new
+        ml_sc[0:1, :] = m
+        ml_sc[1:2, :] = total
+        acc_sc[...] = acc
 
     def body(j, _):
-        chunk(j, False)
+        chunks((2 * j, 2 * j + 1), False)
         return 0
 
-    lax.fori_loop(0, n_full, body, 0)
-    chunk(n_full, True)
+    lax.fori_loop(0, blk // 2, body, 0)
+
+    @pl.when(blk % 2 == 1)
+    def _():
+        chunks((blk - 1, blk), True)
+
+    @pl.when(blk % 2 == 0)
+    def _():
+        chunks((blk,), True)
+
     total = ml_sc[1:2, :]
     out_t = acc_sc[...] / total
     ot_ref[0, 0] = out_t
@@ -251,26 +278,34 @@
     row_sc[1:2, :] = jnp.sum(ot_ref[0, 0] * do_t, axis=0, keepdims=True)
     dq_sc[...] = jnp.zeros_like(dq_sc)
 
-    def chunk(j, masked):
-        rows = pl.ds(j * BK, BK)
-        s = mm(k_ref[rows, :], qt_sc[...], ((1,), (0,))) * (SCALE * LOG2E)
-        p = jnp.exp2(s - row_sc[0:1, :])
-        if masked:
-            p = jnp.where(causal(blk * BQ, j * BK, s.shape), p, 0.0)
-        dp = mm(v_ref[rows, :], dt_sc[...], ((1,), (0,)))
-        dv_sc[rows, :] += mm(p.astype(BF16), ds_sc[...], ((1,), (0,)))
-        d_s = (p * (dp - row_sc[1:2, :]) * SCALE).astype(BF16)
-        dk_sc[rows, :] += mm(d_s, qs_sc[...], ((1,), (0,)))
-        dq_sc[...] += mm(kt_sc[j], d_s, ((1,), (0,)))
-
-    n_full = (blk * BQ) // BK
+    def chunks(js, masked):
+        rows = [pl.ds(j * BK, BK) for j in js]
+        scores = [mm(k_ref[r, :], qt_sc[...], ((1,), (0,))) * (SCALE * LOG2E) for r in rows]
+        dps = [mm(v_ref[r, :], dt_sc[...], ((1,), (0,))) for r in rows]
+        dq = dq_sc[...]
+        for n, (j, r) in enumerate(zip(js, rows)):
+            p = jnp.exp2(scores[n] - row_sc[0:1, :])
+            if masked and n == len(js) - 1:
+                p = jnp.where(causal(p.shape), p, 0.0)
+            dv_sc[r, :] += mm(p.astype(BF16), ds_sc[...], ((1,), (0,)))
+            d_s = (p * (dps[n] - row_sc[1:2, :]) * SCALE).astype(BF16)
+            dk_sc[r, :] += mm(d_s, qs_sc[...], ((1,), (0,)))
+            dq = dq + mm(kt_sc[j], d_s, ((1,), (0,)))
+        dq_sc[...] = dq
 
     def body(j, _):
-        chunk(j, False)
+        chunks((2 * j, 2 * j + 1), False)
         return 0
 
-    lax.fori_loop(0, n_full, body, 0)
-    chunk(n_full, True)
+    lax.fori_loop(0, blk // 2, body, 0)
+
+    @pl.when(blk % 2 == 1)
+    def _():
+        chunks((blk - 1, blk), True)
+
+    @pl.when(blk % 2 == 0)
+    def _():
+        chunks((blk,), True)
 
     rows = pl.ds(blk * BQ, BQ)
     cos_t = cos_ref[rows, :]
@@ -367,6 +402,51 @@
     )(dh0, dh1, x, ln_w)
 
 
+def reserve(*shapes):
+    return pl.pallas_call(
+        lambda *refs: None,
+        out_shape=tuple(jax.ShapeDtypeStruct(s, BF16) for s in shapes),
+        out_specs=tuple(pl.BlockSpec(memory_space=pl.ANY) for _ in shapes),
+        cost_estimate=cost(1, 1),
+        name="reserve",
+    )()
+
+
+def place_kernel(idx, *refs):
+    pieces, outs = refs[:4], refs[-3:]
+    wide = outs[0].shape[1]
+    for n, piece in enumerate(pieces):
+        @pl.when(pl.program_id(0) == n)
+        def _():
+            outs[0][...] = piece[:, :wide]
+            outs[1][...] = piece[:, wide:wide + HEAD_DIM]
+            outs[2][...] = piece[:, wide + HEAD_DIM:]
+
+
+def place(idx, pieces, bufs):
+    dim, cols = pieces[0].shape
+    wide = cols - 2 * HEAD_DIM
+    blk = dim // 4
+
+    def piece_spec(n):
+        return pl.BlockSpec((blk, cols), lambda s, i, ix: (jnp.where(s == n, i, jnp.where(s < n, 0, 3)), 0))
+
+    there = lambda s, i, ix: (i, ix[s])
+    return pl.pallas_call(
+        place_kernel,
+        out_shape=tuple(jax.ShapeDtypeStruct(b.shape, BF16) for b in bufs),
+        grid_spec=pltpu.PrefetchScalarGridSpec(
+            num_scalar_prefetch=1, grid=(4, 4),
+            in_specs=[piece_spec(n) for n in range(4)] + [pl.BlockSpec(memory_space=pl.ANY)] * 3,
+            out_specs=(pl.BlockSpec((blk, wide), there), pl.BlockSpec((blk, HEAD_DIM), there),
+                       pl.BlockSpec((blk, HEAD_DIM), there))),
+        input_output_aliases={5: 0, 6: 1, 7: 2},
+        compiler_params=pltpu.CompilerParams(dimension_semantics=("arbitrary", "arbitrary"), vmem_limit_bytes=VMEM_BYTES),
+        cost_estimate=cost(8 * dim * cols, 16 * dim * cols),
+        name="place",
+    )(idx, *pieces, *bufs)
+
+
 def solution(mesh):
     n_dev = mesh.shape['sp']
     row_spec = P(('dp', 'sp'), None)
@@ -393,25 +473,28 @@
         hbs = [hb, hb ^ 1, hb ^ 2, hb ^ 3]
         toks = [me, me ^ 2, me ^ 1, me ^ 3]
 
-        x_par = over_chip(hidden)
+        pos_par = over_chip(positions)
+        pos_src = (positions, over_core(positions), pos_par, over_core(pos_par))
+        pos = jnp.concatenate([lax.select_n(me ^ b, *pos_src) for b in range(n_dev)])
+        ln_row = ln_weight.reshape(1, dim)
+        h_own = ln_forward(hidden, ln_row)
+        h_par = over_chip(h_own)
         g_par = over_chip(d_attn)
-        x_sib = over_core(hidden)
+        h_sib = over_core(h_own)
         g_sib = over_core(d_attn)
-        pos = lax.all_gather(positions, 'sp', tiled=True)
 
         inv_freq = ROPE_BASE ** (-jnp.arange(0, HEAD_DIM, 2, dtype=F32) / HEAD_DIM)
         angles = pos.astype(F32)[:, None] * jnp.repeat(inv_freq, 2)[None, :]
         cos_t = jnp.cos(angles)
         sin_t = jnp.sin(angles) * jnp.where(jnp.arange(HEAD_DIM) % 2 == 0, -1.0, 1.0)[None, :]
-        ln_row = ln_weight.reshape(1, dim)
-
-        x_sp = over_core(x_par)
+
+        h_sp = over_core(h_par)
         g_sp = over_core(g_par)
 
         hq = None
-        for tok, x in ((toks[0], hidden), (toks[2], x_sib), (toks[1], x_par), (toks[3], x_sp)):
+        for tok, h in ((toks[0], h_own), (toks[2], h_sib), (toks[1], h_par), (toks[3], h_sp)):
             idx = jnp.stack([hb, tok]).astype(jnp.int32)
-            hq = qkv_block(idx, x, ln_row, w_q, w_k, w_v, cos_t, sin_t, seq, n_dev, hq)
+            hq = qkv_block(idx, h, w_q, w_k, w_v, cos_t, sin_t, seq, n_dev, hq)
         h_all, qkv = hq
         o_own, o_t, lse = attn_forward(qkv, kv_local)
 
@@ -435,13 +518,10 @@
 
         dwo_own = token_dot(o_own, g_all)
         dwo_par = token_dot(o_par, g_all)
-        d_w_o = jnp.zeros(w_o.shape, BF16)
+        d_w_o, *d_w = reserve(w_o.shape, w_q.shape, w_k.shape, w_v.shape)
         for b, piece in zip(hbs, (dwo_own, dwo_par, over_core(dwo_own), over_core(dwo_par))):
             d_w_o = lax.dynamic_update_slice_in_dim(d_w_o, piece, b * cq, 0)
 
-        d_w_q = jnp.zeros(w_q.shape, BF16)
-        d_w_k = jnp.zeros(w_k.shape, BF16)
-        d_w_v = jnp.zeros(w_v.shape, BF16)
         dhs = []
         for t in range(kv_local):
             gr_own = attn_backward(qkv, d_o, o_t, lse, cos_t, sin_t, kv_local, t)
@@ -457,15 +537,13 @@
             dhs.append(mm(jnp.concatenate(gr_tok, axis=1), w_perm, ((1,), (1,))))
             dw_own = token_dot(h_all, gr_own)
             dw_par = token_dot(h_all, gr_par)
-            for b, piece in zip(hbs, (dw_own, dw_par, over_core(dw_own), over_core(dw_par))):
-                d_w_q = lax.dynamic_update_slice_in_dim(d_w_q, piece[:, :wide], b * cq + t * wide, 1)
-                d_w_k = lax.dynamic_update_slice_in_dim(d_w_k, piece[:, wide:wide + HEAD_DIM], b * ck + t * HEAD_DIM, 1)
-                d_w_v = lax.dynamic_update_slice_in_dim(d_w_v, piece[:, wide + HEAD_DIM:], b * ck + t * HEAD_DIM, 1)
+            pieces = (dw_own, dw_par, over_core(dw_own), over_core(dw_par))
+            d_w = place(jnp.stack([b * kv_local + t for b in hbs]).astype(jnp.int32), pieces, d_w)
 
         d_hid, d_lnw = ln_backward(dhs[0], dhs[1], hidden, ln_row)
         d_lnw = d_lnw + over_core(d_lnw)
         d_lnw = d_lnw + over_chip(d_lnw)
-        return (attn_out, d_hid, d_lnw.reshape(dim).astype(BF16), d_w_q, d_w_k, d_w_v, d_w_o)
+        return (attn_out, d_hid, d_lnw.reshape(dim).astype(BF16), *d_w, d_w_o)
 
     return jax.shard_map(layer, mesh=mesh,
                          in_specs=(row_spec, pos_spec, row_spec, P(None), full_spec, full_spec, full_spec, full_spec),

time: 1330 us -> 1320 us (level)
  waiting for transfers between devices: 168 us -> 483 us
  blocking collectives: 272 us -> 0 us
  local copies, waits for them, and re-layouts: 150 us -> 76.4 us
    ppermute x6 -> x7, waiting for transfers between devices: 168 us -> 482 us  [over_chip(): return lax.ppermute(val, 'sp', [(i, i ^ 2) for i in range(n_dev)])]
    all_gather x1 -> x0, blocking collectives: 272 us -> none  [layer(): pos = lax.all_gather(positions, 'sp', tiled=True)]
    dynamic_update_slice x17 -> x0, local copies, waits for them, and re-layouts: 47.8 us -> none  [the longest x8 26.4 us: layer(): lax.dynamic_update_slice_in_dim(d_w_q, piece[:, :wide], b * cq + t * wide...]
    pallas_call x0 -> x4, Pallas kernels: none -> 47.2 us  [the longest x2 37.9 us: place(): pl.pallas_call(place_kernel, out_shape=tuple((jax.ShapeDtypeStruct(b.shap...]
    another operation x4 -> x0, local copies, waits for them, and re-layouts: 20.9 us -> none
    pallas_call x1, Pallas kernels: 153 us -> 137 us  [attn_forward(): pl.pallas_call(fwd_kernel, grid=(kv_local, nq), in_specs=[pl.BlockSpec((B...]
    unnamed x47 -> x33, local copies, waits for them, and re-layouts: 33.6 us -> 32.4 us
  transfers between devices with their start and end apart: 23 -> 26, of which waited for: 2 -> 5; matrix products, arithmetic and copies ran while one was open for 29% -> 24% of each run, Pallas kernels for 21% -> 22%
where the time goes in v2:
time: 1320 us; the launch traced here: 1310 us
  Pallas kernels  493 us (37%)
  waiting for transfers between devices  483 us (37%)
  matrix products  225 us (17%)
  local copies, waits for them, and re-layouts  76.4 us (6%)
  starting transfers between devices  13.9 us (1%)
  other arithmetic  13.7 us (1%)
    ppermute x7, waiting for transfers between devices, over_chip(): return lax.ppermute(val, 'sp', [(i, i ^ 2) for i in range(n_dev)])  482 us
    dot_general x8, matrix products, mm(): lax.dot_general(lhs, rhs, (dims, ((), ())), preferred_element_type=F32)  200 us
    pallas_call x2, Pallas kernels, attn_backward(): pl.pallas_call(bwd_kernel, grid=(nq,), in_specs=[pl.BlockSpec((BQ, wide),...  190 us
    pallas_call x1, Pallas kernels, attn_forward(): pl.pallas_call(fwd_kernel, grid=(kv_local, nq), in_specs=[pl.BlockSpec((B...  137 us
    pallas_call x4, Pallas kernels, qkv_block(): pl.pallas_call(qkv_kernel, out_shape=(jax.ShapeDtypeStruct((seq, dim), BF...  61.4 us
    pallas_call x4, Pallas kernels, do_block(): pl.pallas_call(do_kernel, out_shape=(jax.ShapeDtypeStruct((seq, dim), BF1...  40.8 us
    pallas_call x2, Pallas kernels, place(): pl.pallas_call(place_kernel, out_shape=tuple((jax.ShapeDtypeStruct(b.shap...  37.9 us
    unnamed x33, local copies, waits for them, and re-layouts  32.4 us
  transfers between devices with their start and end apart: 26, of which 5 were waited for; matrix products, arithmetic and copies ran while one was open for 24% of the time, Pallas kernels for 22%

profile of v2, /device:TPU:0, one launch (start us, length us, event | category | flops | bytes accessed | tf_op | source)
XLA Modules:
  0.0 1306.9 jit_solution(7666881759993430247)
XLA Ops:
  1.9 9.3 ln_fwd.1.h_ref
  11.2 3.3 collective-permute-start
  15.1 1.7 collective-permute-start.3
  17.4 5.4 dynamic-slice_dynamic-update-slice_fusion.3
  22.9 3.5 dynamic-slice_dynamic-update-slice_fusion.15
  28.0 6.0 dynamic-slice_dynamic-update-slice_fusion.2
  34.0 1.7 dynamic-slice_dynamic-update-slice_fusion.13
  35.7 1.7 dynamic-slice_dynamic-update-slice_fusion.12
  37.5 3.2 dynamic-slice_dynamic-update-slice_fusion.1
  42.3 1.7 dynamic-slice_dynamic-update-slice_fusion.10
  44.0 3.1 dynamic-slice_dynamic-update-slice_fusion
  50.3 100.9 %collective-permute-done.h_ref = bf16[1024,3072]{1,0:T(8,128)(2,1)} collective-permute-done((bf16[1024,3072]{1,0:T(8,128)(2,1)}, bf16[1024,3072]{1,0:T(8,128)(2,1)}, u32[]{:S(2)}, u32[]{:S(2)}) %collective-permute-start) | collective-permute-done | bytes 6291488 | tf_op jit(solution)/shard_map/ppermute | solution.py:458
  152.4 10.2 d_o.4
  162.6 13.7 %constant_dynamic-slice_fusion.11 = (bf16[768,3072]{1,0:T(8,128)(2,1)}, bf16[768,3072]{1,0:T(8,128)(2,1)}, bf16[768,3072]{1,0:T(8,128)(2,1)}, bf16[768,3072]{1,0:T(8,128)(2,1)}) fusion(bf16[3072,3072]{1,0:T(8,128)(2,1)} %wo_ref.7, s32[]{:T(128)S(6)} %select_n.259, s32[]{:T(128)S(6)} %select_n.262, s32[]{:T(128)S(6)} %select_n.261, s32[]{:T(128)S(6)} %select_n.260), kind=kLoop, calls=%fused_computation.82 | loop fusion | bytes 37748752 | tf_op jit(solution)/shard_map/dynamic_slice | solution.py:513
  176.9 108.4 %collective-permute-done.3 = s32[1024]{0:T(1024)S(1)} collective-permute-done((s32[1024]{0:T(1024)S(1)}, s32[1024]{0:T(1024)S(1)}, u32[]{:S(2)}, u32[]{:S(2)}) %collective-permute-start.3) | collective-permute-done | bytes 4128 | tf_op jit(solution)/shard_map/ppermute | solution.py:458
  287.6 9.4 fusion.36
  297.0 15.5 %qkv.4 = (bf16[4096,3072]{1,0:T(8,128)(2,1)}, bf16[4096,1280]{1,0:T(8,128)(2,1)}) custom-call(s32[2]{0:T(128)} %pad_add_fusion.3.idx, bf16[1024,3072]{1,0:T(8,128)(2,1)} %ln_fwd.1.h_ref, bf16[3072,3072]{1,0:T(8,128)(2,1)} %wq_ref.7, bf16[3072,1024]{1,0:T(8,128)(2,1)} %wk_ref.7, bf16[3072,1024]{1,0:T(8,128)(2,1)} %wv_ref.7, ...), custom_call_target="tpu_custom_call" | custom-call | flops 8053063680 | bytes 23068672 | tf_op jit(solution)/shard_map/qkv/pallas_call | solution.py:99
  312.6 10.2 d_o.5
  322.8 10.2 d_o.6
  333.0 15.2 %qkv.5 = (bf16[4096,3072]{1,0:T(8,128)(2,1)}, bf16[4096,1280]{1,0:T(8,128)(2,1)}) custom-call(s32[2]{0:T(128)} %pad_add_fusion.2.idx, bf16[1024,3072]{1,0:T(8,128)(2,1)} %collective-permute-done.5.h_ref, bf16[3072,3072]{1,0:T(8,128)(2,1)} %wq_ref.7, bf16[3072,1024]{1,0:T(8,128)(2,1)} %wk_ref.7, ...), custom_call_target="tpu_custom_call", output_to_operand_aliasing={{0}: (7, {}), {1}: (8, {})} | custom-call | flops 8053063680 | bytes 23068672 | tf_op jit(solution)/shard_map/qkv/pallas_call | solution.py:99
  348.1 15.6 %qkv.6 = (bf16[4096,3072]{1,0:T(8,128)(2,1)}, bf16[4096,1280]{1,0:T(8,128)(2,1)}) custom-call(s32[2]{0:T(128)} %pad_add_fusion.1.idx, bf16[1024,3072]{1,0:T(8,128)(2,1)} %collective-permute-done.h_ref, bf16[3072,3072]{1,0:T(8,128)(2,1)} %wq_ref.7, bf16[3072,1024]{1,0:T(8,128)(2,1)} %wk_ref.7, ...), custom_call_target="tpu_custom_call", output_to_operand_aliasing={{0}: (7, {}), {1}: (8, {})} | custom-call | flops 8053063680 | bytes 23068672 | tf_op jit(solution)/shard_map/qkv/pallas_call | solution.py:99
  363.7 15.2 %qkv.7 = (bf16[4096,3072]{1,0:T(8,128)(2,1)}, bf16[4096,1280]{1,0:T(8,128)(2,1)}) custom-call(s32[2]{0:T(128)} %pad_add_fusion.idx, bf16[1024,3072]{1,0:T(8,128)(2,1)} %collective-permute-done.1.h_ref, bf16[3072,3072]{1,0:T(8,128)(2,1)} %wq_ref.7, bf16[3072,1024]{1,0:T(8,128)(2,1)} %wk_ref.7, ...), custom_call_target="tpu_custom_call", output_to_operand_aliasing={{0}: (7, {}), {1}: (8, {})} | custom-call | flops 8053063680 | bytes 23068672 | tf_op jit(solution)/shard_map/qkv/pallas_call | solution.py:99
  378.9 136.6 %attn_fwd.1 = (bf16[4096,768]{1,0:T(8,128)(2,1)}, f32[2,16,128,768]{3,2,1,0:T(8,128)}, f32[2,16,1,768]{3,2,1,0:T(1,128)}) custom-call(bf16[4096,1280]{1,0:T(8,128)(2,1)} %get-tuple-element.44.q_ref.k_ref.v_ref, bf16[4096,1280]{1,0:T(8,128)(2,1)} %get-tuple-element.44.q_ref.k_ref.v_ref, bf16[4096,1280]{1,0:T(8,128)(2,1)} %get-tuple-element.44.q_ref.k_ref.v_ref), custom_call_target="tpu_custom_call" | custom-call | flops 51539607552 | bytes 25165824 | tf_op jit(solution)/shard_map/attn_fwd/pallas_call | solution.py:223
  515.5 10.2 d_o.7
  525.7 95.0 %attn_bwd.2 = bf16[4096,640]{1,0:T(8,128)(2,1)} custom-call(bf16[4096,1280]{1,0:T(8,128)(2,1)} %get-tuple-element.44.q_ref.k_ref.v_ref, bf16[4096,1280]{1,0:T(8,128)(2,1)} %get-tuple-element.44.q_ref.k_ref.v_ref, bf16[4096,1280]{1,0:T(8,128)(2,1)} %get-tuple-element.44.q_ref.k_ref.v_ref, bf16[4096,768]{1,0:T(8,128)(2,1)} %get-tuple-element.52.do_ref, ...), custom_call_target="tpu_custom_call" | custom-call | flops 64424509440 | bytes 25165824 | tf_op jit(solution)/shard_map/attn_bwd/pallas_call | solution.py:336
  620.7 94.9 %attn_bwd.3 = bf16[4096,640]{1,0:T(8,128)(2,1)} custom-call(bf16[4096,1280]{1,0:T(8,128)(2,1)} %get-tuple-element.44.q_ref.k_ref.v_ref, bf16[4096,1280]{1,0:T(8,128)(2,1)} %get-tuple-element.44.q_ref.k_ref.v_ref, bf16[4096,1280]{1,0:T(8,128)(2,1)} %get-tuple-element.44.q_ref.k_ref.v_ref, bf16[4096,768]{1,0:T(8,128)(2,1)} %get-tuple-element.52.do_ref, ...), custom_call_target="tpu_custom_call" | custom-call | flops 64424509440 | bytes 25165824 | tf_op jit(solution)/shard_map/attn_bwd/pallas_call | solution.py:336
  715.6 1.8 collective-permute-start.6
  717.4 26.8 %constant_dynamic-update-slice_fusion.3 = (bf16[3072,3072]{1,0:T(8,128)(2,1)}, bf16[768,3072]{1,0:T(8,128)(2,1)}) fusion(bf16[3072,3072]{1,0:T(8,128)(2,1)} %get-tuple-element.67, s32[]{:T(128)S(6)} %select_n.259, bf16[4096,768]{1,0:T(8,128)(2,1)} %get-tuple-element.45, bf16[4096,3072]{1,0:T(8,128)(2,1)} %get-tuple-element.68), kind=kOutput, calls=%fused_computation.70 | convolution fusion | flops 19329712128 | bytes 40894468 | tf_op jit(solution)/shard_map/dot_general | solution.py:28
  746.3 25.3 %convolution_convert_fusion.3.refs_0_ = bf16[3072,640]{1,0:T(8,128)(2,1)} fusion(bf16[4096,3072]{1,0:T(8,128)(2,1)S(1)} %copy-done.1, bf16[4096,640]{1,0:T(8,128)(2,1)} %attn_bwd.2), kind=kOutput, calls=%fused_computation.35 | convolution fusion | flops 16108093440 | bytes 34340864 | tf_op jit(solution)/shard_map/dot_general | solution.py:28
  771.6 3.1 constant_dynamic-slice_fusion.3
  775.3 1.8 constant_dynamic-slice_fusion.7
  777.1 3.2 constant_dynamic-slice_fusion.15
  780.3 25.4 %convolution_convert_fusion.5.refs_0_ = bf16[3072,640]{1,0:T(8,128)(2,1)} fusion(bf16[4096,3072]{1,0:T(8,128)(2,1)S(1)} %copy-done.1, bf16[4096,640]{1,0:T(8,128)(2,1)} %attn_bwd.3), kind=kOutput, calls=%fused_computation.37 | convolution fusion | flops 16108093440 | bytes 34340864 | tf_op jit(solution)/shard_map/dot_general | solution.py:28
  805.7 272.9 %collective-permute-done.15 = bf16[4096,640]{1,0:T(8,128)(2,1)} collective-permute-done((bf16[4096,640]{1,0:T(8,128)(2,1)}, bf16[4096,640]{1,0:T(8,128)(2,1)}, u32[]{:S(2)}, u32[]{:S(2)}) %collective-permute-start.15) | collective-permute-done | bytes 5242912 | tf_op jit(solution)/shard_map/ppermute | solution.py:458
  1078.7 3.0 constant_dynamic-slice_fusion.2
  1081.6 25.2 %convolution_convert_fusion.4.refs_1_ = bf16[3072,640]{1,0:T(8,128)(2,1)} fusion(bf16[4096,3072]{1,0:T(8,128)(2,1)S(1)} %copy-done.1, bf16[4096,640]{1,0:T(8,128)(2,1)} %collective-permute-done.15), kind=kOutput, calls=%fused_computation.36 | convolution fusion | flops 16108093440 | bytes 34340864 | tf_op jit(solution)/shard_map/dot_general | solution.py:28
  1107.4 25.2 %convolution_convert_fusion.2.refs_1_ = bf16[3072,640]{1,0:T(8,128)(2,1)} fusion(bf16[4096,3072]{1,0:T(8,128)(2,1)S(1)} %copy-done.1, bf16[4096,640]{1,0:T(8,128)(2,1)} %collective-permute-done.12), kind=kOutput, calls=%fused_computation.34 | convolution fusion | flops 16108093440 | bytes 34340864 | tf_op jit(solution)/shard_map/dot_general | solution.py:28
  1132.6 3.1 constant_dynamic-slice_fusion.6
  1135.8 3.3 constant_dynamic-slice_fusion.14
  1140.1 22.7 %fusion.28.dh1_ref = f32[1024,3072]{1,0:T(8,128)} fusion(bf16[3072,2560]{1,0:T(8,128)(2,1)} %get-tuple-element.81, bf16[1024,640]{1,0:T(8,128)(2,1)} %collective-permute-done.17, bf16[1024,640]{1,0:T(8,128)(2,1)} %copy-done.8, bf16[1024,640]{1,0:T(8,128)(2,1)} %get-tuple-element.103, bf16[1024,640]{1,0:T(8,128)(2,1)S(1)} %copy-done.5), kind=kOutput, calls=%fused_computation.24 | convolution fusion | flops 16127098880 | bytes 33554432 | tf_op jit(solution)/shard_map/dot_general | solution.py:28
  1163.3 22.5 %fusion.20.dh0_ref = f32[1024,3072]{1,0:T(8,128)} fusion(bf16[3072,2560]{1,0:T(8,128)(2,1)} %get-tuple-element.82, bf16[1024,640]{1,0:T(8,128)(2,1)} %collective-permute-done.14, bf16[1024,640]{1,0:T(8,128)(2,1)} %collective-permute-done.13, bf16[1024,640]{1,0:T(8,128)(2,1)S(1)} %get-tuple-element.107, bf16[1024,640]{1,0:T(8,128)(2,1)S(1)} %copy-done.4), kind=kOutput, calls=%fused_computation.16 | convolution fusion | flops 16127098880 | bytes 33554432 | tf_op jit(solution)/shard_map/dot_general | solution.py:28
  1185.8 17.6 %ln_bwd.1 = (bf16[1024,3072]{1,0:T(8,128)(2,1)}, f32[1,3072]{1,0:T(1,128)}) custom-call(f32[1024,3072]{1,0:T(8,128)} %fusion.20.dh0_ref, f32[1024,3072]{1,0:T(8,128)} %fusion.28.dh1_ref, bf16[1024,3072]{1,0:T(8,128)(2,1)} %x_ref.3, bf16[1,3072]{1,0:T(2,128)(2,1)} %reshape.60.lnw_ref), custom_call_target="tpu_custom_call" | custom-call | flops 62914560 | bytes 37748736 | tf_op jit(solution)/shard_map/ln_bwd/pallas_call | solution.py:392
  1203.4 26.6 %constant_dynamic-update-slice_fusion.2 = (bf16[3072,3072]{1,0:T(8,128)(2,1)}, bf16[768,3072]{1,0:T(8,128)(2,1)}) fusion(bf16[3072,3072]{1,0:T(8,128)(2,1)} %get-tuple-element.115, s32[]{:T(128)S(6)} %select_n.260, bf16[4096,768]{1,0:T(8,128)(2,1)} %collective-permute-done.6, bf16[4096,3072]{1,0:T(8,128)(2,1)} %get-tuple-element.68), kind=kOutput, calls=%fused_computation.69 | convolution fusion | flops 19329712128 | bytes 40894468 | tf_op jit(solution)/shard_map/dot_general | solution.py:28
  1232.1 4.8 constant_dynamic-update-slice_fusion.1
  1238.1 25.5 %fusion.15 = bf16[1024,3072]{1,0:T(8,128)(2,1)} fusion(bf16[768,3072]{1,0:T(8,128)(2,1)} %get-tuple-element.78, bf16[768,3072]{1,0:T(8,128)(2,1)} %get-tuple-element.79, bf16[768,3072]{1,0:T(8,128)(2,1)} %get-tuple-element.80, bf16[768,3072]{1,0:T(8,128)(2,1)} %get-tuple-element.77, bf16[1024,768]{1,0:T(8,128)(2,1)} %collective-permute-done.8, ...), kind=kOutput, calls=%fused_computation.15 | convolution fusion | flops 19431161856 | bytes 31457280 | tf_op jit(solution)/shard_map/dot_general | solution.py:514
  1263.6 18.9 %place.2 = (bf16[3072,3072]{1,0:T(8,128)(2,1)}, bf16[3072,1024]{1,0:T(8,128)(2,1)}, bf16[3072,1024]{1,0:T(8,128)(2,1)}) custom-call(s32[4]{0:T(128)} %pad_add_fusion.5.idx, bf16[3072,640]{1,0:T(8,128)(2,1)} %convolution_convert_fusion.3.refs_0_, ...), custom_call_target="tpu_custom_call", output_to_operand_aliasing={{0}: (5, {}), {1}: (6, {}), {2}: (7, {})} | custom-call | flops 15728640 | bytes 31457280 | tf_op jit(solution)/shard_map/place/pallas_call | solution.py:435
  1282.6 18.9 %place.3 = (bf16[3072,3072]{1,0:T(8,128)(2,1)}, bf16[3072,1024]{1,0:T(8,128)(2,1)}, bf16[3072,1024]{1,0:T(8,128)(2,1)}) custom-call(s32[4]{0:T(128)} %pad_add_fusion.4.idx, bf16[3072,640]{1,0:T(8,128)(2,1)} %convolution_convert_fusion.5.refs_0_, ...), custom_call_target="tpu_custom_call", output_to_operand_aliasing={{0}: (5, {}), {1}: (6, {}), {2}: (7, {})} | custom-call | flops 15728640 | bytes 31457280 | tf_op jit(solution)/shard_map/place/pallas_call | solution.py:435
  1301.5 4.8 constant_dynamic-update-slice_fusion
  (89 shorter events, 21.3 us)
Async XLA Ops:
  1.9 13.1 %copy-start.7 = (s32[1024]{0:T(1024)S(1)}, s32[1024]{0:T(1024)}, u32[]{:S(2)}) copy-start(s32[1024]{0:T(1024)} %param.9) | copy-start | bytes 12292
  1.9 32.1 %slice-start = ((s8[6291456]{0:T(1024)(128)(4,1)}), s8[2097152]{0:T(1024)(128)(4,1)S(1)}, s32[]{:S(2)}) async-start(s8[6291456]{0:T(1024)(128)(4,1)} %bitcast.27), calls=%async_computation | async-start | bytes 4194304
  11.2 140.0 %collective-permute-start = (bf16[1024,3072]{1,0:T(8,128)(2,1)}, bf16[1024,3072]{1,0:T(8,128)(2,1)}, u32[]{:S(2)}, u32[]{:S(2)}) collective-permute-start(bf16[1024,3072]{1,0:T(8,128)(2,1)} %ln_fwd.1.h_ref), channel_id=1, source_target_pairs={{0,2},{1,3},{2,0},{3,1},{4,6},{5,7},{6,4},{7,5}} | collective-permute-start | bytes 18874376 | tf_op jit(solution)/shard_map/ppermute | solution.py:458
  14.5 298.0 %collective-permute-start.11 = (bf16[1024,3072]{1,0:T(8,128)(2,1)}, bf16[1024,3072]{1,0:T(8,128)(2,1)}, u32[]{:S(2)}, u32[]{:S(2)}) collective-permute-start(bf16[1024,3072]{1,0:T(8,128)(2,1)} %g_ref.1), channel_id=1, source_target_pairs={{0,1},{1,0},{2,3},{3,2},{4,5},{5,4},{6,7},{7,6}} | collective-permute-start | bytes 18874376 | tf_op jit(solution)/shard_map/ppermute | solution.py:461
  14.5 297.9 %collective-permute-start.9 = (bf16[1024,3072]{1,0:T(8,128)(2,1)}, bf16[1024,3072]{1,0:T(8,128)(2,1)}, u32[]{:S(2)}, u32[]{:S(2)}) collective-permute-start(bf16[1024,3072]{1,0:T(8,128)(2,1)} %g_ref.1), channel_id=1, source_target_pairs={{0,2},{1,3},{2,0},{3,1},{4,6},{5,7},{6,4},{7,5}} | collective-permute-start | bytes 18874376 | tf_op jit(solution)/shard_map/ppermute | solution.py:458
  14.6 318.4 %collective-permute-start.5 = (bf16[1024,3072]{1,0:T(8,128)(2,1)}, bf16[1024,3072]{1,0:T(8,128)(2,1)}, u32[]{:S(2)}, u32[]{:S(2)}) collective-permute-start(bf16[1024,3072]{1,0:T(8,128)(2,1)} %ln_fwd.1.h_ref), channel_id=1, source_target_pairs={{0,1},{1,0},{2,3},{3,2},{4,5},{5,4},{6,7},{7,6}} | collective-permute-start | bytes 18874376 | tf_op jit(solution)/shard_map/ppermute | solution.py:461
  15.1 270.2 %collective-permute-start.3 = (s32[1024]{0:T(1024)S(1)}, s32[1024]{0:T(1024)S(1)}, u32[]{:S(2)}, u32[]{:S(2)}) collective-permute-start(s32[1024]{0:T(1024)S(1)} %copy-done.7), channel_id=1, source_target_pairs={{0,2},{1,3},{2,0},{3,1},{4,6},{5,7},{6,4},{7,5}} | collective-permute-start | bytes 12296 | tf_op jit(solution)/shard_map/ppermute | solution.py:458
  17.4 8.9 copy-start.2
  17.4 16.6 %slice-start.1 = ((s8[6291456]{0:T(1024)(128)(4,1)}), s8[4194304]{0:T(1024)(128)(4,1)S(1)}, s32[]{:S(2)}) async-start(s8[6291456]{0:T(1024)(128)(4,1)} %bitcast.27), calls=%async_computation.1 | async-start | bytes 8388608
  26.4 11.1 copy-start
  151.2 212.5 %collective-permute-start.1 = (bf16[1024,3072]{1,0:T(8,128)(2,1)}, bf16[1024,3072]{1,0:T(8,128)(2,1)}, u32[]{:S(2)}, u32[]{:S(2)}) collective-permute-start(bf16[1024,3072]{1,0:T(8,128)(2,1)} %collective-permute-done.h_ref), channel_id=1, source_target_pairs={{0,1},{1,0},{2,3},{3,2},{4,5},{5,4},{6,7},{7,6}} | collective-permute-start | bytes 18874376 | tf_op jit(solution)/shard_map/ppermute | solution.py:461
  285.2 1.2 collective-permute-start.2
  286.4 1.2 collective-permute-start.4
  312.5 203.1 %collective-permute-start.10 = (bf16[1024,3072]{1,0:T(8,128)(2,1)}, bf16[1024,3072]{1,0:T(8,128)(2,1)}, u32[]{:S(2)}, u32[]{:S(2)}) collective-permute-start(bf16[1024,3072]{1,0:T(8,128)(2,1)} %collective-permute-done.9.g_ref), channel_id=1, source_target_pairs={{0,1},{1,0},{2,3},{3,2},{4,5},{5,4},{6,7},{7,6}} | collective-permute-start | bytes 18874376 | tf_op jit(solution)/shard_map/ppermute | solution.py:461
  715.6 420.1 %collective-permute-start.6 = (bf16[4096,768]{1,0:T(8,128)(2,1)}, bf16[4096,768]{1,0:T(8,128)(2,1)}, u32[]{:S(2)}, u32[]{:S(2)}) collective-permute-start(bf16[4096,768]{1,0:T(8,128)(2,1)} %get-tuple-element.45), channel_id=1, source_target_pairs={{0,2},{1,3},{2,0},{3,1},{4,6},{5,7},{6,4},{7,5}} | collective-permute-start | bytes 18874376 | tf_op jit(solution)/shard_map/ppermute | solution.py:458
  717.4 28.9 %copy-start.1 = (bf16[4096,3072]{1,0:T(8,128)(2,1)S(1)}, bf16[4096,3072]{1,0:T(8,128)(2,1)}, u32[]{:S(2)}) copy-start(bf16[4096,3072]{1,0:T(8,128)(2,1)} %get-tuple-element.57) | copy-start | bytes 75497472
  744.2 486.3 %collective-permute-start.24 = (bf16[768,3072]{1,0:T(8,128)(2,1)}, bf16[768,3072]{1,0:T(8,128)(2,1)}, u32[]{:S(2)}, u32[]{:S(2)}) collective-permute-start(bf16[768,3072]{1,0:T(8,128)(2,1)} %get-tuple-element.116), channel_id=1, source_target_pairs={{0,1},{1,0},{2,3},{3,2},{4,5},{5,4},{6,7},{7,6}} | collective-permute-start | bytes 14155784 | tf_op jit(solution)/shard_map/ppermute | solution.py:461
  744.2 362.6 %collective-permute-start.12 = (bf16[4096,640]{1,0:T(8,128)(2,1)}, bf16[4096,640]{1,0:T(8,128)(2,1)}, u32[]{:S(2)}, u32[]{:S(2)}) collective-permute-start(bf16[4096,640]{1,0:T(8,128)(2,1)} %attn_bwd.2), channel_id=1, source_target_pairs={{0,2},{1,3},{2,0},{3,1},{4,6},{5,7},{6,4},{7,5}} | collective-permute-start | bytes 15728648 | tf_op jit(solution)/shard_map/ppermute | solution.py:458
  744.7 333.9 %collective-permute-start.15 = (bf16[4096,640]{1,0:T(8,128)(2,1)}, bf16[4096,640]{1,0:T(8,128)(2,1)}, u32[]{:S(2)}, u32[]{:S(2)}) collective-permute-start(bf16[4096,640]{1,0:T(8,128)(2,1)} %attn_bwd.3), channel_id=1, source_target_pairs={{0,2},{1,3},{2,0},{3,1},{4,6},{5,7},{6,4},{7,5}} | collective-permute-start | bytes 15728648 | tf_op jit(solution)/shard_map/ppermute | solution.py:458
  771.6 3.7 copy-start.3
  771.6 492.0 %collective-permute-start.22 = (bf16[3072,640]{1,0:T(8,128)(2,1)}, bf16[3072,640]{1,0:T(8,128)(2,1)}, u32[]{:S(2)}, u32[]{:S(2)}) collective-permute-start(bf16[3072,640]{1,0:T(8,128)(2,1)} %convolution_convert_fusion.3.refs_0_), channel_id=1, source_target_pairs={{0,1},{1,0},{2,3},{3,2},{4,5},{5,4},{6,7},{7,6}} | collective-permute-start | bytes 11796488 | tf_op jit(solution)/shard_map/ppermute | solution.py:461
  1078.6 60.4 %collective-permute-start.16 = (bf16[1024,640]{1,0:T(8,128)(2,1)S(1)}, bf16[1024,640]{1,0:T(8,128)(2,1)S(1)}, u32[]{:S(2)}, u32[]{:S(2)}) collective-permute-start(bf16[1024,640]{1,0:T(8,128)(2,1)S(1)} %get-tuple-element.102), channel_id=1, source_target_pairs={{0,1},{1,0},{2,3},{3,2},{4,5},{5,4},{6,7},{7,6}} | collective-permute-start | bytes 3932168 | tf_op jit(solution)/shard_map/ppermute | solution.py:461
  1106.9 32.6 %collective-permute-start.17 = (bf16[1024,640]{1,0:T(8,128)(2,1)S(1)}, bf16[1024,640]{1,0:T(8,128)(2,1)}, u32[]{:S(2)}, u32[]{:S(2)}) collective-permute-start(bf16[1024,640]{1,0:T(8,128)(2,1)S(1)} %get-tuple-element.104), channel_id=1, source_target_pairs={{0,1},{1,0},{2,3},{3,2},{4,5},{5,4},{6,7},{7,6}} | collective-permute-start | bytes 3932168 | tf_op jit(solution)/shard_map/ppermute | solution.py:461
  1132.6 7.5 copy-start.5
  1135.7 27.1 %collective-permute-start.13 = (bf16[1024,640]{1,0:T(8,128)(2,1)}, bf16[1024,640]{1,0:T(8,128)(2,1)}, u32[]{:S(2)}, u32[]{:S(2)}) collective-permute-start(bf16[1024,640]{1,0:T(8,128)(2,1)} %get-tuple-element.106), channel_id=1, source_target_pairs={{0,1},{1,0},{2,3},{3,2},{4,5},{5,4},{6,7},{7,6}} | collective-permute-start | bytes 3932168 | tf_op jit(solution)/shard_map/ppermute | solution.py:461
  1139.0 1.1 copy-start.8
  1139.0 98.6 %collective-permute-start.7 = (bf16[1024,768]{1,0:T(8,128)(2,1)}, bf16[1024,768]{1,0:T(8,128)(2,1)}, u32[]{:S(2)}, u32[]{:S(2)}) collective-permute-start(bf16[1024,768]{1,0:T(8,128)(2,1)} %get-tuple-element.98), channel_id=1, source_target_pairs={{0,1},{1,0},{2,3},{3,2},{4,5},{5,4},{6,7},{7,6}} | collective-permute-start | bytes 4718600 | tf_op jit(solution)/shard_map/ppermute | solution.py:461
  1139.5 23.8 %collective-permute-start.14 = (bf16[1024,640]{1,0:T(8,128)(2,1)}, bf16[1024,640]{1,0:T(8,128)(2,1)}, u32[]{:S(2)}, u32[]{:S(2)}) collective-permute-start(bf16[1024,640]{1,0:T(8,128)(2,1)} %get-tuple-element.108), channel_id=1, source_target_pairs={{0,1},{1,0},{2,3},{3,2},{4,5},{5,4},{6,7},{7,6}} | collective-permute-start | bytes 3932168 | tf_op jit(solution)/shard_map/ppermute | solution.py:461
  1140.1 23.2 %copy-start.4 = (bf16[1024,640]{1,0:T(8,128)(2,1)S(1)}, bf16[1024,640]{1,0:T(8,128)(2,1)}, u32[]{:S(2)}) copy-start(bf16[1024,640]{1,0:T(8,128)(2,1)} %get-tuple-element.105) | copy-start | bytes 3932164
  1162.8 75.3 %collective-permute-start.8 = (bf16[1024,768]{1,0:T(8,128)(2,1)S(1)}, bf16[1024,768]{1,0:T(8,128)(2,1)}, u32[]{:S(2)}, u32[]{:S(2)}) collective-permute-start(bf16[1024,768]{1,0:T(8,128)(2,1)S(1)} %get-tuple-element.100), channel_id=1, source_target_pairs={{0,1},{1,0},{2,3},{3,2},{4,5},{5,4},{6,7},{7,6}} | collective-permute-start | bytes 4718600 | tf_op jit(solution)/shard_map/ppermute | solution.py:461
  1203.4 26.6 %collective-permute-start.18 = (f32[1,3072]{1,0:T(1,128)}, f32[1,3072]{1,0:T(1,128)S(1)}, u32[]{:S(2)}, u32[]{:S(2)}) collective-permute-start(f32[1,3072]{1,0:T(1,128)} %get-tuple-element.56), channel_id=1, source_target_pairs={{0,1},{1,0},{2,3},{3,2},{4,5},{5,4},{6,7},{7,6}} | collective-permute-start | bytes 36872 | tf_op jit(solution)/shard_map/ppermute | solution.py:461
  1203.4 27.1 %copy-start.6 = (f32[1,3072]{1,0:T(1,128)S(1)}, f32[1,3072]{1,0:T(1,128)}, u32[]{:S(2)}) copy-start(f32[1,3072]{1,0:T(1,128)} %get-tuple-element.56) | copy-start | bytes 36868
  1230.0 71.5 %collective-permute-start.25 = (bf16[768,3072]{1,0:T(8,128)(2,1)}, bf16[768,3072]{1,0:T(8,128)(2,1)}, u32[]{:S(2)}, u32[]{:S(2)}) collective-permute-start(bf16[768,3072]{1,0:T(8,128)(2,1)} %get-tuple-element.118), channel_id=1, source_target_pairs={{0,1},{1,0},{2,3},{3,2},{4,5},{5,4},{6,7},{7,6}} | collective-permute-start | bytes 14155784 | tf_op jit(solution)/shard_map/ppermute | solution.py:461
  1230.6 6.4 collective-permute-start.19
  1236.9 45.6 %collective-permute-start.20 = (bf16[3072,640]{1,0:T(8,128)(2,1)}, bf16[3072,640]{1,0:T(8,128)(2,1)}, u32[]{:S(2)}, u32[]{:S(2)}) collective-permute-start(bf16[3072,640]{1,0:T(8,128)(2,1)} %convolution_convert_fusion.5.refs_0_), channel_id=1, source_target_pairs={{0,1},{1,0},{2,3},{3,2},{4,5},{5,4},{6,7},{7,6}} | collective-permute-start | bytes 11796488 | tf_op jit(solution)/shard_map/ppermute | solution.py:461
  1237.6 26.0 %collective-permute-start.23 = (bf16[3072,640]{1,0:T(8,128)(2,1)}, bf16[3072,640]{1,0:T(8,128)(2,1)}, u32[]{:S(2)}, u32[]{:S(2)}) collective-permute-start(bf16[3072,640]{1,0:T(8,128)(2,1)} %convolution_convert_fusion.2.refs_1_), channel_id=1, source_target_pairs={{0,1},{1,0},{2,3},{3,2},{4,5},{5,4},{6,7},{7,6}} | collective-permute-start | bytes 11796488 | tf_op jit(solution)/shard_map/ppermute | solution.py:461
  1238.1 44.5 %collective-permute-start.21 = (bf16[3072,640]{1,0:T(8,128)(2,1)}, bf16[3072,640]{1,0:T(8,128)(2,1)}, u32[]{:S(2)}, u32[]{:S(2)}) collective-permute-start(bf16[3072,640]{1,0:T(8,128)(2,1)} %convolution_convert_fusion.4.refs_1_), channel_id=1, source_target_pairs={{0,1},{1,0},{2,3},{3,2},{4,5},{5,4},{6,7},{7,6}} | collective-permute-start | bytes 11796488 | tf_op jit(solution)/shard_map/ppermute | solution.py:461

commit v3 on v2

--- a/solution.py
+++ b/solution.py
@@ -1,3 +1,4 @@
+import functools
 import math
 import jax
 import jax.numpy as jnp
@@ -109,23 +110,43 @@
     )(*args)
 
 
+def wo_t_kernel(idx, wo_ref, out_ref):
+    out_ref[...] = wo_ref[...].astype(F32).T.astype(BF16)
+
+
+def transpose_rows(idx, w_o, n_dev):
+    ce, dim = w_o.shape[0] // n_dev, w_o.shape[1]
+    blk = 512
+    return pl.pallas_call(
+        wo_t_kernel,
+        out_shape=jax.ShapeDtypeStruct((dim, ce), BF16),
+        grid_spec=pltpu.PrefetchScalarGridSpec(
+            num_scalar_prefetch=1, grid=(dim // blk,),
+            in_specs=[pl.BlockSpec((ce, blk), lambda i, ix: (ix[0], i))],
+            out_specs=pl.BlockSpec((blk, ce), lambda i, ix: (i, 0))),
+        compiler_params=pltpu.CompilerParams(dimension_semantics=("arbitrary",)),
+        cost_estimate=cost(4 * ce * dim, 4 * ce * dim),
+        name="wo_t",
+    )(idx, w_o)
+
+
 def do_kernel(idx, g_ref, wo_ref, *rest):
     gall_ref, do_ref = rest[-2:]
     g = g_ref[...]
     gall_ref[...] = g
-    do_ref[...] = mm(g, wo_ref[...], ((1,), (1,))).astype(BF16)
-
-
-def do_block(idx, g, w_o, seq, n_dev, prev):
+    do_ref[...] = mm(g, wo_ref[...], ((1,), (0,))).astype(BF16)
+
+
+def do_block(idx, g, wo_t, seq, prev):
     rows, dim = g.shape
-    ce = w_o.shape[0] // n_dev
+    ce = wo_t.shape[1]
     per = rows // ROWS
     here = lambda i, ix: (ix[1] * per + i, 0)
     in_specs = [
         pl.BlockSpec((ROWS, dim), lambda i, ix: (i, 0)),
-        pl.BlockSpec((ce, dim), lambda i, ix: (ix[0], 0)),
+        pl.BlockSpec((dim, ce), lambda i, ix: (0, 0)),
     ]
-    args = [idx, g, w_o]
+    args = [idx, g, wo_t]
     aliases = {}
     if prev is not None:
         in_specs += [pl.BlockSpec(memory_space=pl.ANY)] * 2
@@ -156,10 +177,10 @@
     return lax.broadcasted_iota(jnp.int32, shape, 0) <= lax.broadcasted_iota(jnp.int32, shape, 1) % BQ
 
 
-def fwd_kernel(q_ref, k_ref, v_ref, o_ref, ot_ref, lse_ref, qt_sc, vt_sc, acc_sc, ml_sc):
+def fwd_kernel(q_ref, k_ref, v_ref, o_ref, ot_ref, lse_ref, qt_sc, vt_sc, acc_sc, ml_sc, s_sc):
     blk = pl.program_id(1)
-    width = REP * BQ
     n_chunks = k_ref.shape[0] // BK
+    pairs = blk // 2
 
     @pl.when(blk == 0)
     def _():
@@ -170,41 +191,61 @@
         lax.fori_loop(0, n_chunks, one, 0)
 
     qt_sc[...] = flip(stack_heads(q_ref[...]))
-    acc_sc[...] = jnp.zeros_like(acc_sc)
-    ml_sc[0:1, :] = jnp.full((1, width), -jnp.inf, F32)
-    ml_sc[1:2, :] = jnp.zeros((1, width), F32)
-
-    def chunks(js, masked):
-        scores = [mm(k_ref[pl.ds(j * BK, BK), :], qt_sc[...], ((1,), (0,))) * (SCALE * LOG2E) for j in js]
-        if masked:
-            scores[-1] = jnp.where(causal(scores[-1].shape), scores[-1], -jnp.inf)
-        m = ml_sc[0:1, :]
-        total = ml_sc[1:2, :]
-        acc = acc_sc[...]
+
+    def score(j):
+        return mm(k_ref[pl.ds(j * BK, BK), :], qt_sc[...], ((1,), (0,))) * (SCALE * LOG2E)
+
+    def ahead(pair):
+        for n in range(2):
+            nxt = score(2 * pair + n)
+            s_sc[n] = nxt
+            ml_sc[2 + n:3 + n, :] = jnp.max(nxt, axis=0, keepdims=True)
+
+    def update(m_new, js, scores, first):
+        if first:
+            total, acc = 0.0, 0.0
+        else:
+            alpha = jnp.exp2(ml_sc[0:1, :] - m_new)
+            total, acc = ml_sc[1:2, :] * alpha, acc_sc[...] * alpha
         for j, s in zip(js, scores):
-            m_new = jnp.maximum(m, jnp.max(s, axis=0, keepdims=True))
-            alpha = jnp.exp2(m - m_new)
             p = jnp.exp2(s - m_new)
-            total = total * alpha + jnp.sum(p, axis=0, keepdims=True)
-            acc = acc * alpha + mm(vt_sc[j], p.astype(BF16), ((1,), (0,)))
-            m = m_new
-        ml_sc[0:1, :] = m
+            total = total + jnp.sum(p, axis=0, keepdims=True)
+            acc = acc + mm(vt_sc[j], p.astype(BF16), ((1,), (0,)))
+        ml_sc[0:1, :] = m_new
         ml_sc[1:2, :] = total
         acc_sc[...] = acc
 
-    def body(j, _):
-        chunks((2 * j, 2 * j + 1), False)
+    def last_chunks(js):
+        scores = [score(j) for j in js]
+        scores[-1] = jnp.where(causal(scores[-1].shape), scores[-1], -jnp.inf)
+        m_new = functools.reduce(jnp.maximum, [jnp.max(s, axis=0, keepdims=True) for s in scores])
+        ahead(0)
+        update(m_new, js, scores, True)
+
+    def held(pair, more):
+        m_new = jnp.maximum(ml_sc[0:1, :], jnp.maximum(ml_sc[2:3, :], ml_sc[3:4, :]))
+        scores = [s_sc[n] for n in range(2)]
+        if more:
+            ahead(pair + 1)
+        update(m_new, (2 * pair, 2 * pair + 1), scores, False)
+
+    @pl.when(blk % 2 == 1)
+    def _():
+        last_chunks((blk - 1, blk))
+
+    @pl.when(blk % 2 == 0)
+    def _():
+        last_chunks((blk,))
+
+    def body(pair, _):
+        held(pair, True)
         return 0
 
-    lax.fori_loop(0, blk // 2, body, 0)
-
-    @pl.when(blk % 2 == 1)
-    def _():
-        chunks((blk - 1, blk), True)
-
-    @pl.when(blk % 2 == 0)
-    def _():
-        chunks((blk,), True)
+    lax.fori_loop(0, pairs - 1, body, 0)
+
+    @pl.when(pairs > 0)
+    def _():
+        held(pairs - 1, False)
 
     total = ml_sc[1:2, :]
     out_t = acc_sc[...] / total
@@ -243,6 +284,7 @@
             pltpu.VMEM((seq // BK, HEAD_DIM, BK), BF16),
             pltpu.VMEM((HEAD_DIM, REP * BQ), F32),
             pltpu.VMEM((8, REP * BQ), F32),
+            pltpu.VMEM((2, BK, REP * BQ), F32),
         ],
         compiler_params=pltpu.CompilerParams(dimension_semantics=("arbitrary", "arbitrary"), vmem_limit_bytes=VMEM_BYTES),
         cost_estimate=cost(flops, 4 * seq * wide * kv_local * 2),
@@ -412,39 +454,80 @@
     )()
 
 
-def place_kernel(idx, *refs):
-    pieces, outs = refs[:4], refs[-3:]
-    wide = outs[0].shape[1]
-    for n, piece in enumerate(pieces):
-        @pl.when(pl.program_id(0) == n)
-        def _():
-            outs[0][...] = piece[:, :wide]
-            outs[1][...] = piece[:, wide:wide + HEAD_DIM]
-            outs[2][...] = piece[:, wide + HEAD_DIM:]
-
-
-def place(idx, pieces, bufs):
-    dim, cols = pieces[0].shape
-    wide = cols - 2 * HEAD_DIM
-    blk = dim // 4
-
-    def piece_spec(n):
-        return pl.BlockSpec((blk, cols), lambda s, i, ix: (jnp.where(s == n, i, jnp.where(s < n, 0, 3)), 0))
-
-    there = lambda s, i, ix: (i, ix[s])
+def dw_kernel(idx, h_ref, *refs):
+    n = len(refs) - 8
+    grs, (q_ref, k_ref, v_ref, piece_ref, gr_sc) = refs[:n], refs[-5:]
+    wide = q_ref.shape[1] // n
+    cols = piece_ref.shape[1]
+
+    @pl.when(pl.program_id(0) == 0)
+    def _():
+        for t, gr in enumerate(grs):
+            gr_sc[:, t * wide:(t + 1) * wide] = gr[:, :wide]
+            for part in range(2):
+                start = n * wide + part * n * HEAD_DIM + t * HEAD_DIM
+                gr_sc[:, start:start + HEAD_DIM] = gr[:, wide + part * HEAD_DIM:wide + (part + 1) * HEAD_DIM]
+
+    for start in range(0, cols, 256):
+        stop = min(start + 256, cols)
+        piece_ref[:, start:stop] = mm(h_ref[...], gr_sc[:, start:stop], ((0,), (0,))).astype(BF16)
+    q_ref[...] = piece_ref[:, :n * wide]
+    k_ref[...] = piece_ref[:, n * wide:n * (wide + HEAD_DIM)]
+    v_ref[...] = piece_ref[:, n * (wide + HEAD_DIM):]
+
+
+def weight_grad(idx, h_all, grs, bufs):
+    seq, dim = h_all.shape
+    n = len(grs)
+    cols = n * grs[0].shape[1]
+    wide = REP * HEAD_DIM * n
+    blk = 512
+    there = lambda i, ix: (i, ix[0])
+    flops = 2 * seq * dim * cols
+    return pl.pallas_call(
+        dw_kernel,
+        out_shape=tuple(jax.ShapeDtypeStruct(b.shape, BF16) for b in bufs) + (jax.ShapeDtypeStruct((dim, cols), BF16),),
+        grid_spec=pltpu.PrefetchScalarGridSpec(
+            num_scalar_prefetch=1, grid=(dim // blk,),
+            in_specs=[pl.BlockSpec((seq, blk), lambda i, ix: (0, i))]
+            + [pl.BlockSpec((seq, cols // n), lambda i, ix: (0, 0), pipeline_mode=pl.Buffered(1)) for _ in grs]
+            + [pl.BlockSpec(memory_space=pl.ANY)] * 3,
+            out_specs=(pl.BlockSpec((blk, wide), there), pl.BlockSpec((blk, n * HEAD_DIM), there),
+                       pl.BlockSpec((blk, n * HEAD_DIM), there), pl.BlockSpec((blk, cols), lambda i, ix: (i, 0))),
+            scratch_shapes=[pltpu.VMEM((seq, cols), BF16)]),
+        input_output_aliases={2 + n: 0, 3 + n: 1, 4 + n: 2},
+        compiler_params=pltpu.CompilerParams(dimension_semantics=("arbitrary",), vmem_limit_bytes=VMEM_BYTES),
+        cost_estimate=cost(flops, 2 * (seq * dim + seq * cols + 2 * dim * cols)),
+        name="weight_grad",
+    )(idx, h_all, *grs, *bufs)
+
+
+def place_kernel(idx, piece_ref, *refs):
+    q_ref, k_ref, v_ref = refs[-3:]
+    wide, one = q_ref.shape[1], k_ref.shape[1]
+    q_ref[...] = piece_ref[:, :wide]
+    k_ref[...] = piece_ref[:, wide:wide + one]
+    v_ref[...] = piece_ref[:, wide + one:]
+
+
+def place(idx, piece, bufs):
+    dim, cols = piece.shape
+    one = cols // (REP + 2)
+    blk = 512
+    there = lambda i, ix: (i, ix[0])
     return pl.pallas_call(
         place_kernel,
         out_shape=tuple(jax.ShapeDtypeStruct(b.shape, BF16) for b in bufs),
         grid_spec=pltpu.PrefetchScalarGridSpec(
-            num_scalar_prefetch=1, grid=(4, 4),
-            in_specs=[piece_spec(n) for n in range(4)] + [pl.BlockSpec(memory_space=pl.ANY)] * 3,
-            out_specs=(pl.BlockSpec((blk, wide), there), pl.BlockSpec((blk, HEAD_DIM), there),
-                       pl.BlockSpec((blk, HEAD_DIM), there))),
-        input_output_aliases={5: 0, 6: 1, 7: 2},
-        compiler_params=pltpu.CompilerParams(dimension_semantics=("arbitrary", "arbitrary"), vmem_limit_bytes=VMEM_BYTES),
-        cost_estimate=cost(8 * dim * cols, 16 * dim * cols),
+            num_scalar_prefetch=1, grid=(dim // blk,),
+            in_specs=[pl.BlockSpec((blk, cols), lambda i, ix: (i, 0))] + [pl.BlockSpec(memory_space=pl.ANY)] * 3,
+            out_specs=(pl.BlockSpec((blk, REP * one), there), pl.BlockSpec((blk, one), there),
+                       pl.BlockSpec((blk, one), there))),
+        input_output_aliases={2: 0, 3: 1, 4: 2},
+        compiler_params=pltpu.CompilerParams(dimension_semantics=("arbitrary",)),
+        cost_estimate=cost(4 * dim * cols, 4 * dim * cols),
         name="place",
-    )(idx, *pieces, *bufs)
+    )(idx, piece, *bufs)
 
 
 def solution(mesh):
@@ -477,10 +560,11 @@
         pos_src = (positions, over_core(positions), pos_par, over_core(pos_par))
         pos = jnp.concatenate([lax.select_n(me ^ b, *pos_src) for b in range(n_dev)])
         ln_row = ln_weight.reshape(1, dim)
-        h_own = ln_forward(hidden, ln_row)
-        h_par = over_chip(h_own)
+        half = rows // 2
+        h_own = [ln_forward(hidden[n * half:(n + 1) * half], ln_row) for n in range(2)]
+        h_par = [over_chip(h) for h in h_own]
         g_par = over_chip(d_attn)
-        h_sib = over_core(h_own)
+        h_sib = [over_core(h) for h in h_own]
         g_sib = over_core(d_attn)
 
         inv_freq = ROPE_BASE ** (-jnp.arange(0, HEAD_DIM, 2, dtype=F32) / HEAD_DIM)
@@ -488,20 +572,24 @@
         cos_t = jnp.cos(angles)
         sin_t = jnp.sin(angles) * jnp.where(jnp.arange(HEAD_DIM) % 2 == 0, -1.0, 1.0)[None, :]
 
-        h_sp = over_core(h_par)
+        h_sp = [over_core(h) for h in h_par]
         g_sp = over_core(g_par)
 
         hq = None
-        for tok, h in ((toks[0], h_own), (toks[2], h_sib), (toks[1], h_par), (toks[3], h_sp)):
-            idx = jnp.stack([hb, tok]).astype(jnp.int32)
-            hq = qkv_block(idx, h, w_q, w_k, w_v, cos_t, sin_t, seq, n_dev, hq)
+        for tok, h in ((toks[0], h_own), (toks[2], h_sib)):
+            for n in range(2):
+                hq = qkv_block(jnp.stack([hb, 2 * tok + n]).astype(jnp.int32), h[n], w_q, w_k, w_v, cos_t, sin_t, seq, n_dev, hq)
+        for n in range(2):
+            for tok, h in ((toks[1], h_par), (toks[3], h_sp)):
+                hq = qkv_block(jnp.stack([hb, 2 * tok + n]).astype(jnp.int32), h[n], w_q, w_k, w_v, cos_t, sin_t, seq, n_dev, hq)
         h_all, qkv = hq
         o_own, o_t, lse = attn_forward(qkv, kv_local)
 
+        wo_t = transpose_rows(hb.reshape(1).astype(jnp.int32), w_o, n_dev)
         gd = None
         for tok, g in ((toks[0], d_attn), (toks[2], g_sib), (toks[1], g_par), (toks[3], g_sp)):
             idx = jnp.stack([hb, tok]).astype(jnp.int32)
-            gd = do_block(idx, g, w_o, seq, n_dev, gd)
+            gd = do_block(idx, g, wo_t, seq, gd)
         g_all, d_o = gd
 
         def own_rows(val, dev):
@@ -523,11 +611,20 @@
             d_w_o = lax.dynamic_update_slice_in_dim(d_w_o, piece, b * cq, 0)
 
         dhs = []
+        gr = []
         for t in range(kv_local):
-            gr_own = attn_backward(qkv, d_o, o_t, lse, cos_t, sin_t, kv_local, t)
-            gr_par = over_chip(gr_own)
-            gr_tok = [own_rows(gr_own, me), own_rows(gr_par, me),
-                      over_core(own_rows(gr_own, me ^ 1)), over_core(own_rows(gr_par, me ^ 1))]
+            gr.append(attn_backward(qkv, d_o, o_t, lse, cos_t, sin_t, kv_local, t))
+        gr_par = [over_chip(val) for val in gr]
+
+        def col(val):
+            return val.reshape(1).astype(jnp.int32)
+
+        *d_w, piece = weight_grad(col(hbs[0]), h_all, gr, d_w)
+        piece = over_core(piece)
+        d_w = place(col(hbs[2]), piece, d_w)
+        for t in range(kv_local):
+            gr_tok = [own_rows(gr[t], me), own_rows(gr_par[t], me),
+                      over_core(own_rows(gr[t], me ^ 1)), over_core(own_rows(gr_par[t], me ^ 1))]
             parts = []
             for b in hbs:
                 parts.append(lax.dynamic_slice_in_dim(w_q, b * cq + t * wide, wide, 1))
@@ -535,10 +632,9 @@
                 parts.append(lax.dynamic_slice_in_dim(w_v, b * ck + t * HEAD_DIM, HEAD_DIM, 1))
             w_perm = jnp.concatenate(parts, axis=1)
             dhs.append(mm(jnp.concatenate(gr_tok, axis=1), w_perm, ((1,), (1,))))
-            dw_own = token_dot(h_all, gr_own)
-            dw_par = token_dot(h_all, gr_par)
-            pieces = (dw_own, dw_par, over_core(dw_own), over_core(dw_par))
-            d_w = place(jnp.stack([b * kv_local + t for b in hbs]).astype(jnp.int32), pieces, d_w)
+            *d_w, piece = weight_grad(col(hbs[1] * kv_local + t), h_all, (gr_par[t],), d_w)
+            piece = over_core(piece)
+            d_w = place(col(hbs[3] * kv_local + t), piece, d_w)
 
         d_hid, d_lnw = ln_backward(dhs[0], dhs[1], hidden, ln_row)
         d_lnw = d_lnw + over_core(d_lnw)

time: 1320 us -> 1200 us (0.909)
  matrix products: 225 us -> 118 us
  waiting for transfers between devices: 483 us -> 377 us
  Pallas kernels: 493 us -> 568 us
  local copies, waits for them, and re-layouts: 76.4 us -> 93 us
    dot_general x8 -> x4, matrix products: 200 us -> 92.9 us  [mm(): lax.dot_general(lhs, rhs, (dims, ((), ())), preferred_element_type=F32)]
    ppermute x7 -> x8, waiting for transfers between devices: 482 us -> 377 us  [over_chip(): return lax.ppermute(val, 'sp', [(i, i ^ 2) for i in range(n_dev)])]
    pallas_call x0 -> x4, Pallas kernels: none -> 103 us  [the longest x3 96 us: weight_grad(): pl.pallas_call(dw_kernel, out_shape=tuple((jax.ShapeDtypeStruct(b.shape,...]
    pallas_call x1, Pallas kernels: 137 us -> 103 us  [attn_forward(): pl.pallas_call(fwd_kernel, grid=(kv_local, nq), in_specs=[pl.BlockSpec((B...]
    pallas_call x4 -> x8, Pallas kernels: 61.4 us -> 84.9 us  [qkv_block(): pl.pallas_call(qkv_kernel, out_shape=(jax.ShapeDtypeStruct((seq, dim), BF...]
    pallas_call x2 -> x3, Pallas kernels: 37.9 us -> 19.2 us  [place(): pl.pallas_call(place_kernel, out_shape=tuple((jax.ShapeDtypeStruct(b.shap...]
    unnamed x33 -> x37, local copies, waits for them, and re-layouts: 32.4 us -> 40.2 us
  transfers between devices with their start and end apart: 26 -> 28, of which waited for: 5 -> 5; matrix products, arithmetic and copies ran while one was open for 24% -> 19% of each run, Pallas kernels for 22% -> 47%
where the time goes in v3:
time: 1200 us; the launch traced here: 1190 us
  Pallas kernels  568 us (47%)
  waiting for transfers between devices  377 us (31%)
  matrix products  118 us (10%)
  local copies, waits for them, and re-layouts  93 us (8%)
  other arithmetic  17 us (1%)
  starting transfers between devices  13.8 us (1%)
    ppermute x8, waiting for transfers between devices, over_chip(): return lax.ppermute(val, 'sp', [(i, i ^ 2) for i in range(n_dev)])  377 us
    pallas_call x2, Pallas kernels, attn_backward(): pl.pallas_call(bwd_kernel, grid=(nq,), in_specs=[pl.BlockSpec((BQ, wide),...  190 us
    pallas_call x1, Pallas kernels, attn_forward(): pl.pallas_call(fwd_kernel, grid=(kv_local, nq), in_specs=[pl.BlockSpec((B...  103 us
    pallas_call x3, Pallas kernels, weight_grad(): pl.pallas_call(dw_kernel, out_shape=tuple((jax.ShapeDtypeStruct(b.shape,...  96 us
    dot_general x4, matrix products, mm(): lax.dot_general(lhs, rhs, (dims, ((), ())), preferred_element_type=F32)  92.9 us
    pallas_call x8, Pallas kernels, qkv_block(): pl.pallas_call(qkv_kernel, out_shape=(jax.ShapeDtypeStruct((seq, dim), BF...  84.9 us
    pallas_call x4, Pallas kernels, do_block(): pl.pallas_call(do_kernel, out_shape=(jax.ShapeDtypeStruct((seq, dim), BF1...  40.7 us
    unnamed x37, local copies, waits for them, and re-layouts  40.2 us
  transfers between devices with their start and end apart: 28, of which 5 were waited for; matrix products, arithmetic and copies ran while one was open for 19% of the time, Pallas kernels for 47%

profile of v3, /device:TPU:0, one launch (start us, length us, event | category | flops | bytes accessed | tf_op | source)
XLA Modules:
  0.0 1187.9 jit_solution(5228688678199285519)
XLA Ops:
  1.9 6.0 fusion.40
  7.9 5.2 ln_fwd.3.h_ref
  18.4 5.1 ln_fwd.2.h_ref
  24.2 5.1 dynamic-slice_dynamic-update-slice_fusion.3
  37.2 6.7 wo_t.1.wo_ref
  43.9 5.3 dynamic-slice_dynamic-update-slice_fusion.2
  51.9 2.8 dynamic-slice_dynamic-update-slice_fusion.12
  54.8 10.4 d_o.4
  66.3 154.2 %collective-permute-done.3 = s32[1024]{0:T(1024)S(1)} collective-permute-done((s32[1024]{0:T(1024)S(1)}, s32[1024]{0:T(1024)S(1)}, u32[]{:S(2)}, u32[]{:S(2)}) %collective-permute-start.3) | collective-permute-done | bytes 4128 | tf_op jit(solution)/shard_map/ppermute | solution.py:541
  224.4 5.2 dynamic-slice_dynamic-update-slice_fusion.1
  229.8 58.0 %collective-permute-done.h_ref = bf16[512,3072]{1,0:T(8,128)(2,1)} collective-permute-done((bf16[512,3072]{1,0:T(8,128)(2,1)}, bf16[512,3072]{1,0:T(8,128)(2,1)}, u32[]{:S(2)}, u32[]{:S(2)}) %collective-permute-start) | collective-permute-done | bytes 3145760 | tf_op jit(solution)/shard_map/ppermute | solution.py:541
  287.8 9.6 fusion.36
  297.4 10.6 qkv.8
  308.0 10.5 qkv.9
  319.1 10.5 qkv.10
  329.7 11.0 qkv.11
  340.6 10.5 qkv.12
  351.2 10.5 qkv.13
  361.6 10.6 qkv.14
  372.2 10.7 qkv.15
  382.9 102.7 %attn_fwd.1 = (bf16[4096,768]{1,0:T(8,128)(2,1)}, f32[2,16,128,768]{3,2,1,0:T(8,128)}, f32[2,16,1,768]{3,2,1,0:T(1,128)}) custom-call(bf16[4096,1280]{1,0:T(8,128)(2,1)} %get-tuple-element.75.q_ref.k_ref.v_ref, bf16[4096,1280]{1,0:T(8,128)(2,1)} %get-tuple-element.75.q_ref.k_ref.v_ref, bf16[4096,1280]{1,0:T(8,128)(2,1)} %get-tuple-element.75.q_ref.k_ref.v_ref), custom_call_target="tpu_custom_call" | custom-call | flops 51539607552 | bytes 25165824 | tf_op jit(solution)/shard_map/attn_fwd/pallas_call | solution.py:264
  486.9 10.1 d_o.5
  497.0 10.1 d_o.6
  507.1 10.1 d_o.7
  517.2 95.1 %attn_bwd.3.refs_1_ = bf16[4096,640]{1,0:T(8,128)(2,1)} custom-call(bf16[4096,1280]{1,0:T(8,128)(2,1)} %get-tuple-element.75.q_ref.k_ref.v_ref, bf16[4096,1280]{1,0:T(8,128)(2,1)} %get-tuple-element.75.q_ref.k_ref.v_ref, bf16[4096,1280]{1,0:T(8,128)(2,1)} %get-tuple-element.75.q_ref.k_ref.v_ref, bf16[4096,768]{1,0:T(8,128)(2,1)} %get-tuple-element.83.do_ref, ...), custom_call_target="tpu_custom_call" | custom-call | flops 64424509440 | bytes 25165824 | tf_op jit(solution)/shard_map/attn_bwd/pallas_call | solution.py:378
  612.3 94.8 %attn_bwd.2.refs_0_ = bf16[4096,640]{1,0:T(8,128)(2,1)} custom-call(bf16[4096,1280]{1,0:T(8,128)(2,1)} %get-tuple-element.75.q_ref.k_ref.v_ref, bf16[4096,1280]{1,0:T(8,128)(2,1)} %get-tuple-element.75.q_ref.k_ref.v_ref, bf16[4096,1280]{1,0:T(8,128)(2,1)} %get-tuple-element.75.q_ref.k_ref.v_ref, bf16[4096,768]{1,0:T(8,128)(2,1)} %get-tuple-element.83.do_ref, ...), custom_call_target="tpu_custom_call" | custom-call | flops 64424509440 | bytes 25165824 | tf_op jit(solution)/shard_map/attn_bwd/pallas_call | solution.py:378
  707.1 42.2 %weight_grad.3 = (bf16[3072,3072]{1,0:T(8,128)(2,1)}, bf16[3072,1024]{1,0:T(8,128)(2,1)}, bf16[3072,1024]{1,0:T(8,128)(2,1)}, bf16[3072,1280]{1,0:T(8,128)(2,1)}) custom-call(s32[1]{0:T(128)} %bitcast.idx, bf16[4096,3072]{1,0:T(8,128)(2,1)} %get-tuple-element.88.h_ref, ...), custom_call_target="tpu_custom_call", output_to_operand_aliasing={{0}: (4, {}), {1}: (5, {}), {2}: (6, {})} | custom-call | flops 32212254720 | bytes 51380224 | tf_op jit(solution)/shard_map/weight_grad/pallas_call | solution.py:487
  755.2 5.1 dynamic-slice_dynamic-update-slice_fusion
  760.3 2.9 dynamic-slice_dynamic-update-slice_fusion.9
  766.0 14.6 %constant_dynamic-slice_fusion.11 = (bf16[768,3072]{1,0:T(8,128)(2,1)}, bf16[768,3072]{1,0:T(8,128)(2,1)}, bf16[768,3072]{1,0:T(8,128)(2,1)}, bf16[768,3072]{1,0:T(8,128)(2,1)}) fusion(bf16[3072,3072]{1,0:T(8,128)(2,1)} %wo_ref.1, s32[]{:T(128)S(6)} %select_n.259, s32[]{:T(128)S(6)} %select_n.261, s32[]{:T(128)S(6)} %select_n.260, s32[]{:T(128)S(6)} %select_n.262), kind=kLoop, calls=%fused_computation.78 | loop fusion | bytes 37748752 | tf_op jit(solution)/shard_map/dynamic_slice | solution.py:601
  784.5 4.4 constant_dynamic-slice_fusion.3
  788.9 3.4 constant_dynamic-slice_fusion.7
  792.4 23.9 %constant_dynamic-update-slice_fusion.3 = (bf16[3072,3072]{1,0:T(8,128)(2,1)}, bf16[768,3072]{1,0:T(8,128)(2,1)}) fusion(bf16[3072,3072]{1,0:T(8,128)(2,1)} %get-tuple-element.113, s32[]{:T(128)S(6)} %select_n.259, bf16[4096,768]{1,0:T(8,128)(2,1)} %get-tuple-element.76, bf16[4096,3072]{1,0:T(8,128)(2,1)S(1)} %bitcast.25), kind=kOutput, calls=%fused_computation.66 | convolution fusion | flops 19329712128 | bytes 40894468 | tf_op jit(solution)/shard_map/dot_general | solution.py:29
  816.7 3.2 constant_dynamic-slice_fusion.14
  820.0 23.9 %constant_dynamic-update-slice_fusion.2 = (bf16[3072,3072]{1,0:T(8,128)(2,1)}, bf16[768,3072]{1,0:T(8,128)(2,1)}) fusion(bf16[3072,3072]{1,0:T(8,128)(2,1)} %get-tuple-element.163, s32[]{:T(128)S(6)} %select_n.260, bf16[4096,768]{1,0:T(8,128)(2,1)} %collective-permute-done.9, bf16[4096,3072]{1,0:T(8,128)(2,1)S(1)} %bitcast.25), kind=kOutput, calls=%fused_computation.65 | convolution fusion | flops 19329712128 | bytes 40894468 | tf_op jit(solution)/shard_map/dot_general | solution.py:29
  843.8 164.4 %collective-permute-done.18.refs_0_ = bf16[4096,640]{1,0:T(8,128)(2,1)} collective-permute-done((bf16[4096,640]{1,0:T(8,128)(2,1)}, bf16[4096,640]{1,0:T(8,128)(2,1)}, u32[]{:S(2)}, u32[]{:S(2)}) %collective-permute-start.18) | collective-permute-done | bytes 5242912 | tf_op jit(solution)/shard_map/ppermute | solution.py:541
  1008.2 3.5 constant_dynamic-slice_fusion.2
  1012.2 7.7 place.3
  1020.0 26.8 %weight_grad.4 = (bf16[3072,3072]{1,0:T(8,128)(2,1)}, bf16[3072,1024]{1,0:T(8,128)(2,1)}, bf16[3072,1024]{1,0:T(8,128)(2,1)}, bf16[3072,640]{1,0:T(8,128)(2,1)}) custom-call(s32[1]{0:T(128)} %bitcast.16.idx, bf16[4096,3072]{1,0:T(8,128)(2,1)} %get-tuple-element.88.h_ref, ...), custom_call_target="tpu_custom_call", output_to_operand_aliasing={{0}: (3, {}), {1}: (4, {}), {2}: (5, {})} | custom-call | flops 16106127360 | bytes 38273024 | tf_op jit(solution)/shard_map/weight_grad/pallas_call | solution.py:487
  1047.3 24.7 %fusion.15 = bf16[1024,3072]{1,0:T(8,128)(2,1)} fusion(bf16[768,3072]{1,0:T(8,128)(2,1)} %get-tuple-element.126, bf16[768,3072]{1,0:T(8,128)(2,1)} %get-tuple-element.124, bf16[768,3072]{1,0:T(8,128)(2,1)} %get-tuple-element.125, bf16[768,3072]{1,0:T(8,128)(2,1)} %get-tuple-element.123, bf16[1024,768]{1,0:T(8,128)(2,1)} %collective-permute-done.11, ...), kind=kOutput, calls=%fused_computation.15 | convolution fusion | flops 19431161856 | bytes 31457280 | tf_op jit(solution)/shard_map/dot_general | solution.py:602
  1074.5 23.0 %fusion.28.dh1_ref = f32[1024,3072]{1,0:T(8,128)} fusion(bf16[3072,2560]{1,0:T(8,128)(2,1)} %get-tuple-element.127, bf16[1024,640]{1,0:T(8,128)(2,1)} %collective-permute-done.20, bf16[1024,640]{1,0:T(8,128)(2,1)} %collective-permute-done.19, bf16[1024,640]{1,0:T(8,128)(2,1)} %get-tuple-element.151, bf16[1024,640]{1,0:T(8,128)(2,1)} %get-tuple-element.149), kind=kOutput, calls=%fused_computation.24 | convolution fusion | flops 16127098880 | bytes 33554432 | tf_op jit(solution)/shard_map/dot_general | solution.py:29
  1097.5 5.7 place.4
  1103.2 27.1 %weight_grad.5 = (bf16[3072,3072]{1,0:T(8,128)(2,1)}, bf16[3072,1024]{1,0:T(8,128)(2,1)}, bf16[3072,1024]{1,0:T(8,128)(2,1)}, bf16[3072,640]{1,0:T(8,128)(2,1)}) custom-call(s32[1]{0:T(128)} %bitcast.14.idx, bf16[4096,3072]{1,0:T(8,128)(2,1)} %get-tuple-element.88.h_ref, ...), custom_call_target="tpu_custom_call", output_to_operand_aliasing={{0}: (3, {}), {1}: (4, {}), {2}: (5, {})} | custom-call | flops 16106127360 | bytes 38273024 | tf_op jit(solution)/shard_map/weight_grad/pallas_call | solution.py:487
  1130.8 22.3 %fusion.20.dh0_ref = f32[1024,3072]{1,0:T(8,128)} fusion(bf16[3072,2560]{1,0:T(8,128)(2,1)} %get-tuple-element.128, bf16[1024,640]{1,0:T(8,128)(2,1)} %collective-permute-done.17, bf16[1024,640]{1,0:T(8,128)(2,1)} %collective-permute-done.16, bf16[1024,640]{1,0:T(8,128)(2,1)S(1)} %get-tuple-element.155, bf16[1024,640]{1,0:T(8,128)(2,1)S(1)} %copy-done.2), kind=kOutput, calls=%fused_computation.16 | convolution fusion | flops 16127098880 | bytes 33554432 | tf_op jit(solution)/shard_map/dot_general | solution.py:29
  1153.1 17.6 %ln_bwd.1 = (bf16[1024,3072]{1,0:T(8,128)(2,1)}, f32[1,3072]{1,0:T(1,128)}) custom-call(f32[1024,3072]{1,0:T(8,128)} %fusion.20.dh0_ref, f32[1024,3072]{1,0:T(8,128)} %fusion.28.dh1_ref, bf16[1024,3072]{1,0:T(8,128)(2,1)} %x_ref.1, bf16[1,3072]{1,0:T(2,128)(2,1)} %reshape.77.lnw_ref), custom_call_target="tpu_custom_call" | custom-call | flops 62914560 | bytes 37748736 | tf_op jit(solution)/shard_map/ln_bwd/pallas_call | solution.py:434
  1170.7 4.8 constant_dynamic-update-slice_fusion.1
  1176.3 4.8 constant_dynamic-update-slice_fusion
  1181.8 5.7 place.5
  (110 shorter events, 43.8 us)
Async XLA Ops:
  7.9 8.5 copy-start.4
  13.1 305.4 %collective-permute-start.8 = (bf16[512,3072]{1,0:T(8,128)(2,1)}, bf16[512,3072]{1,0:T(8,128)(2,1)}, u32[]{:S(2)}, u32[]{:S(2)}) collective-permute-start(bf16[512,3072]{1,0:T(8,128)(2,1)} %ln_fwd.3.h_ref), channel_id=1, source_target_pairs={{0,1},{1,0},{2,3},{3,2},{4,5},{5,4},{6,7},{7,6}} | collective-permute-start | bytes 9437192 | tf_op jit(solution)/shard_map/ppermute | solution.py:544
  13.9 215.7 %collective-permute-start.5 = (bf16[512,3072]{1,0:T(8,128)(2,1)}, bf16[512,3072]{1,0:T(8,128)(2,1)}, u32[]{:S(2)}, u32[]{:S(2)}) collective-permute-start(bf16[512,3072]{1,0:T(8,128)(2,1)} %ln_fwd.3.h_ref), channel_id=1, source_target_pairs={{0,2},{1,3},{2,0},{3,1},{4,6},{5,7},{6,4},{7,5}} | collective-permute-start | bytes 9437192 | tf_op jit(solution)/shard_map/ppermute | solution.py:541
  16.4 334.7 %collective-permute-start.12 = (bf16[1024,3072]{1,0:T(8,128)(2,1)}, bf16[1024,3072]{1,0:T(8,128)(2,1)}, u32[]{:S(2)}, u32[]{:S(2)}) collective-permute-start(bf16[1024,3072]{1,0:T(8,128)(2,1)} %g_ref.1), channel_id=1, source_target_pairs={{0,2},{1,3},{2,0},{3,1},{4,6},{5,7},{6,4},{7,5}} | collective-permute-start | bytes 18874376 | tf_op jit(solution)/shard_map/ppermute | solution.py:541
  16.4 204.1 %collective-permute-start.3 = (s32[1024]{0:T(1024)S(1)}, s32[1024]{0:T(1024)S(1)}, u32[]{:S(2)}, u32[]{:S(2)}) collective-permute-start(s32[1024]{0:T(1024)S(1)} %copy-done.4), channel_id=1, source_target_pairs={{0,2},{1,3},{2,0},{3,1},{4,6},{5,7},{6,4},{7,5}} | collective-permute-start | bytes 12296 | tf_op jit(solution)/shard_map/ppermute | solution.py:541
  23.6 264.2 %collective-permute-start = (bf16[512,3072]{1,0:T(8,128)(2,1)}, bf16[512,3072]{1,0:T(8,128)(2,1)}, u32[]{:S(2)}, u32[]{:S(2)}) collective-permute-start(bf16[512,3072]{1,0:T(8,128)(2,1)} %ln_fwd.2.h_ref), channel_id=1, source_target_pairs={{0,2},{1,3},{2,0},{3,1},{4,6},{5,7},{6,4},{7,5}} | collective-permute-start | bytes 9437192 | tf_op jit(solution)/shard_map/ppermute | solution.py:541
  54.8 168.1 %copy-start = (bf16[512,3072]{1,0:T(8,128)(2,1)S(1)}, bf16[512,3072]{1,0:T(8,128)(2,1)}, u32[]{:S(2)}) copy-start(bf16[512,3072]{1,0:T(8,128)(2,1)} %ln_fwd.2.h_ref) | copy-start | bytes 9437188
  220.5 1.2 collective-permute-start.2
  221.7 1.2 collective-permute-start.4
  222.8 106.8 %collective-permute-start.7 = (bf16[512,3072]{1,0:T(8,128)(2,1)S(1)}, bf16[512,3072]{1,0:T(8,128)(2,1)}, u32[]{:S(2)}, u32[]{:S(2)}) collective-permute-start(bf16[512,3072]{1,0:T(8,128)(2,1)S(1)} %copy-done), channel_id=1, source_target_pairs={{0,1},{1,0},{2,3},{3,2},{4,5},{5,4},{6,7},{7,6}} | collective-permute-start | bytes 9437192 | tf_op jit(solution)/shard_map/ppermute | solution.py:544
  229.6 121.6 %collective-permute-start.6 = (bf16[512,3072]{1,0:T(8,128)(2,1)}, bf16[512,3072]{1,0:T(8,128)(2,1)}, u32[]{:S(2)}, u32[]{:S(2)}) collective-permute-start(bf16[512,3072]{1,0:T(8,128)(2,1)} %collective-permute-done.5.h_ref), channel_id=1, source_target_pairs={{0,1},{1,0},{2,3},{3,2},{4,5},{5,4},{6,7},{7,6}} | collective-permute-start | bytes 9437192 | tf_op jit(solution)/shard_map/ppermute | solution.py:544
  287.8 84.4 %collective-permute-start.1 = (bf16[512,3072]{1,0:T(8,128)(2,1)}, bf16[512,3072]{1,0:T(8,128)(2,1)}, u32[]{:S(2)}, u32[]{:S(2)}) collective-permute-start(bf16[512,3072]{1,0:T(8,128)(2,1)} %collective-permute-done.h_ref), channel_id=1, source_target_pairs={{0,1},{1,0},{2,3},{3,2},{4,5},{5,4},{6,7},{7,6}} | collective-permute-start | bytes 9437192 | tf_op jit(solution)/shard_map/ppermute | solution.py:544
  318.5 168.3 %collective-permute-start.14 = (bf16[1024,3072]{1,0:T(8,128)(2,1)}, bf16[1024,3072]{1,0:T(8,128)(2,1)}, u32[]{:S(2)}, u32[]{:S(2)}) collective-permute-start(bf16[1024,3072]{1,0:T(8,128)(2,1)} %g_ref.1), channel_id=1, source_target_pairs={{0,1},{1,0},{2,3},{3,2},{4,5},{5,4},{6,7},{7,6}} | collective-permute-start | bytes 18874376 | tf_op jit(solution)/shard_map/ppermute | solution.py:544
  351.1 156.0 %collective-permute-start.13 = (bf16[1024,3072]{1,0:T(8,128)(2,1)}, bf16[1024,3072]{1,0:T(8,128)(2,1)}, u32[]{:S(2)}, u32[]{:S(2)}) collective-permute-start(bf16[1024,3072]{1,0:T(8,128)(2,1)} %collective-permute-done.12.g_ref), channel_id=1, source_target_pairs={{0,1},{1,0},{2,3},{3,2},{4,5},{5,4},{6,7},{7,6}} | collective-permute-start | bytes 18874376 | tf_op jit(solution)/shard_map/ppermute | solution.py:544
  485.6 330.7 %collective-permute-start.9 = (bf16[4096,768]{1,0:T(8,128)(2,1)}, bf16[4096,768]{1,0:T(8,128)(2,1)}, u32[]{:S(2)}, u32[]{:S(2)}) collective-permute-start(bf16[4096,768]{1,0:T(8,128)(2,1)} %get-tuple-element.76), channel_id=1, source_target_pairs={{0,2},{1,3},{2,0},{3,1},{4,6},{5,7},{6,4},{7,5}} | collective-permute-start | bytes 18874376 | tf_op jit(solution)/shard_map/ppermute | solution.py:541
  749.2 262.4 %collective-permute-start.23 = (bf16[3072,1280]{1,0:T(8,128)(2,1)}, bf16[3072,1280]{1,0:T(8,128)(2,1)}, u32[]{:S(2)}, u32[]{:S(2)}) collective-permute-start(bf16[3072,1280]{1,0:T(8,128)(2,1)} %get-tuple-element.92), channel_id=1, source_target_pairs={{0,1},{1,0},{2,3},{3,2},{4,5},{5,4},{6,7},{7,6}} | collective-permute-start | bytes 23592968 | tf_op jit(solution)/shard_map/ppermute | solution.py:544
  760.3 22.2 %slice-start.6 = ((s8[6291456]{0:T(1024)(128)(4,1)}), s8[4194304]{0:T(1024)(128)(4,1)S(1)}, s32[]{:S(2)}) async-start(s8[6291456]{0:T(1024)(128)(4,1)} %bitcast.26), calls=%async_computation.6 | async-start | bytes 8388608
  765.9 16.6 %slice-start.7 = ((s8[6291456]{0:T(1024)(128)(4,1)}), s8[2097152]{0:T(1024)(128)(4,1)S(1)}, s32[]{:S(2)}) async-start(s8[6291456]{0:T(1024)(128)(4,1)} %bitcast.26), calls=%async_computation.7 | async-start | bytes 4194304
  765.9 26.4 %slice-start = ((s8[25165824]{0:T(1024)(128)(4,1)}), s8[4194304]{0:T(1024)(128)(4,1)S(1)}, s32[]{:S(2)}) async-start(s8[25165824]{0:T(1024)(128)(4,1)} %bitcast.24), calls=%async_computation | async-start | bytes 8388608
  766.0 26.4 %slice-start.1 = ((s8[25165824]{0:T(1024)(128)(4,1)}), s8[4194304]{0:T(1024)(128)(4,1)S(1)}, s32[]{:S(2)}) async-start(s8[25165824]{0:T(1024)(128)(4,1)} %bitcast.24), calls=%async_computation.1 | async-start | bytes 8388608
  766.0 26.4 %slice-start.2 = ((s8[25165824]{0:T(1024)(128)(4,1)}), s8[4194304]{0:T(1024)(128)(4,1)S(1)}, s32[]{:S(2)}) async-start(s8[25165824]{0:T(1024)(128)(4,1)} %bitcast.24), calls=%async_computation.2 | async-start | bytes 8388608
  766.0 26.4 %slice-start.3 = ((s8[25165824]{0:T(1024)(128)(4,1)}), s8[4194304]{0:T(1024)(128)(4,1)S(1)}, s32[]{:S(2)}) async-start(s8[25165824]{0:T(1024)(128)(4,1)} %bitcast.24), calls=%async_computation.3 | async-start | bytes 8388608
  766.0 26.4 %slice-start.4 = ((s8[25165824]{0:T(1024)(128)(4,1)}), s8[4194304]{0:T(1024)(128)(4,1)S(1)}, s32[]{:S(2)}) async-start(s8[25165824]{0:T(1024)(128)(4,1)} %bitcast.24), calls=%async_computation.4 | async-start | bytes 8388608
  780.6 239.4 %collective-permute-start.15 = (bf16[4096,640]{1,0:T(8,128)(2,1)}, bf16[4096,640]{1,0:T(8,128)(2,1)}, u32[]{:S(2)}, u32[]{:S(2)}) collective-permute-start(bf16[4096,640]{1,0:T(8,128)(2,1)} %attn_bwd.2.refs_0_), channel_id=1, source_target_pairs={{0,2},{1,3},{2,0},{3,1},{4,6},{5,7},{6,4},{7,5}} | collective-permute-start | bytes 15728648 | tf_op jit(solution)/shard_map/ppermute | solution.py:541
  781.0 227.2 %collective-permute-start.18 = (bf16[4096,640]{1,0:T(8,128)(2,1)}, bf16[4096,640]{1,0:T(8,128)(2,1)}, u32[]{:S(2)}, u32[]{:S(2)}) collective-permute-start(bf16[4096,640]{1,0:T(8,128)(2,1)} %attn_bwd.3.refs_1_), channel_id=1, source_target_pairs={{0,2},{1,3},{2,0},{3,1},{4,6},{5,7},{6,4},{7,5}} | collective-permute-start | bytes 15728648 | tf_op jit(solution)/shard_map/ppermute | solution.py:541
  784.5 7.8 slice-start.5
  784.5 262.2 %collective-permute-start.10 = (bf16[1024,768]{1,0:T(8,128)(2,1)}, bf16[1024,768]{1,0:T(8,128)(2,1)}, u32[]{:S(2)}, u32[]{:S(2)}) collective-permute-start(bf16[1024,768]{1,0:T(8,128)(2,1)} %get-tuple-element.144), channel_id=1, source_target_pairs={{0,1},{1,0},{2,3},{3,2},{4,5},{5,4},{6,7},{7,6}} | collective-permute-start | bytes 4718600 | tf_op jit(solution)/shard_map/ppermute | solution.py:544
  816.2 354.4 %collective-permute-start.26 = (bf16[768,3072]{1,0:T(8,128)(2,1)}, bf16[768,3072]{1,0:T(8,128)(2,1)}, u32[]{:S(2)}, u32[]{:S(2)}) collective-permute-start(bf16[768,3072]{1,0:T(8,128)(2,1)} %get-tuple-element.164), channel_id=1, source_target_pairs={{0,1},{1,0},{2,3},{3,2},{4,5},{5,4},{6,7},{7,6}} | collective-permute-start | bytes 14155784 | tf_op jit(solution)/shard_map/ppermute | solution.py:544
  1008.2 39.1 %collective-permute-start.11 = (bf16[1024,768]{1,0:T(8,128)(2,1)}, bf16[1024,768]{1,0:T(8,128)(2,1)}, u32[]{:S(2)}, u32[]{:S(2)}) collective-permute-start(bf16[1024,768]{1,0:T(8,128)(2,1)} %get-tuple-element.146), channel_id=1, source_target_pairs={{0,1},{1,0},{2,3},{3,2},{4,5},{5,4},{6,7},{7,6}} | collective-permute-start | bytes 4718600 | tf_op jit(solution)/shard_map/ppermute | solution.py:544
  1011.7 164.6 %collective-permute-start.27 = (bf16[768,3072]{1,0:T(8,128)(2,1)}, bf16[768,3072]{1,0:T(8,128)(2,1)}, u32[]{:S(2)}, u32[]{:S(2)}) collective-permute-start(bf16[768,3072]{1,0:T(8,128)(2,1)} %get-tuple-element.166), channel_id=1, source_target_pairs={{0,1},{1,0},{2,3},{3,2},{4,5},{5,4},{6,7},{7,6}} | collective-permute-start | bytes 14155784 | tf_op jit(solution)/shard_map/ppermute | solution.py:544
  1019.9 54.1 %collective-permute-start.19 = (bf16[1024,640]{1,0:T(8,128)(2,1)}, bf16[1024,640]{1,0:T(8,128)(2,1)}, u32[]{:S(2)}, u32[]{:S(2)}) collective-permute-start(bf16[1024,640]{1,0:T(8,128)(2,1)} %get-tuple-element.150), channel_id=1, source_target_pairs={{0,1},{1,0},{2,3},{3,2},{4,5},{5,4},{6,7},{7,6}} | collective-permute-start | bytes 3932168 | tf_op jit(solution)/shard_map/ppermute | solution.py:544
  1020.0 27.4 %copy-start.1 = (bf16[1024,768]{1,0:T(8,128)(2,1)S(1)}, bf16[1024,768]{1,0:T(8,128)(2,1)}, u32[]{:S(2)}) copy-start(bf16[1024,768]{1,0:T(8,128)(2,1)} %get-tuple-element.143) | copy-start | bytes 4718596
  1046.8 27.7 %collective-permute-start.20 = (bf16[1024,640]{1,0:T(8,128)(2,1)}, bf16[1024,640]{1,0:T(8,128)(2,1)}, u32[]{:S(2)}, u32[]{:S(2)}) collective-permute-start(bf16[1024,640]{1,0:T(8,128)(2,1)} %get-tuple-element.152), channel_id=1, source_target_pairs={{0,1},{1,0},{2,3},{3,2},{4,5},{5,4},{6,7},{7,6}} | collective-permute-start | bytes 3932168 | tf_op jit(solution)/shard_map/ppermute | solution.py:544
  1047.3 50.2 %collective-permute-start.24 = (bf16[3072,640]{1,0:T(8,128)(2,1)}, bf16[3072,640]{1,0:T(8,128)(2,1)}, u32[]{:S(2)}, u32[]{:S(2)}) collective-permute-start(bf16[3072,640]{1,0:T(8,128)(2,1)} %get-tuple-element.99), channel_id=1, source_target_pairs={{0,1},{1,0},{2,3},{3,2},{4,5},{5,4},{6,7},{7,6}} | collective-permute-start | bytes 11796488 | tf_op jit(solution)/shard_map/ppermute | solution.py:544
  1074.0 56.8 %collective-permute-start.16 = (bf16[1024,640]{1,0:T(8,128)(2,1)}, bf16[1024,640]{1,0:T(8,128)(2,1)}, u32[]{:S(2)}, u32[]{:S(2)}) collective-permute-start(bf16[1024,640]{1,0:T(8,128)(2,1)} %get-tuple-element.154), channel_id=1, source_target_pairs={{0,1},{1,0},{2,3},{3,2},{4,5},{5,4},{6,7},{7,6}} | collective-permute-start | bytes 3932168 | tf_op jit(solution)/shard_map/ppermute | solution.py:544
  1074.5 56.3 %collective-permute-start.17 = (bf16[1024,640]{1,0:T(8,128)(2,1)S(1)}, bf16[1024,640]{1,0:T(8,128)(2,1)}, u32[]{:S(2)}, u32[]{:S(2)}) collective-permute-start(bf16[1024,640]{1,0:T(8,128)(2,1)S(1)} %get-tuple-element.156), channel_id=1, source_target_pairs={{0,1},{1,0},{2,3},{3,2},{4,5},{5,4},{6,7},{7,6}} | collective-permute-start | bytes 3932168 | tf_op jit(solution)/shard_map/ppermute | solution.py:544
  1103.2 27.5 %copy-start.2 = (bf16[1024,640]{1,0:T(8,128)(2,1)S(1)}, bf16[1024,640]{1,0:T(8,128)(2,1)}, u32[]{:S(2)}) copy-start(bf16[1024,640]{1,0:T(8,128)(2,1)} %get-tuple-element.153) | copy-start | bytes 3932164
  1130.3 51.5 %collective-permute-start.25 = (bf16[3072,640]{1,0:T(8,128)(2,1)}, bf16[3072,640]{1,0:T(8,128)(2,1)}, u32[]{:S(2)}, u32[]{:S(2)}) collective-permute-start(bf16[3072,640]{1,0:T(8,128)(2,1)} %get-tuple-element.106), channel_id=1, source_target_pairs={{0,1},{1,0},{2,3},{3,2},{4,5},{5,4},{6,7},{7,6}} | collective-permute-start | bytes 11796488 | tf_op jit(solution)/shard_map/ppermute | solution.py:544
  1170.6 4.9 copy-start.3
  1170.6 4.9 collective-permute-start.21
  1175.5 5.6 collective-permute-start.22

commit v4 on v3

--- a/solution.py
+++ b/solution.py
@@ -59,9 +59,8 @@
 
 
 def qkv_kernel(idx, h_ref, wq_ref, wk_ref, wv_ref, cos_ref, sin_ref, *rest):
-    hall_ref, qkv_ref = rest[-2:]
+    qkv_ref = rest[-1]
     h = h_ref[...]
-    hall_ref[...] = h
     cos_t = cos_ref[...]
     sin_t = sin_ref[...]
     nq = wq_ref.shape[1]
@@ -93,19 +92,19 @@
     args = [idx, h, w_q, w_k, w_v, cos_t, sin_t]
     aliases = {}
     if prev is not None:
-        in_specs += [pl.BlockSpec(memory_space=pl.ANY)] * 2
-        args += list(prev)
-        aliases = {7: 0, 8: 1}
+        in_specs.append(pl.BlockSpec(memory_space=pl.ANY))
+        args.append(prev)
+        aliases = {7: 0}
     cols = cq + 2 * ck
     return pl.pallas_call(
         qkv_kernel,
-        out_shape=(jax.ShapeDtypeStruct((seq, dim), BF16), jax.ShapeDtypeStruct((seq, cols), BF16)),
+        out_shape=jax.ShapeDtypeStruct((seq, cols), BF16),
         grid_spec=pltpu.PrefetchScalarGridSpec(
             num_scalar_prefetch=1, grid=(per,), in_specs=in_specs,
-            out_specs=(pl.BlockSpec((ROWS, dim), here), pl.BlockSpec((ROWS, cols), here))),
+            out_specs=pl.BlockSpec((ROWS, cols), here)),
         input_output_aliases=aliases,
         compiler_params=pltpu.CompilerParams(dimension_semantics=("arbitrary",), vmem_limit_bytes=VMEM_BYTES),
-        cost_estimate=cost(2 * rows * dim * cols, 2 * (2 * rows * dim + dim * cols + rows * cols)),
+        cost_estimate=cost(2 * rows * dim * cols, 2 * (rows * dim + dim * cols + rows * cols)),
         name="qkv",
     )(*args)
 
@@ -131,10 +130,8 @@
 
 
 def do_kernel(idx, g_ref, wo_ref, *rest):
-    gall_ref, do_ref = rest[-2:]
-    g = g_ref[...]
-    gall_ref[...] = g
-    do_ref[...] = mm(g, wo_ref[...], ((1,), (0,))).astype(BF16)
+    do_ref = rest[-1]
+    do_ref[...] = mm(g_ref[...], wo_ref[...], ((1,), (0,))).astype(BF16)
 
 
 def do_block(idx, g, wo_t, seq, prev):
@@ -149,18 +146,18 @@
     args = [idx, g, wo_t]
     aliases = {}
     if prev is not None:
-        in_specs += [pl.BlockSpec(memory_space=pl.ANY)] * 2
-        args += list(prev)
-        aliases = {3: 0, 4: 1}
+        in_specs.append(pl.BlockSpec(memory_space=pl.ANY))
+        args.append(prev)
+        aliases = {3: 0}
     return pl.pallas_call(
         do_kernel,
-        out_shape=(jax.ShapeDtypeStruct((seq, dim), BF16), jax.ShapeDtypeStruct((seq, ce), BF16)),
+        out_shape=jax.ShapeDtypeStruct((seq, ce), BF16),
         grid_spec=pltpu.PrefetchScalarGridSpec(
             num_scalar_prefetch=1, grid=(per,), in_specs=in_specs,
-            out_specs=(pl.BlockSpec((ROWS, dim), here), pl.BlockSpec((ROWS, ce), here))),
+            out_specs=pl.BlockSpec((ROWS, ce), here)),
         input_output_aliases=aliases,
         compiler_params=pltpu.CompilerParams(dimension_semantics=("arbitrary",), vmem_limit_bytes=VMEM_BYTES),
-        cost_estimate=cost(2 * rows * dim * ce, 2 * (2 * rows * dim + dim * ce + rows * ce)),
+        cost_estimate=cost(2 * rows * dim * ce, 2 * (rows * dim + dim * ce + rows * ce)),
         name="d_o",
     )(*args)
 
@@ -407,41 +404,147 @@
     )(qkv, qkv, qkv, d_o, o_t, lse, cos_t, sin_t)
 
 
-def ln_bwd_kernel(dh0_ref, dh1_ref, x_ref, lnw_ref, dx_ref, dw_ref):
-    @pl.when(pl.program_id(0) == 0)
-    def _():
+N_TILE = 1024
+
+
+def accumulate(acc_sc, weight):
+    def tile(n, _):
+        cols = pl.ds(pl.multiple_of(n * N_TILE, N_TILE), N_TILE)
+        acc_sc[:, cols] += weight(cols)
+        return 0
+
+    lax.fori_loop(0, acc_sc.shape[1] // N_TILE, tile, 0)
+
+
+def out_kernel(idx, *refs):
+    pieces, (w_ref, out_ref, cur_sc, acc_sc) = refs[:4], refs[4:]
+    src = pl.program_id(0)
+    for n, piece in enumerate(pieces):
+        @pl.when(src == n)
+        def _():
+            cur_sc[...] = piece[...]
+
+    @pl.when(src == 0)
+    def _():
+        acc_sc[...] = jnp.zeros_like(acc_sc)
+
+    accumulate(acc_sc, lambda cols: mm(cur_sc[...], w_ref[:, cols], ((1,), (0,))))
+
+    @pl.when(src == 3)
+    def _():
+        out_ref[...] = acc_sc[...].astype(BF16)
+
+
+def single(shape, index):
+    return pl.BlockSpec(shape, index, pipeline_mode=pl.Buffered(1))
+
+
+def out_proj(idx, pieces, w_o, rows):
+    wide = pieces[0].shape[1]
+    dim = w_o.shape[1]
+    mine = single((rows, wide), lambda s, ix: (ix[0], 0))
+    sent = single((rows, wide), lambda s, ix: (0, 0))
+    return pl.pallas_call(
+        out_kernel,
+        out_shape=jax.ShapeDtypeStruct((rows, dim), BF16),
+        grid_spec=pltpu.PrefetchScalarGridSpec(
+            num_scalar_prefetch=1, grid=(4,),
+            in_specs=[mine, mine, sent, sent, pl.BlockSpec((wide, dim), lambda s, ix: (ix[1 + s], 0))],
+            out_specs=pl.BlockSpec((rows, dim), lambda s, ix: (0, 0)),
+            scratch_shapes=[pltpu.VMEM((rows, wide), BF16), pltpu.VMEM((rows, dim), F32)]),
+        compiler_params=pltpu.CompilerParams(dimension_semantics=("arbitrary",), vmem_limit_bytes=VMEM_BYTES),
+        cost_estimate=cost(8 * rows * dim * wide, 2 * (5 * rows * dim)),
+        name="out_proj",
+    )(idx, *pieces, w_o)
+
+
+def dh_kernel(idx, *refs):
+    pieces = refs[:8]
+    wq_ref, wk_ref, wv_ref, x_ref, lnw_ref, dx_ref, dw_ref, cur_sc, acc_sc, dx_sc, sem = refs[8:]
+    src = pl.program_id(0)
+    wide = wq_ref.shape[1]
+    each = wide // 2
+    for n in range(4):
+        @pl.when(src == n)
+        def _():
+            for t in range(2):
+                piece = pieces[2 * n + t]
+                cur_sc[:, t * each:(t + 1) * each] = piece[:, :each]
+                for part in range(2):
+                    start = wide + (2 * part + t) * HEAD_DIM
+                    cur_sc[:, start:start + HEAD_DIM] = piece[:, each + part * HEAD_DIM:each + (part + 1) * HEAD_DIM]
+
+    @pl.when(src == 0)
+    def _():
+        acc_sc[...] = jnp.zeros_like(acc_sc)
+
+    both = wide + 2 * HEAD_DIM
+    accumulate(acc_sc, lambda cols: mm(cur_sc[:, :wide], wq_ref[cols, :], ((1,), (1,)))
+               + mm(cur_sc[:, wide:both], wk_ref[cols, :], ((1,), (1,)))
+               + mm(cur_sc[:, both:], wv_ref[cols, :], ((1,), (1,))))
+
+    @pl.when(src == 3)
+    def _():
+        blk = dx_sc.shape[1]
+        n_blk = x_ref.shape[0] // blk
+        weight = lnw_ref[...].astype(F32)
         dw_ref[...] = jnp.zeros_like(dw_ref)
 
-    xf = x_ref[...].astype(F32)
-    mean = jnp.mean(xf, axis=-1, keepdims=True)
-    cen = xf - mean
-    var = jnp.mean(cen * cen, axis=-1, keepdims=True)
-    rstd = lax.rsqrt(var + LN_EPS)
-    xhat = cen * rstd
-    dh = dh0_ref[...] + dh1_ref[...]
-    dw_ref[...] += jnp.sum(dh * xhat, axis=0, keepdims=True)
-    dxh = dh * lnw_ref[...].astype(F32)
-    mean_d = jnp.mean(dxh, axis=-1, keepdims=True)
-    mean_dx = jnp.mean(dxh * xhat, axis=-1, keepdims=True)
-    dx_ref[...] = (rstd * (dxh - mean_d - xhat * mean_dx)).astype(BF16)
-
-
-def ln_backward(dh0, dh1, x, ln_w):
+        def put(n, slot):
+            return pltpu.make_async_copy(dx_sc.at[slot], dx_ref.at[pl.ds(n * blk, blk), :], sem.at[slot])
+
+        def one(n, _):
+            slot = n % 2
+            rows = pl.ds(n * blk, blk)
+
+            @pl.when(n >= 2)
+            def _():
+                put(n - 2, slot).wait()
+
+            xf = x_ref[rows, :].astype(F32)
+            mean = jnp.mean(xf, axis=-1, keepdims=True)
+            cen = xf - mean
+            var = jnp.mean(cen * cen, axis=-1, keepdims=True)
+            rstd = lax.rsqrt(var + LN_EPS)
+            xhat = cen * rstd
+            dh = acc_sc[rows, :]
+            dw_ref[...] += jnp.sum(dh * xhat, axis=0, keepdims=True)
+            dxh = dh * weight
+            mean_d = jnp.mean(dxh, axis=-1, keepdims=True)
+            mean_dx = jnp.mean(dxh * xhat, axis=-1, keepdims=True)
+            dx_sc[slot] = (rstd * (dxh - mean_d - xhat * mean_dx)).astype(BF16)
+            put(n, slot).start()
+            return 0
+
+        lax.fori_loop(0, n_blk, one, 0)
+        for n in range(n_blk - 2, n_blk):
+            put(n, n % 2).wait()
+
+
+def hidden_grad(idx, pieces, w_q, w_k, w_v, x, ln_w, n_dev):
     rows, dim = x.shape
+    cols = pieces[0].shape[1]
+    cq, ck = w_q.shape[1] // n_dev, w_k.shape[1] // n_dev
+    mine = single((rows, cols), lambda s, ix: (ix[0], 0))
+    sent = single((rows, cols), lambda s, ix: (0, 0))
+    const = lambda s, ix: (0, 0)
+    head = lambda s, ix: (0, ix[1 + s])
     blk = 128
-    row = lambda i: (i, 0)
-    const = lambda i: (0, 0)
-    return pl.pallas_call(
-        ln_bwd_kernel,
-        grid=(rows // blk,),
-        in_specs=[pl.BlockSpec((blk, dim), row), pl.BlockSpec((blk, dim), row),
-                  pl.BlockSpec((blk, dim), row), pl.BlockSpec((1, dim), const)],
-        out_specs=(pl.BlockSpec((blk, dim), row), pl.BlockSpec((1, dim), const)),
+    return pl.pallas_call(
+        dh_kernel,
         out_shape=(jax.ShapeDtypeStruct((rows, dim), BF16), jax.ShapeDtypeStruct((1, dim), F32)),
+        grid_spec=pltpu.PrefetchScalarGridSpec(
+            num_scalar_prefetch=1, grid=(4,),
+            in_specs=[mine] * 4 + [sent] * 4
+            + [pl.BlockSpec((dim, cq), head), pl.BlockSpec((dim, ck), head), pl.BlockSpec((dim, ck), head),
+               single((rows, dim), const), pl.BlockSpec((1, dim), const)],
+            out_specs=(pl.BlockSpec(memory_space=pl.ANY), pl.BlockSpec((1, dim), const)),
+            scratch_shapes=[pltpu.VMEM((rows, 2 * cols), BF16), pltpu.VMEM((rows, dim), F32),
+                            pltpu.VMEM((2, blk, dim), BF16), pltpu.SemaphoreType.DMA((2,))]),
         compiler_params=pltpu.CompilerParams(dimension_semantics=("arbitrary",), vmem_limit_bytes=VMEM_BYTES),
-        cost_estimate=cost(20 * rows * dim, 12 * rows * dim),
-        name="ln_bwd",
-    )(dh0, dh1, x, ln_w)
+        cost_estimate=cost(16 * rows * dim * cols, 2 * (2 * rows * dim + 8 * cols * (rows + dim))),
+        name="hidden_grad",
+    )(idx, *pieces, w_q, w_k, w_v, x, ln_w)
 
 
 def reserve(*shapes):
@@ -454,30 +557,37 @@
     )()
 
 
-def dw_kernel(idx, h_ref, *refs):
+def dw_kernel(idx, *refs):
+    hs, refs = refs[:4], refs[4:]
     n = len(refs) - 8
+    rows = hs[0].shape[0]
     grs, (q_ref, k_ref, v_ref, piece_ref, gr_sc) = refs[:n], refs[-5:]
     wide = q_ref.shape[1] // n
     cols = piece_ref.shape[1]
 
     @pl.when(pl.program_id(0) == 0)
     def _():
-        for t, gr in enumerate(grs):
-            gr_sc[:, t * wide:(t + 1) * wide] = gr[:, :wide]
-            for part in range(2):
-                start = n * wide + part * n * HEAD_DIM + t * HEAD_DIM
-                gr_sc[:, start:start + HEAD_DIM] = gr[:, wide + part * HEAD_DIM:wide + (part + 1) * HEAD_DIM]
+        for b in range(4):
+            to = slice(b * rows, (b + 1) * rows)
+            at = pl.ds(idx[1 + b] * rows, rows)
+            for t, gr in enumerate(grs):
+                gr_sc[to, t * wide:(t + 1) * wide] = gr[at, :wide]
+                for part in range(2):
+                    start = n * wide + part * n * HEAD_DIM + t * HEAD_DIM
+                    gr_sc[to, start:start + HEAD_DIM] = gr[at, wide + part * HEAD_DIM:wide + (part + 1) * HEAD_DIM]
 
     for start in range(0, cols, 256):
         stop = min(start + 256, cols)
-        piece_ref[:, start:stop] = mm(h_ref[...], gr_sc[:, start:stop], ((0,), (0,))).astype(BF16)
+        val = sum(mm(h[...], gr_sc[b * rows:(b + 1) * rows, start:stop], ((0,), (0,))) for b, h in enumerate(hs))
+        piece_ref[:, start:stop] = val.astype(BF16)
     q_ref[...] = piece_ref[:, :n * wide]
     k_ref[...] = piece_ref[:, n * wide:n * (wide + HEAD_DIM)]
     v_ref[...] = piece_ref[:, n * (wide + HEAD_DIM):]
 
 
-def weight_grad(idx, h_all, grs, bufs):
-    seq, dim = h_all.shape
+def weight_grad(idx, hs, grs, bufs):
+    rows, dim = hs[0].shape
+    seq = 4 * rows
     n = len(grs)
     cols = n * grs[0].shape[1]
     wide = REP * HEAD_DIM * n
@@ -489,17 +599,46 @@
         out_shape=tuple(jax.ShapeDtypeStruct(b.shape, BF16) for b in bufs) + (jax.ShapeDtypeStruct((dim, cols), BF16),),
         grid_spec=pltpu.PrefetchScalarGridSpec(
             num_scalar_prefetch=1, grid=(dim // blk,),
-            in_specs=[pl.BlockSpec((seq, blk), lambda i, ix: (0, i))]
+            in_specs=[pl.BlockSpec((rows, blk), lambda i, ix: (0, i))] * 4
             + [pl.BlockSpec((seq, cols // n), lambda i, ix: (0, 0), pipeline_mode=pl.Buffered(1)) for _ in grs]
             + [pl.BlockSpec(memory_space=pl.ANY)] * 3,
             out_specs=(pl.BlockSpec((blk, wide), there), pl.BlockSpec((blk, n * HEAD_DIM), there),
                        pl.BlockSpec((blk, n * HEAD_DIM), there), pl.BlockSpec((blk, cols), lambda i, ix: (i, 0))),
             scratch_shapes=[pltpu.VMEM((seq, cols), BF16)]),
-        input_output_aliases={2 + n: 0, 3 + n: 1, 4 + n: 2},
+        input_output_aliases={5 + n: 0, 6 + n: 1, 7 + n: 2},
         compiler_params=pltpu.CompilerParams(dimension_semantics=("arbitrary",), vmem_limit_bytes=VMEM_BYTES),
         cost_estimate=cost(flops, 2 * (seq * dim + seq * cols + 2 * dim * cols)),
         name="weight_grad",
-    )(idx, h_all, *grs, *bufs)
+    )(idx, *hs, *grs, *bufs)
+
+
+def dwo_kernel(idx, o_ref, *refs):
+    gs, (buf_ref, out_ref, piece_ref) = refs[:4], refs[4:]
+    rows = gs[0].shape[0]
+    for start in range(0, piece_ref.shape[1], 256):
+        cols = slice(start, start + 256)
+        val = sum(mm(o_ref[pl.ds(idx[1 + b] * rows, rows), :], g[:, cols], ((0,), (0,))) for b, g in enumerate(gs))
+        piece_ref[:, cols] = val.astype(BF16)
+    out_ref[...] = piece_ref[...]
+
+
+def out_weight_grad(idx, o, gs, buf):
+    seq, wide = o.shape
+    rows, dim = gs[0].shape
+    blk = 512
+    return pl.pallas_call(
+        dwo_kernel,
+        out_shape=(jax.ShapeDtypeStruct(buf.shape, BF16), jax.ShapeDtypeStruct((wide, dim), BF16)),
+        grid_spec=pltpu.PrefetchScalarGridSpec(
+            num_scalar_prefetch=1, grid=(dim // blk,),
+            in_specs=[single((seq, wide), lambda i, ix: (0, 0))]
+            + [pl.BlockSpec((rows, blk), lambda i, ix: (0, i))] * 4 + [pl.BlockSpec(memory_space=pl.ANY)],
+            out_specs=(pl.BlockSpec((wide, blk), lambda i, ix: (ix[0], i)), pl.BlockSpec((wide, blk), lambda i, ix: (0, i)))),
+        input_output_aliases={6: 0},
+        compiler_params=pltpu.CompilerParams(dimension_semantics=("arbitrary",), vmem_limit_bytes=VMEM_BYTES),
+        cost_estimate=cost(2 * seq * wide * dim, 2 * (seq * dim + seq * wide + 2 * wide * dim)),
+        name="out_weight_grad",
+    )(idx, o, *gs, buf)
 
 
 def place_kernel(idx, piece_ref, *refs):
@@ -547,9 +686,7 @@
         rows, dim = hidden.shape
         seq = rows * n_dev
         kv_local = w_k.shape[1] // HEAD_DIM // n_dev
-        wide = REP * HEAD_DIM
         cq = w_q.shape[1] // n_dev
-        ck = w_k.shape[1] // n_dev
         me = lax.axis_index('sp')
         chip, core = me // 2, me % 2
         hb = 2 * core + chip
@@ -560,11 +697,9 @@
         pos_src = (positions, over_core(positions), pos_par, over_core(pos_par))
         pos = jnp.concatenate([lax.select_n(me ^ b, *pos_src) for b in range(n_dev)])
         ln_row = ln_weight.reshape(1, dim)
-        half = rows // 2
-        h_own = [ln_forward(hidden[n * half:(n + 1) * half], ln_row) for n in range(2)]
-        h_par = [over_chip(h) for h in h_own]
+        x_par = over_chip(hidden)
         g_par = over_chip(d_attn)
-        h_sib = [over_core(h) for h in h_own]
+        x_sib = over_core(hidden)
         g_sib = over_core(d_attn)
 
         inv_freq = ROPE_BASE ** (-jnp.arange(0, HEAD_DIM, 2, dtype=F32) / HEAD_DIM)
@@ -572,45 +707,41 @@
         cos_t = jnp.cos(angles)
         sin_t = jnp.sin(angles) * jnp.where(jnp.arange(HEAD_DIM) % 2 == 0, -1.0, 1.0)[None, :]
 
-        h_sp = [over_core(h) for h in h_par]
+        x_sp = over_core(x_par)
         g_sp = over_core(g_par)
 
-        hq = None
-        for tok, h in ((toks[0], h_own), (toks[2], h_sib)):
-            for n in range(2):
-                hq = qkv_block(jnp.stack([hb, 2 * tok + n]).astype(jnp.int32), h[n], w_q, w_k, w_v, cos_t, sin_t, seq, n_dev, hq)
-        for n in range(2):
-            for tok, h in ((toks[1], h_par), (toks[3], h_sp)):
-                hq = qkv_block(jnp.stack([hb, 2 * tok + n]).astype(jnp.int32), h[n], w_q, w_k, w_v, cos_t, sin_t, seq, n_dev, hq)
-        h_all, qkv = hq
+        hs = [None] * 4
+        qkv = None
+        for b, x in ((0, hidden), (2, x_sib), (1, x_par), (3, x_sp)):
+            hs[b] = ln_forward(x, ln_row)
+            qkv = qkv_block(jnp.stack([hb, toks[b]]).astype(jnp.int32), hs[b], w_q, w_k, w_v, cos_t, sin_t, seq, n_dev, qkv)
         o_own, o_t, lse = attn_forward(qkv, kv_local)
 
         wo_t = transpose_rows(hb.reshape(1).astype(jnp.int32), w_o, n_dev)
-        gd = None
-        for tok, g in ((toks[0], d_attn), (toks[2], g_sib), (toks[1], g_par), (toks[3], g_sp)):
-            idx = jnp.stack([hb, tok]).astype(jnp.int32)
-            gd = do_block(idx, g, wo_t, seq, gd)
-        g_all, d_o = gd
+        gs = [d_attn, g_par, g_sib, g_sp]
+        d_o = None
+        for b in (0, 2, 1, 3):
+            d_o = do_block(jnp.stack([hb, toks[b]]).astype(jnp.int32), gs[b], wo_t, seq, d_o)
 
         def own_rows(val, dev):
             return lax.dynamic_slice_in_dim(val, dev * rows, rows, 0)
 
         o_par = over_chip(o_own)
-        o_tok = [own_rows(o_own, me), own_rows(o_par, me),
-                 over_core(own_rows(o_own, me ^ 1)), over_core(own_rows(o_par, me ^ 1))]
-        wo_perm = jnp.concatenate([lax.dynamic_slice_in_dim(w_o, b * cq, cq, 0) for b in hbs], axis=0)
-        attn_out = jnp.dot(jnp.concatenate(o_tok, axis=1), wo_perm, preferred_element_type=F32).astype(BF16)
-
-        def token_dot(lhs, rhs):
-            return mm(lhs, rhs, ((0,), (0,))).astype(BF16)
-
-        dwo_own = token_dot(o_own, g_all)
-        dwo_par = token_dot(o_par, g_all)
+        sources = jnp.stack([me, *hbs]).astype(jnp.int32)
+        o_tok = [o_own, o_par, over_core(own_rows(o_own, me ^ 1)), over_core(own_rows(o_par, me ^ 1))]
+        attn_out = out_proj(sources, o_tok, w_o, rows)
+
+        def blocks(where):
+            return jnp.stack([where, *toks]).astype(jnp.int32)
+
         d_w_o, *d_w = reserve(w_o.shape, w_q.shape, w_k.shape, w_v.shape)
-        for b, piece in zip(hbs, (dwo_own, dwo_par, over_core(dwo_own), over_core(dwo_par))):
+        sent = []
+        for b, o in ((hbs[0], o_own), (hbs[1], o_par)):
+            d_w_o, piece = out_weight_grad(blocks(b), o, gs, d_w_o)
+            sent.append(over_core(piece))
+        for b, piece in zip(hbs[2:], sent):
             d_w_o = lax.dynamic_update_slice_in_dim(d_w_o, piece, b * cq, 0)
 
-        dhs = []
         gr = []
         for t in range(kv_local):
             gr.append(attn_backward(qkv, d_o, o_t, lse, cos_t, sin_t, kv_local, t))
@@ -619,24 +750,17 @@
         def col(val):
             return val.reshape(1).astype(jnp.int32)
 
-        *d_w, piece = weight_grad(col(hbs[0]), h_all, gr, d_w)
+        *d_w, piece = weight_grad(blocks(hbs[0]), hs, gr, d_w)
         piece = over_core(piece)
         d_w = place(col(hbs[2]), piece, d_w)
+        gr_tok = [gr, gr_par, [], []]
         for t in range(kv_local):
-            gr_tok = [own_rows(gr[t], me), own_rows(gr_par[t], me),
-                      over_core(own_rows(gr[t], me ^ 1)), over_core(own_rows(gr_par[t], me ^ 1))]
-            parts = []
-            for b in hbs:
-                parts.append(lax.dynamic_slice_in_dim(w_q, b * cq + t * wide, wide, 1))
-                parts.append(lax.dynamic_slice_in_dim(w_k, b * ck + t * HEAD_DIM, HEAD_DIM, 1))
-                parts.append(lax.dynamic_slice_in_dim(w_v, b * ck + t * HEAD_DIM, HEAD_DIM, 1))
-            w_perm = jnp.concatenate(parts, axis=1)
-            dhs.append(mm(jnp.concatenate(gr_tok, axis=1), w_perm, ((1,), (1,))))
-            *d_w, piece = weight_grad(col(hbs[1] * kv_local + t), h_all, (gr_par[t],), d_w)
+            gr_tok[2].append(over_core(own_rows(gr[t], me ^ 1)))
+            gr_tok[3].append(over_core(own_rows(gr_par[t], me ^ 1)))
+            *d_w, piece = weight_grad(blocks(hbs[1] * kv_local + t), hs, (gr_par[t],), d_w)
             piece = over_core(piece)
             d_w = place(col(hbs[3] * kv_local + t), piece, d_w)
-
-        d_hid, d_lnw = ln_backward(dhs[0], dhs[1], hidden, ln_row)
+        d_hid, d_lnw = hidden_grad(sources, [val for pair in gr_tok for val in pair], w_q, w_k, w_v, hidden, ln_row, n_dev)
         d_lnw = d_lnw + over_core(d_lnw)
         d_lnw = d_lnw + over_chip(d_lnw)
         return (attn_out, d_hid, d_lnw.reshape(dim).astype(BF16), *d_w, d_w_o)

time: 1200 us -> 1300 us (1.083)
  waiting for transfers between devices: 377 us -> 533 us
  Pallas kernels: 568 us -> 701 us
  matrix products: 118 us -> 0 us
  local copies, waits for them, and re-layouts: 93 us -> 25.6 us
    ppermute x8 -> x7, waiting for transfers between devices: 377 us -> 533 us  [over_chip(): return lax.ppermute(val, 'sp', [(i, i ^ 2) for i in range(n_dev)])]
    dot_general x5 -> x0, matrix products: 118 us -> none  [the longest x4 92.9 us: mm(): lax.dot_general(lhs, rhs, (dims, ((), ())), preferred_element_type=F32)]
    pallas_call x13 -> x12, Pallas kernels: 143 us -> 247 us  [the longest x4 61 us: qkv_block(): pl.pallas_call(qkv_kernel, out_shape=jax.ShapeDtypeStruct((seq, cols), BF...]
    unnamed x37 -> x6, local copies, waits for them, and re-layouts: 40.2 us -> 0.01 us
    pallas_call x2 -> x4, Pallas kernels: 10.3 us -> 36.8 us  [ln_forward(): pl.pallas_call(ln_kernel, grid=(rows // blk,), in_specs=[pl.BlockSpec((bl...]
    dynamic_slice x1 -> x0, local copies, waits for them, and re-layouts: 14.6 us -> none  [layer(): lax.dynamic_slice_in_dim(w_o, b * cq, cq, 0)]
  transfers between devices with their start and end apart: 28 -> 25, of which waited for: 5 -> 6; matrix products, arithmetic and copies ran while one was open for 19% -> 3% of each run, Pallas kernels for 47% -> 35%
where the time goes in v4:
time: 1300 us; the launch traced here: 1290 us
  Pallas kernels  701 us (54%)
  waiting for transfers between devices  533 us (41%)
  local copies, waits for them, and re-layouts  25.6 us (2%)
  starting transfers between devices  14.4 us (1%)
    ppermute x7, waiting for transfers between devices, over_chip(): return lax.ppermute(val, 'sp', [(i, i ^ 2) for i in range(n_dev)])  533 us
    pallas_call x2, Pallas kernels, attn_backward(): pl.pallas_call(bwd_kernel, grid=(nq,), in_specs=[pl.BlockSpec((BQ, wide),...  190 us
    pallas_call x1, Pallas kernels, attn_forward(): pl.pallas_call(fwd_kernel, grid=(kv_local, nq), in_specs=[pl.BlockSpec((B...  103 us
    pallas_call x3, Pallas kernels, weight_grad(): pl.pallas_call(dw_kernel, out_shape=tuple((jax.ShapeDtypeStruct(b.shape,...  98.6 us
    pallas_call x4, Pallas kernels, qkv_block(): pl.pallas_call(qkv_kernel, out_shape=jax.ShapeDtypeStruct((seq, cols), BF...  61 us
    pallas_call x1, Pallas kernels, hidden_grad(): pl.pallas_call(dh_kernel, out_shape=(jax.ShapeDtypeStruct((rows, dim), BF...  58.8 us
    pallas_call x2, Pallas kernels, out_weight_grad(): pl.pallas_call(dwo_kernel, out_shape=(jax.ShapeDtypeStruct(buf.shape, BF1...  54.8 us
    pallas_call x4, Pallas kernels, do_block(): pl.pallas_call(do_kernel, out_shape=jax.ShapeDtypeStruct((seq, ce), BF16)...  40.7 us
  transfers between devices with their start and end apart: 25, of which 6 were waited for; matrix products, arithmetic and copies ran while one was open for 3% of the time, Pallas kernels for 35%

profile of v4, /device:TPU:0, one launch (start us, length us, event | category | flops | bytes accessed | tf_op | source)
XLA Modules:
  0.0 1287.3 jit_solution(4253264427970613585)
XLA Ops:
  0.6 3.3 collective-permute-start
  4.5 136.1 %collective-permute-done.x_ref = bf16[1024,3072]{1,0:T(8,128)(2,1)} collective-permute-done((bf16[1024,3072]{1,0:T(8,128)(2,1)}, bf16[1024,3072]{1,0:T(8,128)(2,1)}, u32[]{:S(2)}, u32[]{:S(2)}) %collective-permute-start) | collective-permute-done | bytes 6291488 | tf_op jit(solution)/shard_map/ppermute | solution.py:680
  140.6 2.0 collective-permute-start.3
  142.7 6.7 wo_t.1.wo_ref
  149.9 10.2 d_o.4.rest_0_
  160.7 113.9 %collective-permute-done.3 = s32[1024]{0:T(1024)S(1)} collective-permute-done((s32[1024]{0:T(1024)}, s32[1024]{0:T(1024)S(1)}, u32[]{:S(2)}, u32[]{:S(2)}) %collective-permute-start.3) | collective-permute-done | bytes 4128 | tf_op jit(solution)/shard_map/ppermute | solution.py:680
  276.6 0.7 stack.55.idx
  278.1 9.2 ln_fwd.7.h_ref.refs_0_
  287.3 9.4 fusion
  296.7 15.2 %qkv.4.rest_0_ = bf16[4096,1280]{1,0:T(8,128)(2,1)} custom-call(s32[2]{0:T(128)} %pad_add_fusion.3.idx, bf16[1024,3072]{1,0:T(8,128)(2,1)} %ln_fwd.7.h_ref.refs_0_, bf16[3072,3072]{1,0:T(8,128)(2,1)} %refs_8_.1, bf16[3072,1024]{1,0:T(8,128)(2,1)} %refs_9_.1, bf16[3072,1024]{1,0:T(8,128)(2,1)} %refs_10_.1, f32[4096,128]{1,0:T(8,128)} %get-tuple-element.76.cos_ref, ...), custom_call_target="tpu_custom_call" | custom-call | flops 8053063680 | bytes 16777216 | tf_op jit(solution)/shard_map/qkv/pallas_call | solution.py:99
  312.1 9.2 ln_fwd.5.h_ref.refs_1_
  321.4 9.2 ln_fwd.6.h_ref.refs_2_
  330.6 10.1 d_o.5.rest_0_
  340.7 10.3 d_o.6.rest_0_
  351.0 15.1 %qkv.5.rest_0_ = bf16[4096,1280]{1,0:T(8,128)(2,1)} custom-call(s32[2]{0:T(128)} %pad_add_fusion.2.idx, bf16[1024,3072]{1,0:T(8,128)(2,1)} %ln_fwd.6.h_ref.refs_2_, bf16[3072,3072]{1,0:T(8,128)(2,1)} %refs_8_.1, bf16[3072,1024]{1,0:T(8,128)(2,1)} %refs_9_.1, bf16[3072,1024]{1,0:T(8,128)(2,1)} %refs_10_.1, ...), custom_call_target="tpu_custom_call", output_to_operand_aliasing={{}: (7, {})} | custom-call | flops 8053063680 | bytes 16777216 | tf_op jit(solution)/shard_map/qkv/pallas_call | solution.py:99
  366.1 15.1 %qkv.6.rest_0_ = bf16[4096,1280]{1,0:T(8,128)(2,1)} custom-call(s32[2]{0:T(128)} %pad_add_fusion.1.idx, bf16[1024,3072]{1,0:T(8,128)(2,1)} %ln_fwd.5.h_ref.refs_1_, bf16[3072,3072]{1,0:T(8,128)(2,1)} %refs_8_.1, bf16[3072,1024]{1,0:T(8,128)(2,1)} %refs_9_.1, bf16[3072,1024]{1,0:T(8,128)(2,1)} %refs_10_.1, ...), custom_call_target="tpu_custom_call", output_to_operand_aliasing={{}: (7, {})} | custom-call | flops 8053063680 | bytes 16777216 | tf_op jit(solution)/shard_map/qkv/pallas_call | solution.py:99
  381.2 9.2 ln_fwd.4.h_ref.refs_3_
  390.4 15.5 %qkv.7.q_ref.k_ref.v_ref = bf16[4096,1280]{1,0:T(8,128)(2,1)} custom-call(s32[2]{0:T(128)} %pad_add_fusion.idx, bf16[1024,3072]{1,0:T(8,128)(2,1)} %ln_fwd.4.h_ref.refs_3_, bf16[3072,3072]{1,0:T(8,128)(2,1)} %refs_8_.1, bf16[3072,1024]{1,0:T(8,128)(2,1)} %refs_9_.1, bf16[3072,1024]{1,0:T(8,128)(2,1)} %refs_10_.1, ...), custom_call_target="tpu_custom_call", output_to_operand_aliasing={{}: (7, {})} | custom-call | flops 8053063680 | bytes 16777216 | tf_op jit(solution)/shard_map/qkv/pallas_call | solution.py:99
  405.9 102.9 %attn_fwd.1 = (bf16[4096,768]{1,0:T(8,128)(2,1)}, f32[2,16,128,768]{3,2,1,0:T(8,128)}, f32[2,16,1,768]{3,2,1,0:T(1,128)}) custom-call(bf16[4096,1280]{1,0:T(8,128)(2,1)} %qkv.7.q_ref.k_ref.v_ref, bf16[4096,1280]{1,0:T(8,128)(2,1)} %qkv.7.q_ref.k_ref.v_ref, bf16[4096,1280]{1,0:T(8,128)(2,1)} %qkv.7.q_ref.k_ref.v_ref), custom_call_target="tpu_custom_call" | custom-call | flops 51539607552 | bytes 25165824 | tf_op jit(solution)/shard_map/attn_fwd/pallas_call | solution.py:261
  508.8 10.1 d_o.7.do_ref
  518.9 94.8 %attn_bwd.3.refs_1_.refs_5_ = bf16[4096,640]{1,0:T(8,128)(2,1)} custom-call(bf16[4096,1280]{1,0:T(8,128)(2,1)} %qkv.7.q_ref.k_ref.v_ref, bf16[4096,1280]{1,0:T(8,128)(2,1)} %qkv.7.q_ref.k_ref.v_ref, bf16[4096,1280]{1,0:T(8,128)(2,1)} %qkv.7.q_ref.k_ref.v_ref, bf16[4096,768]{1,0:T(8,128)(2,1)} %d_o.7.do_ref, f32[2,16,128,768]{3,2,1,0:T(8,128)} %get-tuple-element.42.ot_ref, ...), custom_call_target="tpu_custom_call" | custom-call | flops 64424509440 | bytes 25165824 | tf_op jit(solution)/shard_map/attn_bwd/pallas_call | solution.py:375
  613.7 95.0 %attn_bwd.2.refs_0_.refs_4_ = bf16[4096,640]{1,0:T(8,128)(2,1)} custom-call(bf16[4096,1280]{1,0:T(8,128)(2,1)} %qkv.7.q_ref.k_ref.v_ref, bf16[4096,1280]{1,0:T(8,128)(2,1)} %qkv.7.q_ref.k_ref.v_ref, bf16[4096,1280]{1,0:T(8,128)(2,1)} %qkv.7.q_ref.k_ref.v_ref, bf16[4096,768]{1,0:T(8,128)(2,1)} %d_o.7.do_ref, f32[2,16,128,768]{3,2,1,0:T(8,128)} %get-tuple-element.42.ot_ref, ...), custom_call_target="tpu_custom_call" | custom-call | flops 64424509440 | bytes 25165824 | tf_op jit(solution)/shard_map/attn_bwd/pallas_call | solution.py:375
  708.7 42.8 %weight_grad.3 = (bf16[3072,3072]{1,0:T(8,128)(2,1)}, bf16[3072,1024]{1,0:T(8,128)(2,1)}, bf16[3072,1024]{1,0:T(8,128)(2,1)}, bf16[3072,1280]{1,0:T(8,128)(2,1)}) custom-call(s32[5]{0:T(128)} %stack.55.idx, bf16[1024,3072]{1,0:T(8,128)(2,1)} %ln_fwd.7.h_ref.refs_0_, ...), custom_call_target="tpu_custom_call", output_to_operand_aliasing={{0}: (7, {}), {1}: (8, {}), {2}: (9, {})} | custom-call | flops 32212254720 | bytes 51380224 | tf_op jit(solution)/shard_map/weight_grad/pallas_call | solution.py:597
  751.7 1.7 collective-permute-start.13
  753.7 1.7 collective-permute-start.6
  755.4 0.7 stack.56.idx
  757.9 2.5 constant_dynamic-slice_fusion.2
  760.4 1.4 constant_dynamic-slice_fusion.3
  761.8 1.5 constant_dynamic-slice_fusion.5
  763.3 27.5 %out_weight_grad.2 = (bf16[3072,3072]{1,0:T(8,128)(2,1)}, bf16[768,3072]{1,0:T(8,128)(2,1)}) custom-call(s32[5]{0:T(128)} %stack.55.idx, bf16[4096,768]{1,0:T(8,128)(2,1)} %get-tuple-element.41.refs_0_.o_ref, bf16[1024,3072]{1,0:T(8,128)(2,1)} %refs_0_.3, bf16[1024,3072]{1,0:T(8,128)(2,1)} %collective-permute-done.9.g_ref.refs_1_, ...), custom_call_target="tpu_custom_call", output_to_operand_aliasing={{0}: (6, {})} | custom-call | flops 19327352832 | bytes 40894464 | tf_op jit(solution)/shard_map/out_weight_grad/pallas_call | solution.py:629
  790.8 77.1 %collective-permute-done.13.refs_3_.refs_4_ = bf16[4096,640]{1,0:T(8,128)(2,1)} collective-permute-done((bf16[4096,640]{1,0:T(8,128)(2,1)}, bf16[4096,640]{1,0:T(8,128)(2,1)}, u32[]{:S(2)}, u32[]{:S(2)}) %collective-permute-start.13) | collective-permute-done | bytes 5242912 | tf_op jit(solution)/shard_map/ppermute | solution.py:680
  867.9 2.5 constant_dynamic-slice_fusion
  870.4 109.8 %collective-permute-done.12.refs_2_.refs_4_ = bf16[4096,640]{1,0:T(8,128)(2,1)} collective-permute-done((bf16[4096,640]{1,0:T(8,128)(2,1)}, bf16[4096,640]{1,0:T(8,128)(2,1)}, u32[]{:S(2)}, u32[]{:S(2)}) %collective-permute-start.12) | collective-permute-done | bytes 5242912 | tf_op jit(solution)/shard_map/ppermute | solution.py:680
  980.3 2.5 constant_dynamic-slice_fusion.1
  983.3 7.7 place.3
  991.0 27.9 %weight_grad.4 = (bf16[3072,3072]{1,0:T(8,128)(2,1)}, bf16[3072,1024]{1,0:T(8,128)(2,1)}, bf16[3072,1024]{1,0:T(8,128)(2,1)}, bf16[3072,640]{1,0:T(8,128)(2,1)}) custom-call(s32[5]{0:T(128)} %stack.54.idx, bf16[1024,3072]{1,0:T(8,128)(2,1)} %ln_fwd.7.h_ref.refs_0_, ...), custom_call_target="tpu_custom_call", output_to_operand_aliasing={{0}: (6, {}), {1}: (7, {}), {2}: (8, {})} | custom-call | flops 16106127360 | bytes 38273024 | tf_op jit(solution)/shard_map/weight_grad/pallas_call | solution.py:597
  1018.9 95.6 %collective-permute-done.6.refs_1_.o_ref = bf16[4096,768]{1,0:T(8,128)(2,1)} collective-permute-done((bf16[4096,768]{1,0:T(8,128)(2,1)}, bf16[4096,768]{1,0:T(8,128)(2,1)}, u32[]{:S(2)}, u32[]{:S(2)}) %collective-permute-start.6) | collective-permute-done | bytes 6291488 | tf_op jit(solution)/shard_map/ppermute | solution.py:680
  1114.4 27.3 %out_weight_grad.3 = (bf16[3072,3072]{1,0:T(8,128)(2,1)}, bf16[768,3072]{1,0:T(8,128)(2,1)}) custom-call(s32[5]{0:T(128)} %stack.56.idx, bf16[4096,768]{1,0:T(8,128)(2,1)} %collective-permute-done.6.refs_1_.o_ref, bf16[1024,3072]{1,0:T(8,128)(2,1)} %refs_0_.3, ...), custom_call_target="tpu_custom_call", output_to_operand_aliasing={{0}: (6, {})} | custom-call | flops 19327352832 | bytes 40894464 | tf_op jit(solution)/shard_map/out_weight_grad/pallas_call | solution.py:629
  1142.8 58.8 %hidden_grad.1 = (bf16[1024,3072]{1,0:T(8,128)(2,1)}, f32[1,3072]{1,0:T(1,128)}) custom-call(s32[5]{0:T(128)} %stack.43.idx, bf16[4096,640]{1,0:T(8,128)(2,1)} %attn_bwd.2.refs_0_.refs_4_, bf16[4096,640]{1,0:T(8,128)(2,1)} %attn_bwd.3.refs_1_.refs_5_, bf16[4096,640]{1,0:T(8,128)(2,1)} %collective-permute-done.12.refs_2_.refs_4_, ...), custom_call_target="tpu_custom_call" | custom-call | flops 32212254720 | bytes 54525952 | tf_op jit(solution)/shard_map/hidden_grad/pallas_call | solution.py:533
  1201.6 5.7 place.4
  1207.4 28.0 %weight_grad.5 = (bf16[3072,3072]{1,0:T(8,128)(2,1)}, bf16[3072,1024]{1,0:T(8,128)(2,1)}, bf16[3072,1024]{1,0:T(8,128)(2,1)}, bf16[3072,640]{1,0:T(8,128)(2,1)}) custom-call(s32[5]{0:T(128)} %stack.52.idx, bf16[1024,3072]{1,0:T(8,128)(2,1)} %ln_fwd.7.h_ref.refs_0_, ...), custom_call_target="tpu_custom_call", output_to_operand_aliasing={{0}: (6, {}), {1}: (7, {}), {2}: (8, {})} | custom-call | flops 16106127360 | bytes 38273024 | tf_op jit(solution)/shard_map/weight_grad/pallas_call | solution.py:597
  1235.8 1.5 constant_dynamic-slice_fusion.4
  1237.4 1.9 collective-permute-start.19
  1239.3 4.8 constant_dynamic-update-slice_fusion.1
  1244.2 0.6 convert_reduce_fusion
  1244.8 31.4 %out_proj.1 = bf16[1024,3072]{1,0:T(8,128)(2,1)} custom-call(s32[5]{0:T(128)} %stack.43.idx, bf16[4096,768]{1,0:T(8,128)(2,1)} %get-tuple-element.41.refs_0_.o_ref, bf16[4096,768]{1,0:T(8,128)(2,1)} %collective-permute-done.6.refs_1_.o_ref, bf16[1024,768]{1,0:T(8,128)(2,1)} %collective-permute-done.7.refs_2_, ...), custom_call_target="tpu_custom_call" | custom-call | flops 19327352832 | bytes 31457280 | tf_op jit(solution)/shard_map/out_proj/pallas_call | solution.py:447
  1276.2 4.8 constant_dynamic-update-slice_fusion
  1281.1 5.7 place.5
  (62 shorter events, 9.4 us)
Async XLA Ops:
  0.6 140.0 %collective-permute-start = (bf16[1024,3072]{1,0:T(8,128)(2,1)}, bf16[1024,3072]{1,0:T(8,128)(2,1)}, u32[]{:S(2)}, u32[]{:S(2)}) collective-permute-start(bf16[1024,3072]{1,0:T(8,128)(2,1)} %refs_11_.1), channel_id=1, source_target_pairs={{0,2},{1,3},{2,0},{3,1},{4,6},{5,7},{6,4},{7,5}} | collective-permute-start | bytes 18874376 | tf_op jit(solution)/shard_map/ppermute | solution.py:680
  4.0 307.9 %collective-permute-start.9 = (bf16[1024,3072]{1,0:T(8,128)(2,1)}, bf16[1024,3072]{1,0:T(8,128)(2,1)}, u32[]{:S(2)}, u32[]{:S(2)}) collective-permute-start(bf16[1024,3072]{1,0:T(8,128)(2,1)} %refs_0_.3), channel_id=1, source_target_pairs={{0,2},{1,3},{2,0},{3,1},{4,6},{5,7},{6,4},{7,5}} | collective-permute-start | bytes 18874376 | tf_op jit(solution)/shard_map/ppermute | solution.py:680
  4.0 317.4 %collective-permute-start.5 = (bf16[1024,3072]{1,0:T(8,128)(2,1)}, bf16[1024,3072]{1,0:T(8,128)(2,1)}, u32[]{:S(2)}, u32[]{:S(2)}) collective-permute-start(bf16[1024,3072]{1,0:T(8,128)(2,1)} %refs_11_.1), channel_id=1, source_target_pairs={{0,1},{1,0},{2,3},{3,2},{4,5},{5,4},{6,7},{7,6}} | collective-permute-start | bytes 18874376 | tf_op jit(solution)/shard_map/ppermute | solution.py:683
  4.0 326.6 %collective-permute-start.11 = (bf16[1024,3072]{1,0:T(8,128)(2,1)}, bf16[1024,3072]{1,0:T(8,128)(2,1)}, u32[]{:S(2)}, u32[]{:S(2)}) collective-permute-start(bf16[1024,3072]{1,0:T(8,128)(2,1)} %refs_0_.3), channel_id=1, source_target_pairs={{0,1},{1,0},{2,3},{3,2},{4,5},{5,4},{6,7},{7,6}} | collective-permute-start | bytes 18874376 | tf_op jit(solution)/shard_map/ppermute | solution.py:683
  140.6 240.6 %collective-permute-start.1 = (bf16[1024,3072]{1,0:T(8,128)(2,1)}, bf16[1024,3072]{1,0:T(8,128)(2,1)}, u32[]{:S(2)}, u32[]{:S(2)}) collective-permute-start(bf16[1024,3072]{1,0:T(8,128)(2,1)} %collective-permute-done.x_ref), channel_id=1, source_target_pairs={{0,1},{1,0},{2,3},{3,2},{4,5},{5,4},{6,7},{7,6}} | collective-permute-start | bytes 18874376 | tf_op jit(solution)/shard_map/ppermute | solution.py:683
  140.6 134.0 %collective-permute-start.3 = (s32[1024]{0:T(1024)}, s32[1024]{0:T(1024)S(1)}, u32[]{:S(2)}, u32[]{:S(2)}) collective-permute-start(s32[1024]{0:T(1024)} %param.9), channel_id=1, source_target_pairs={{0,2},{1,3},{2,0},{3,1},{4,6},{5,7},{6,4},{7,5}} | collective-permute-start | bytes 12296 | tf_op jit(solution)/shard_map/ppermute | solution.py:680
  149.9 124.8 %copy-start.2 = (s32[1024]{0:T(1024)S(1)}, s32[1024]{0:T(1024)}, u32[]{:S(2)}) copy-start(s32[1024]{0:T(1024)} %param.9) | copy-start | bytes 12292
  149.9 127.6 %copy-start.1 = (bf16[3072]{0:T(1024)(128)(2,1)S(1)}, bf16[3072]{0:T(1024)(128)(2,1)}, u32[]{:S(2)}) copy-start(bf16[3072]{0:T(1024)(128)(2,1)} %param.11) | copy-start | bytes 18436
  274.7 1.2 collective-permute-start.2
  275.8 11.4 collective-permute-start.4
  311.8 196.9 %collective-permute-start.10 = (bf16[1024,3072]{1,0:T(8,128)(2,1)}, bf16[1024,3072]{1,0:T(8,128)(2,1)}, u32[]{:S(2)}, u32[]{:S(2)}) collective-permute-start(bf16[1024,3072]{1,0:T(8,128)(2,1)} %collective-permute-done.9.g_ref.refs_1_), channel_id=1, source_target_pairs={{0,1},{1,0},{2,3},{3,2},{4,5},{5,4},{6,7},{7,6}} | collective-permute-start | bytes 18874376 | tf_op jit(solution)/shard_map/ppermute | solution.py:683
  751.5 231.3 %collective-permute-start.20 = (bf16[3072,1280]{1,0:T(8,128)(2,1)}, bf16[3072,1280]{1,0:T(8,128)(2,1)}, u32[]{:S(2)}, u32[]{:S(2)}) collective-permute-start(bf16[3072,1280]{1,0:T(8,128)(2,1)} %get-tuple-element.49), channel_id=1, source_target_pairs={{0,1},{1,0},{2,3},{3,2},{4,5},{5,4},{6,7},{7,6}} | collective-permute-start | bytes 23592968 | tf_op jit(solution)/shard_map/ppermute | solution.py:683
  751.7 116.2 %collective-permute-start.13 = (bf16[4096,640]{1,0:T(8,128)(2,1)}, bf16[4096,640]{1,0:T(8,128)(2,1)}, u32[]{:S(2)}, u32[]{:S(2)}) collective-permute-start(bf16[4096,640]{1,0:T(8,128)(2,1)} %attn_bwd.3.refs_1_.refs_5_), channel_id=1, source_target_pairs={{0,2},{1,3},{2,0},{3,1},{4,6},{5,7},{6,4},{7,5}} | collective-permute-start | bytes 15728648 | tf_op jit(solution)/shard_map/ppermute | solution.py:680
  753.4 226.9 %collective-permute-start.12 = (bf16[4096,640]{1,0:T(8,128)(2,1)}, bf16[4096,640]{1,0:T(8,128)(2,1)}, u32[]{:S(2)}, u32[]{:S(2)}) collective-permute-start(bf16[4096,640]{1,0:T(8,128)(2,1)} %attn_bwd.2.refs_0_.refs_4_), channel_id=1, source_target_pairs={{0,2},{1,3},{2,0},{3,1},{4,6},{5,7},{6,4},{7,5}} | collective-permute-start | bytes 15728648 | tf_op jit(solution)/shard_map/ppermute | solution.py:680
  753.7 360.7 %collective-permute-start.6 = (bf16[4096,768]{1,0:T(8,128)(2,1)}, bf16[4096,768]{1,0:T(8,128)(2,1)}, u32[]{:S(2)}, u32[]{:S(2)}) collective-permute-start(bf16[4096,768]{1,0:T(8,128)(2,1)} %get-tuple-element.41.refs_0_.o_ref), channel_id=1, source_target_pairs={{0,2},{1,3},{2,0},{3,1},{4,6},{5,7},{6,4},{7,5}} | collective-permute-start | bytes 18874376 | tf_op jit(solution)/shard_map/ppermute | solution.py:680
  760.4 381.4 %collective-permute-start.15 = (bf16[1024,640]{1,0:T(8,128)(2,1)}, bf16[1024,640]{1,0:T(8,128)(2,1)}, u32[]{:S(2)}, u32[]{:S(2)}) collective-permute-start(bf16[1024,640]{1,0:T(8,128)(2,1)} %constant_dynamic-slice_fusion.2), channel_id=1, source_target_pairs={{0,1},{1,0},{2,3},{3,2},{4,5},{5,4},{6,7},{7,6}} | collective-permute-start | bytes 3932168 | tf_op jit(solution)/shard_map/ppermute | solution.py:683
  867.9 274.3 %collective-permute-start.14 = (bf16[1024,640]{1,0:T(8,128)(2,1)S(1)}, bf16[1024,640]{1,0:T(8,128)(2,1)}, u32[]{:S(2)}, u32[]{:S(2)}) collective-permute-start(bf16[1024,640]{1,0:T(8,128)(2,1)S(1)} %constant_dynamic-slice_fusion.3), channel_id=1, source_target_pairs={{0,1},{1,0},{2,3},{3,2},{4,5},{5,4},{6,7},{7,6}} | collective-permute-start | bytes 3932168 | tf_op jit(solution)/shard_map/ppermute | solution.py:683
  980.3 162.0 %collective-permute-start.17 = (bf16[1024,640]{1,0:T(8,128)(2,1)}, bf16[1024,640]{1,0:T(8,128)(2,1)}, u32[]{:S(2)}, u32[]{:S(2)}) collective-permute-start(bf16[1024,640]{1,0:T(8,128)(2,1)} %constant_dynamic-slice_fusion), channel_id=1, source_target_pairs={{0,1},{1,0},{2,3},{3,2},{4,5},{5,4},{6,7},{7,6}} | collective-permute-start | bytes 3932168 | tf_op jit(solution)/shard_map/ppermute | solution.py:683
  982.8 160.0 %collective-permute-start.16 = (bf16[1024,640]{1,0:T(8,128)(2,1)}, bf16[1024,640]{1,0:T(8,128)(2,1)}, u32[]{:S(2)}, u32[]{:S(2)}) collective-permute-start(bf16[1024,640]{1,0:T(8,128)(2,1)} %constant_dynamic-slice_fusion.1), channel_id=1, source_target_pairs={{0,1},{1,0},{2,3},{3,2},{4,5},{5,4},{6,7},{7,6}} | collective-permute-start | bytes 3932168 | tf_op jit(solution)/shard_map/ppermute | solution.py:683
  1114.4 87.2 %collective-permute-start.21 = (bf16[3072,640]{1,0:T(8,128)(2,1)}, bf16[3072,640]{1,0:T(8,128)(2,1)}, u32[]{:S(2)}, u32[]{:S(2)}) collective-permute-start(bf16[3072,640]{1,0:T(8,128)(2,1)} %get-tuple-element.56), channel_id=1, source_target_pairs={{0,1},{1,0},{2,3},{3,2},{4,5},{5,4},{6,7},{7,6}} | collective-permute-start | bytes 11796488 | tf_op jit(solution)/shard_map/ppermute | solution.py:683
  1141.7 95.7 %collective-permute-start.23 = (bf16[768,3072]{1,0:T(8,128)(2,1)}, bf16[768,3072]{1,0:T(8,128)(2,1)}, u32[]{:S(2)}, u32[]{:S(2)}) collective-permute-start(bf16[768,3072]{1,0:T(8,128)(2,1)} %get-tuple-element.73), channel_id=1, source_target_pairs={{0,1},{1,0},{2,3},{3,2},{4,5},{5,4},{6,7},{7,6}} | collective-permute-start | bytes 14155784 | tf_op jit(solution)/shard_map/ppermute | solution.py:683
  1142.3 102.6 %collective-permute-start.7 = (bf16[1024,768]{1,0:T(8,128)(2,1)S(1)}, bf16[1024,768]{1,0:T(8,128)(2,1)}, u32[]{:S(2)}, u32[]{:S(2)}) collective-permute-start(bf16[1024,768]{1,0:T(8,128)(2,1)S(1)} %constant_dynamic-slice_fusion.5), channel_id=1, source_target_pairs={{0,1},{1,0},{2,3},{3,2},{4,5},{5,4},{6,7},{7,6}} | collective-permute-start | bytes 4718600 | tf_op jit(solution)/shard_map/ppermute | solution.py:683
  1142.3 133.9 %collective-permute-start.24 = (bf16[768,3072]{1,0:T(8,128)(2,1)}, bf16[768,3072]{1,0:T(8,128)(2,1)}, u32[]{:S(2)}, u32[]{:S(2)}) collective-permute-start(bf16[768,3072]{1,0:T(8,128)(2,1)} %get-tuple-element.74), channel_id=1, source_target_pairs={{0,1},{1,0},{2,3},{3,2},{4,5},{5,4},{6,7},{7,6}} | collective-permute-start | bytes 14155784 | tf_op jit(solution)/shard_map/ppermute | solution.py:683
  1201.6 35.8 %collective-permute-start.18 = (f32[1,3072]{1,0:T(1,128)}, f32[1,3072]{1,0:T(1,128)S(1)}, u32[]{:S(2)}, u32[]{:S(2)}) collective-permute-start(f32[1,3072]{1,0:T(1,128)} %get-tuple-element.45), channel_id=1, source_target_pairs={{0,1},{1,0},{2,3},{3,2},{4,5},{5,4},{6,7},{7,6}} | collective-permute-start | bytes 36872 | tf_op jit(solution)/shard_map/ppermute | solution.py:683
  1207.4 30.1 %copy-start = (f32[1,3072]{1,0:T(1,128)S(1)}, f32[1,3072]{1,0:T(1,128)}, u32[]{:S(2)}) copy-start(f32[1,3072]{1,0:T(1,128)} %get-tuple-element.45) | copy-start | bytes 36868
  1235.4 45.7 %collective-permute-start.22 = (bf16[3072,640]{1,0:T(8,128)(2,1)}, bf16[3072,640]{1,0:T(8,128)(2,1)}, u32[]{:S(2)}, u32[]{:S(2)}) collective-permute-start(bf16[3072,640]{1,0:T(8,128)(2,1)} %get-tuple-element.63), channel_id=1, source_target_pairs={{0,1},{1,0},{2,3},{3,2},{4,5},{5,4},{6,7},{7,6}} | collective-permute-start | bytes 11796488 | tf_op jit(solution)/shard_map/ppermute | solution.py:683
  1237.3 7.5 collective-permute-start.8
  1237.4 6.7 collective-permute-start.19

commit v5 on v4

--- a/solution.py
+++ b/solution.py
@@ -35,77 +35,77 @@
     return val * cos_t + swapped * sin_t
 
 
-def ln_kernel(x_ref, lnw_ref, h_ref):
-    xf = x_ref[...].astype(F32)
-    mean = jnp.mean(xf, axis=-1, keepdims=True)
-    cen = xf - mean
-    var = jnp.mean(cen * cen, axis=-1, keepdims=True)
-    h_ref[...] = (cen * lax.rsqrt(var + LN_EPS) * lnw_ref[...].astype(F32)).astype(BF16)
-
-
-def ln_forward(x, ln_w):
-    rows, dim = x.shape
-    blk = 128
-    return pl.pallas_call(
-        ln_kernel,
-        grid=(rows // blk,),
-        in_specs=[pl.BlockSpec((blk, dim), lambda i: (i, 0)), pl.BlockSpec((1, dim), lambda i: (0, 0))],
-        out_specs=pl.BlockSpec((blk, dim), lambda i: (i, 0)),
-        out_shape=jax.ShapeDtypeStruct((rows, dim), BF16),
-        compiler_params=pltpu.CompilerParams(dimension_semantics=("arbitrary",)),
-        cost_estimate=cost(10 * rows * dim, 4 * rows * dim),
-        name="ln_fwd",
-    )(x, ln_w)
-
-
-def qkv_kernel(idx, h_ref, wq_ref, wk_ref, wv_ref, cos_ref, sin_ref, *rest):
-    qkv_ref = rest[-1]
-    h = h_ref[...]
-    cos_t = cos_ref[...]
-    sin_t = sin_ref[...]
+def pick(pair, sc):
+    for n, ref in enumerate(pair):
+        @pl.when(pl.program_id(0) == n)
+        def _():
+            sc[...] = ref[...]
+
+
+def pair_specs(shape, per):
+    return [pl.BlockSpec(shape, lambda p, i, ix: (jnp.where(p == 0, i, per - 1), 0)),
+            pl.BlockSpec(shape, lambda p, i, ix: (jnp.where(p == 1, i, 0), 0))]
+
+
+def qkv_kernel(idx, xa_ref, xb_ref, lnw_ref, wq_ref, wk_ref, wv_ref, cos_ref, sin_ref, *rest):
+    h_ref, qkv_ref, x_sc = rest[-3:]
+    pick((xa_ref, xb_ref), x_sc)
+    weight = lnw_ref[...].astype(F32)
     nq = wq_ref.shape[1]
     nk = wk_ref.shape[1]
     step = 2 * HEAD_DIM
-    for start in range(0, nq + nk, step):
-        w = wq_ref[:, start:start + step] if start < nq else wk_ref[:, start - nq:start - nq + step]
-        val = mm(h, w, ((1,), (0,)))
-        for n in range(2):
-            sl = slice(n * HEAD_DIM, (n + 1) * HEAD_DIM)
-            qkv_ref[:, start + n * HEAD_DIM:start + (n + 1) * HEAD_DIM] = rotate(val[:, sl], cos_t, sin_t).astype(BF16)
-    qkv_ref[:, nq + nk:] = mm(h, wv_ref[...], ((1,), (0,))).astype(BF16)
-
-
-def qkv_block(idx, h, w_q, w_k, w_v, cos_t, sin_t, seq, n_dev, prev):
-    rows, dim = h.shape
+    for sub in range(ROWS // BQ):
+        rows = slice(sub * BQ, (sub + 1) * BQ)
+        xf = x_sc[rows, :].astype(F32)
+        mean = jnp.mean(xf, axis=-1, keepdims=True)
+        cen = xf - mean
+        var = jnp.mean(cen * cen, axis=-1, keepdims=True)
+        h = (cen * lax.rsqrt(var + LN_EPS) * weight).astype(BF16)
+        h_ref[rows, :] = h
+        cos_t = cos_ref[rows, :]
+        sin_t = sin_ref[rows, :]
+        for start in range(0, nq + nk, step):
+            w = wq_ref[:, start:start + step] if start < nq else wk_ref[:, start - nq:start - nq + step]
+            val = mm(h, w, ((1,), (0,)))
+            for n in range(2):
+                at = start + n * HEAD_DIM
+                part = val[:, n * HEAD_DIM:(n + 1) * HEAD_DIM]
+                qkv_ref[rows, at:at + HEAD_DIM] = rotate(part, cos_t, sin_t).astype(BF16)
+        qkv_ref[rows, nq + nk:] = mm(h, wv_ref[...], ((1,), (0,))).astype(BF16)
+
+
+def qkv_blocks(idx, xs, ln_w, w_q, w_k, w_v, cos_t, sin_t, seq, n_dev, prev):
+    rows, dim = xs[0].shape
     cq, ck = w_q.shape[1] // n_dev, w_k.shape[1] // n_dev
     per = rows // ROWS
-    head = lambda i, ix: (0, ix[0])
-    here = lambda i, ix: (ix[1] * per + i, 0)
-    in_specs = [
-        pl.BlockSpec((ROWS, dim), lambda i, ix: (i, 0)),
+    head = lambda p, i, ix: (0, ix[0])
+    here = lambda p, i, ix: (ix[1 + p] * per + i, 0)
+    in_specs = pair_specs((ROWS, dim), per) + [
+        pl.BlockSpec((1, dim), lambda p, i, ix: (0, 0)),
         pl.BlockSpec((dim, cq), head),
         pl.BlockSpec((dim, ck), head),
         pl.BlockSpec((dim, ck), head),
         pl.BlockSpec((ROWS, HEAD_DIM), here),
         pl.BlockSpec((ROWS, HEAD_DIM), here),
     ]
-    args = [idx, h, w_q, w_k, w_v, cos_t, sin_t]
+    args = [idx, *xs, ln_w, w_q, w_k, w_v, cos_t, sin_t]
     aliases = {}
     if prev is not None:
         in_specs.append(pl.BlockSpec(memory_space=pl.ANY))
         args.append(prev)
-        aliases = {7: 0}
+        aliases = {9: 1}
     cols = cq + 2 * ck
     return pl.pallas_call(
         qkv_kernel,
-        out_shape=jax.ShapeDtypeStruct((seq, cols), BF16),
+        out_shape=(jax.ShapeDtypeStruct((2 * rows, dim), BF16), jax.ShapeDtypeStruct((seq, cols), BF16)),
         grid_spec=pltpu.PrefetchScalarGridSpec(
-            num_scalar_prefetch=1, grid=(per,), in_specs=in_specs,
-            out_specs=pl.BlockSpec((ROWS, cols), here)),
+            num_scalar_prefetch=1, grid=(2, per), in_specs=in_specs,
+            out_specs=(pl.BlockSpec((ROWS, dim), lambda p, i, ix: (p * per + i, 0)), pl.BlockSpec((ROWS, cols), here)),
+            scratch_shapes=[pltpu.VMEM((ROWS, dim), BF16)]),
         input_output_aliases=aliases,
-        compiler_params=pltpu.CompilerParams(dimension_semantics=("arbitrary",), vmem_limit_bytes=VMEM_BYTES),
-        cost_estimate=cost(2 * rows * dim * cols, 2 * (rows * dim + dim * cols + rows * cols)),
-        name="qkv",
+        compiler_params=pltpu.CompilerParams(dimension_semantics=("arbitrary", "arbitrary"), vmem_limit_bytes=VMEM_BYTES),
+        cost_estimate=cost(4 * rows * dim * cols, 2 * (4 * rows * dim + dim * cols + 2 * rows * cols)),
+        name="ln_qkv",
     )(*args)
 
 
@@ -129,35 +129,33 @@
     )(idx, w_o)
 
 
-def do_kernel(idx, g_ref, wo_ref, *rest):
-    do_ref = rest[-1]
-    do_ref[...] = mm(g_ref[...], wo_ref[...], ((1,), (0,))).astype(BF16)
-
-
-def do_block(idx, g, wo_t, seq, prev):
-    rows, dim = g.shape
+def do_kernel(idx, ga_ref, gb_ref, wo_ref, *rest):
+    do_ref, g_sc = rest[-2:]
+    pick((ga_ref, gb_ref), g_sc)
+    do_ref[...] = mm(g_sc[...], wo_ref[...], ((1,), (0,))).astype(BF16)
+
+
+def do_blocks(idx, gs, wo_t, seq, prev):
+    rows, dim = gs[0].shape
     ce = wo_t.shape[1]
-    per = rows // ROWS
-    here = lambda i, ix: (ix[1] * per + i, 0)
-    in_specs = [
-        pl.BlockSpec((ROWS, dim), lambda i, ix: (i, 0)),
-        pl.BlockSpec((dim, ce), lambda i, ix: (0, 0)),
-    ]
-    args = [idx, g, wo_t]
+    per = rows // BQ
+    in_specs = pair_specs((BQ, dim), per) + [pl.BlockSpec((dim, ce), lambda p, i, ix: (0, 0))]
+    args = [idx, *gs, wo_t]
     aliases = {}
     if prev is not None:
         in_specs.append(pl.BlockSpec(memory_space=pl.ANY))
         args.append(prev)
-        aliases = {3: 0}
+        aliases = {4: 0}
     return pl.pallas_call(
         do_kernel,
         out_shape=jax.ShapeDtypeStruct((seq, ce), BF16),
         grid_spec=pltpu.PrefetchScalarGridSpec(
-            num_scalar_prefetch=1, grid=(per,), in_specs=in_specs,
-            out_specs=pl.BlockSpec((ROWS, ce), here)),
+            num_scalar_prefetch=1, grid=(2, per), in_specs=in_specs,
+            out_specs=pl.BlockSpec((BQ, ce), lambda p, i, ix: (ix[1 + p] * per + i, 0)),
+            scratch_shapes=[pltpu.VMEM((BQ, dim), BF16)]),
         input_output_aliases=aliases,
-        compiler_params=pltpu.CompilerParams(dimension_semantics=("arbitrary",), vmem_limit_bytes=VMEM_BYTES),
-        cost_estimate=cost(2 * rows * dim * ce, 2 * (rows * dim + dim * ce + rows * ce)),
+        compiler_params=pltpu.CompilerParams(dimension_semantics=("arbitrary", "arbitrary"), vmem_limit_bytes=VMEM_BYTES),
+        cost_estimate=cost(4 * rows * dim * ce, 2 * (2 * rows * dim + dim * ce + 2 * rows * ce)),
         name="d_o",
     )(*args)
 
@@ -416,19 +414,38 @@
     lax.fori_loop(0, acc_sc.shape[1] // N_TILE, tile, 0)
 
 
-def out_kernel(idx, *refs):
-    pieces, (w_ref, out_ref, cur_sc, acc_sc) = refs[:4], refs[4:]
-    src = pl.program_id(0)
-    for n, piece in enumerate(pieces):
+def fetch_ahead(src, copies):
+    @pl.when(src == 0)
+    def _():
+        for c in copies(0):
+            c.start()
+
+    for n in range(4):
         @pl.when(src == n)
         def _():
-            cur_sc[...] = piece[...]
+            if n < 3:
+                for c in copies(n + 1):
+                    c.start()
+            for c in copies(n):
+                c.wait()
+
+
+def out_kernel(idx, *refs):
+    pieces, (w_ref, out_ref, cur_sc, acc_sc, sem) = refs[:4], refs[4:]
+    src = pl.program_id(0)
+    rows = cur_sc.shape[1]
+
+    def copies(n):
+        at = pl.ds(pl.multiple_of(idx[0] * rows, rows) if n == 0 else pl.multiple_of(idx[0] % 2 * rows, rows) if n == 1 else 0, rows)
+        return [pltpu.make_async_copy(pieces[n].at[at, :], cur_sc.at[n % 2], sem.at[n % 2])]
+
+    fetch_ahead(src, copies)
 
     @pl.when(src == 0)
     def _():
         acc_sc[...] = jnp.zeros_like(acc_sc)
 
-    accumulate(acc_sc, lambda cols: mm(cur_sc[...], w_ref[:, cols], ((1,), (0,))))
+    accumulate(acc_sc, lambda cols: mm(cur_sc[src % 2], w_ref[:, cols], ((1,), (0,))))
 
     @pl.when(src == 3)
     def _():
@@ -442,16 +459,14 @@
 def out_proj(idx, pieces, w_o, rows):
     wide = pieces[0].shape[1]
     dim = w_o.shape[1]
-    mine = single((rows, wide), lambda s, ix: (ix[0], 0))
-    sent = single((rows, wide), lambda s, ix: (0, 0))
     return pl.pallas_call(
         out_kernel,
         out_shape=jax.ShapeDtypeStruct((rows, dim), BF16),
         grid_spec=pltpu.PrefetchScalarGridSpec(
             num_scalar_prefetch=1, grid=(4,),
-            in_specs=[mine, mine, sent, sent, pl.BlockSpec((wide, dim), lambda s, ix: (ix[1 + s], 0))],
+            in_specs=[pl.BlockSpec(memory_space=pl.ANY)] * 4 + [pl.BlockSpec((wide, dim), lambda s, ix: (ix[1 + s], 0))],
             out_specs=pl.BlockSpec((rows, dim), lambda s, ix: (0, 0)),
-            scratch_shapes=[pltpu.VMEM((rows, wide), BF16), pltpu.VMEM((rows, dim), F32)]),
+            scratch_shapes=[pltpu.VMEM((2, rows, wide), BF16), pltpu.VMEM((rows, dim), F32), pltpu.SemaphoreType.DMA((2,))]),
         compiler_params=pltpu.CompilerParams(dimension_semantics=("arbitrary",), vmem_limit_bytes=VMEM_BYTES),
         cost_estimate=cost(8 * rows * dim * wide, 2 * (5 * rows * dim)),
         name="out_proj",
@@ -460,31 +475,40 @@
 
 def dh_kernel(idx, *refs):
     pieces = refs[:8]
-    wq_ref, wk_ref, wv_ref, x_ref, lnw_ref, dx_ref, dw_ref, cur_sc, acc_sc, dx_sc, sem = refs[8:]
+    wq_ref, wk_ref, wv_ref, x_hbm, lnw_ref, dx_ref, dw_ref, cur_sc, acc_sc, x_ref, dx_sc, sem, piece_sem, x_sem = refs[8:]
     src = pl.program_id(0)
     wide = wq_ref.shape[1]
     each = wide // 2
-    for n in range(4):
-        @pl.when(src == n)
-        def _():
-            for t in range(2):
-                piece = pieces[2 * n + t]
-                cur_sc[:, t * each:(t + 1) * each] = piece[:, :each]
-                for part in range(2):
-                    start = wide + (2 * part + t) * HEAD_DIM
-                    cur_sc[:, start:start + HEAD_DIM] = piece[:, each + part * HEAD_DIM:each + (part + 1) * HEAD_DIM]
+    rows = cur_sc.shape[1]
+    x_copy = pltpu.make_async_copy(x_hbm, x_ref, x_sem)
+
+    def copies(n):
+        at = pl.ds(pl.multiple_of(idx[0] * rows, rows) if n < 2 else 0, rows)
+        out = []
+        for t in range(2):
+            piece = pieces[2 * n + t]
+            spans = [(0, each, t * each)] + [(each + part * HEAD_DIM, HEAD_DIM, wide + (2 * part + t) * HEAD_DIM) for part in range(2)]
+            for start, size, to in spans:
+                out.append(pltpu.make_async_copy(piece.at[at, start:start + size], cur_sc.at[n % 2, :, to:to + size],
+                                                 piece_sem.at[n % 2]))
+        return out
+
+    fetch_ahead(src, copies)
 
     @pl.when(src == 0)
     def _():
+        x_copy.start()
         acc_sc[...] = jnp.zeros_like(acc_sc)
 
     both = wide + 2 * HEAD_DIM
-    accumulate(acc_sc, lambda cols: mm(cur_sc[:, :wide], wq_ref[cols, :], ((1,), (1,)))
-               + mm(cur_sc[:, wide:both], wk_ref[cols, :], ((1,), (1,)))
-               + mm(cur_sc[:, both:], wv_ref[cols, :], ((1,), (1,))))
+    cur = src % 2
+    accumulate(acc_sc, lambda cols: mm(cur_sc[cur, :, :wide], wq_ref[cols, :], ((1,), (1,)))
+               + mm(cur_sc[cur, :, wide:both], wk_ref[cols, :], ((1,), (1,)))
+               + mm(cur_sc[cur, :, both:], wv_ref[cols, :], ((1,), (1,))))
 
     @pl.when(src == 3)
     def _():
+        x_copy.wait()
         blk = dx_sc.shape[1]
         n_blk = x_ref.shape[0] // blk
         weight = lnw_ref[...].astype(F32)
@@ -525,8 +549,6 @@
     rows, dim = x.shape
     cols = pieces[0].shape[1]
     cq, ck = w_q.shape[1] // n_dev, w_k.shape[1] // n_dev
-    mine = single((rows, cols), lambda s, ix: (ix[0], 0))
-    sent = single((rows, cols), lambda s, ix: (0, 0))
     const = lambda s, ix: (0, 0)
     head = lambda s, ix: (0, ix[1 + s])
     blk = 128
@@ -535,12 +557,13 @@
         out_shape=(jax.ShapeDtypeStruct((rows, dim), BF16), jax.ShapeDtypeStruct((1, dim), F32)),
         grid_spec=pltpu.PrefetchScalarGridSpec(
             num_scalar_prefetch=1, grid=(4,),
-            in_specs=[mine] * 4 + [sent] * 4
+            in_specs=[pl.BlockSpec(memory_space=pl.ANY)] * 8
             + [pl.BlockSpec((dim, cq), head), pl.BlockSpec((dim, ck), head), pl.BlockSpec((dim, ck), head),
-               single((rows, dim), const), pl.BlockSpec((1, dim), const)],
+               pl.BlockSpec(memory_space=pl.ANY), pl.BlockSpec((1, dim), const)],
             out_specs=(pl.BlockSpec(memory_space=pl.ANY), pl.BlockSpec((1, dim), const)),
-            scratch_shapes=[pltpu.VMEM((rows, 2 * cols), BF16), pltpu.VMEM((rows, dim), F32),
-                            pltpu.VMEM((2, blk, dim), BF16), pltpu.SemaphoreType.DMA((2,))]),
+            scratch_shapes=[pltpu.VMEM((2, rows, 2 * cols), BF16), pltpu.VMEM((rows, dim), F32),
+                            pltpu.VMEM((rows, dim), BF16), pltpu.VMEM((2, blk, dim), BF16),
+                            pltpu.SemaphoreType.DMA((2,)), pltpu.SemaphoreType.DMA((2,)), pltpu.SemaphoreType.DMA]),
         compiler_params=pltpu.CompilerParams(dimension_semantics=("arbitrary",), vmem_limit_bytes=VMEM_BYTES),
         cost_estimate=cost(16 * rows * dim * cols, 2 * (2 * rows * dim + 8 * cols * (rows + dim))),
         name="hidden_grad",
@@ -586,9 +609,9 @@
 
 
 def weight_grad(idx, hs, grs, bufs):
-    rows, dim = hs[0].shape
-    seq = 4 * rows
-    n = len(grs)
+    (both, dim), n = hs[0].shape, len(grs)
+    rows = both // 2
+    seq = 2 * both
     cols = n * grs[0].shape[1]
     wide = REP * HEAD_DIM * n
     blk = 512
@@ -599,7 +622,7 @@
         out_shape=tuple(jax.ShapeDtypeStruct(b.shape, BF16) for b in bufs) + (jax.ShapeDtypeStruct((dim, cols), BF16),),
         grid_spec=pltpu.PrefetchScalarGridSpec(
             num_scalar_prefetch=1, grid=(dim // blk,),
-            in_specs=[pl.BlockSpec((rows, blk), lambda i, ix: (0, i))] * 4
+            in_specs=[pl.BlockSpec((rows, blk), lambda i, ix: (0, i))] * 2 + [pl.BlockSpec((rows, blk), lambda i, ix: (1, i))] * 2
             + [pl.BlockSpec((seq, cols // n), lambda i, ix: (0, 0), pipeline_mode=pl.Buffered(1)) for _ in grs]
             + [pl.BlockSpec(memory_space=pl.ANY)] * 3,
             out_specs=(pl.BlockSpec((blk, wide), there), pl.BlockSpec((blk, n * HEAD_DIM), there),
@@ -710,37 +733,35 @@
         x_sp = over_core(x_par)
         g_sp = over_core(g_par)
 
-        hs = [None] * 4
-        qkv = None
-        for b, x in ((0, hidden), (2, x_sib), (1, x_par), (3, x_sp)):
-            hs[b] = ln_forward(x, ln_row)
-            qkv = qkv_block(jnp.stack([hb, toks[b]]).astype(jnp.int32), hs[b], w_q, w_k, w_v, cos_t, sin_t, seq, n_dev, qkv)
+        def pair(b):
+            return jnp.stack([hb, toks[b], toks[b + 2]]).astype(jnp.int32)
+
+        h_mine, qkv = qkv_blocks(pair(0), (hidden, x_sib), ln_row, w_q, w_k, w_v, cos_t, sin_t, seq, n_dev, None)
+        h_far, qkv = qkv_blocks(pair(1), (x_par, x_sp), ln_row, w_q, w_k, w_v, cos_t, sin_t, seq, n_dev, qkv)
+        hs = (h_mine, h_far, h_mine, h_far)
         o_own, o_t, lse = attn_forward(qkv, kv_local)
 
         wo_t = transpose_rows(hb.reshape(1).astype(jnp.int32), w_o, n_dev)
         gs = [d_attn, g_par, g_sib, g_sp]
-        d_o = None
-        for b in (0, 2, 1, 3):
-            d_o = do_block(jnp.stack([hb, toks[b]]).astype(jnp.int32), gs[b], wo_t, seq, d_o)
+        d_o = do_blocks(pair(0), (d_attn, g_sib), wo_t, seq, None)
+        d_o = do_blocks(pair(1), (g_par, g_sp), wo_t, seq, d_o)
 
         def own_rows(val, dev):
             return lax.dynamic_slice_in_dim(val, dev * rows, rows, 0)
 
-        o_par = over_chip(o_own)
+        o_par = over_chip(lax.dynamic_slice_in_dim(o_own, (chip ^ 1) * 2 * rows, 2 * rows, 0))
         sources = jnp.stack([me, *hbs]).astype(jnp.int32)
-        o_tok = [o_own, o_par, over_core(own_rows(o_own, me ^ 1)), over_core(own_rows(o_par, me ^ 1))]
+        o_tok = [o_own, o_par, over_core(own_rows(o_own, me ^ 1)), over_core(own_rows(o_par, core ^ 1))]
         attn_out = out_proj(sources, o_tok, w_o, rows)
 
         def blocks(where):
             return jnp.stack([where, *toks]).astype(jnp.int32)
 
         d_w_o, *d_w = reserve(w_o.shape, w_q.shape, w_k.shape, w_v.shape)
-        sent = []
-        for b, o in ((hbs[0], o_own), (hbs[1], o_par)):
-            d_w_o, piece = out_weight_grad(blocks(b), o, gs, d_w_o)
-            sent.append(over_core(piece))
-        for b, piece in zip(hbs[2:], sent):
-            d_w_o = lax.dynamic_update_slice_in_dim(d_w_o, piece, b * cq, 0)
+        d_w_o, piece = out_weight_grad(blocks(hbs[0]), o_own, gs, d_w_o)
+        far = over_chip(piece)
+        for b, val in ((hbs[2], over_core(piece)), (hbs[1], far), (hbs[3], over_core(far))):
+            d_w_o = lax.dynamic_update_slice_in_dim(d_w_o, val, b * cq, 0)
 
         gr = []
         for t in range(kv_local):

time: 1300 us -> 1240 us (0.954)
  Pallas kernels: 701 us -> 626 us
    pallas_call x12 -> x4, Pallas kernels: 138 us -> 95.4 us  [the longest x2 61.3 us: qkv_blocks(): pl.pallas_call(qkv_kernel, out_shape=(jax.ShapeDtypeStruct((2 * rows, dim...]
    pallas_call x2 -> x1, Pallas kernels: 54.8 us -> 27.2 us  [out_weight_grad(): pl.pallas_call(dwo_kernel, out_shape=(jax.ShapeDtypeStruct(buf.shape, BF1...]
    ppermute x7 -> x8, waiting for transfers between devices: 533 us -> 537 us  [over_chip(): return lax.ppermute(val, 'sp', [(i, i ^ 2) for i in range(n_dev)])]
  transfers between devices with their start and end apart: 25 -> 26, of which waited for: 6 -> 6; matrix products, arithmetic and copies ran while one was open for 3% -> 4% of each run, Pallas kernels for 35% -> 30%
where the time goes in v5:
time: 1240 us; the launch traced here: 1230 us
  Pallas kernels  626 us (50%)
  waiting for transfers between devices  538 us (43%)
  local copies, waits for them, and re-layouts  34.9 us (3%)
  starting transfers between devices  16.1 us (1%)
    ppermute x8, waiting for transfers between devices, over_chip(): return lax.ppermute(val, 'sp', [(i, i ^ 2) for i in range(n_dev)])  537 us
    pallas_call x2, Pallas kernels, attn_backward(): pl.pallas_call(bwd_kernel, grid=(nq,), in_specs=[pl.BlockSpec((BQ, wide),...  190 us
    pallas_call x1, Pallas kernels, attn_forward(): pl.pallas_call(fwd_kernel, grid=(kv_local, nq), in_specs=[pl.BlockSpec((B...  103 us
    pallas_call x3, Pallas kernels, weight_grad(): pl.pallas_call(dw_kernel, out_shape=tuple((jax.ShapeDtypeStruct(b.shape,...  99.4 us
    pallas_call x2, Pallas kernels, qkv_blocks(): pl.pallas_call(qkv_kernel, out_shape=(jax.ShapeDtypeStruct((2 * rows, dim...  61.3 us
    pallas_call x1, Pallas kernels, hidden_grad(): pl.pallas_call(dh_kernel, out_shape=(jax.ShapeDtypeStruct((rows, dim), BF...  55 us
    pallas_call x2, Pallas kernels, do_blocks(): pl.pallas_call(do_kernel, out_shape=jax.ShapeDtypeStruct((seq, ce), BF16)...  34 us
    pallas_call x1, Pallas kernels, out_proj(): pl.pallas_call(out_kernel, out_shape=jax.ShapeDtypeStruct((rows, dim), BF...  30.9 us
  transfers between devices with their start and end apart: 26, of which 6 were waited for; matrix products, arithmetic and copies ran while one was open for 4% of the time, Pallas kernels for 30%

profile of v5, /device:TPU:0, one launch (start us, length us, event | category | flops | bytes accessed | tf_op | source)
XLA Modules:
  0.0 1228.1 jit_solution(4099790166029850628)
XLA Ops:
  0.6 3.3 collective-permute-start
  4.5 136.1 %collective-permute-done.xa_ref = bf16[1024,3072]{1,0:T(8,128)(2,1)} collective-permute-done((bf16[1024,3072]{1,0:T(8,128)(2,1)}, bf16[1024,3072]{1,0:T(8,128)(2,1)}, u32[]{:S(2)}, u32[]{:S(2)}) %collective-permute-start) | collective-permute-done | bytes 6291488 | tf_op jit(solution)/shard_map/ppermute | solution.py:703
  140.6 2.0 collective-permute-start.3
  142.7 132.0 %collective-permute-done.3 = s32[1024]{0:T(1024)S(1)} collective-permute-done((s32[1024]{0:T(1024)}, s32[1024]{0:T(1024)S(1)}, u32[]{:S(2)}, u32[]{:S(2)}) %collective-permute-start.3) | collective-permute-done | bytes 4128 | tf_op jit(solution)/shard_map/ppermute | solution.py:703
  274.7 0.7 pad_add_fusion.1.idx
  275.3 0.7 collective-permute-done.2
  276.2 0.7 pad_add_fusion.idx
  276.9 0.7 stack.93.idx
  277.7 1.3 reshape.68.lnw_ref.refs_12_
  279.0 6.6 wo_t.1.wo_ref
  285.7 9.4 fusion
  295.5 17.0 %d_o.2.rest_0_ = bf16[4096,768]{1,0:T(8,128)(2,1)} custom-call(s32[3]{0:T(128)} %pad_add_fusion.1.idx, bf16[1024,3072]{1,0:T(8,128)(2,1)} %refs_0_.1, bf16[1024,3072]{1,0:T(8,128)(2,1)} %collective-permute-done.11.gb_ref.refs_2_, bf16[3072,768]{1,0:T(8,128)(2,1)} %wo_t.1.wo_ref), custom_call_target="tpu_custom_call" | custom-call | flops 9663676416 | bytes 20447232 | tf_op jit(solution)/shard_map/d_o/pallas_call | solution.py:149
  312.5 30.4 %ln_qkv.2 = (bf16[2048,3072]{1,0:T(8,128)(2,1)}, bf16[4096,1280]{1,0:T(8,128)(2,1)}) custom-call(s32[3]{0:T(128)} %pad_add_fusion.1.idx, bf16[1024,3072]{1,0:T(8,128)(2,1)} %refs_11_.1, bf16[1024,3072]{1,0:T(8,128)(2,1)} %collective-permute-done.5.xb_ref, bf16[1,3072]{1,0:T(2,128)(2,1)} %reshape.68.lnw_ref.refs_12_, bf16[3072,3072]{1,0:T(8,128)(2,1)} %refs_8_.1, ...), custom_call_target="tpu_custom_call" | custom-call | flops 16106127360 | bytes 38273024 | tf_op jit(solution)/shard_map/ln_qkv/pallas_call | solution.py:98
  342.9 30.9 %ln_qkv.3 = (bf16[2048,3072]{1,0:T(8,128)(2,1)}, bf16[4096,1280]{1,0:T(8,128)(2,1)}) custom-call(s32[3]{0:T(128)} %pad_add_fusion.idx, bf16[1024,3072]{1,0:T(8,128)(2,1)} %collective-permute-done.xa_ref, bf16[1024,3072]{1,0:T(8,128)(2,1)} %collective-permute-done.1.xb_ref, ...), custom_call_target="tpu_custom_call", output_to_operand_aliasing={{1}: (9, {})} | custom-call | flops 16106127360 | bytes 38273024 | tf_op jit(solution)/shard_map/ln_qkv/pallas_call | solution.py:98
  373.8 102.7 %attn_fwd.1 = (bf16[4096,768]{1,0:T(8,128)(2,1)}, f32[2,16,128,768]{3,2,1,0:T(8,128)}, f32[2,16,1,768]{3,2,1,0:T(1,128)}) custom-call(bf16[4096,1280]{1,0:T(8,128)(2,1)} %get-tuple-element.44.q_ref.k_ref.v_ref, bf16[4096,1280]{1,0:T(8,128)(2,1)} %get-tuple-element.44.q_ref.k_ref.v_ref, bf16[4096,1280]{1,0:T(8,128)(2,1)} %get-tuple-element.44.q_ref.k_ref.v_ref), custom_call_target="tpu_custom_call" | custom-call | flops 51539607552 | bytes 25165824 | tf_op jit(solution)/shard_map/attn_fwd/pallas_call | solution.py:259
  476.5 17.0 %d_o.3.do_ref = bf16[4096,768]{1,0:T(8,128)(2,1)} custom-call(s32[3]{0:T(128)} %pad_add_fusion.idx, bf16[1024,3072]{1,0:T(8,128)(2,1)} %collective-permute-done.9.ga_ref.refs_1_, bf16[1024,3072]{1,0:T(8,128)(2,1)} %collective-permute-done.10.gb_ref.refs_3_, bf16[3072,768]{1,0:T(8,128)(2,1)} %wo_t.1.wo_ref, ...), custom_call_target="tpu_custom_call", output_to_operand_aliasing={{}: (4, {})} | custom-call | flops 9663676416 | bytes 20447232 | tf_op jit(solution)/shard_map/d_o/pallas_call | solution.py:149
  493.6 94.9 %attn_bwd.3.refs_1_.refs_5_ = bf16[4096,640]{1,0:T(8,128)(2,1)} custom-call(bf16[4096,1280]{1,0:T(8,128)(2,1)} %get-tuple-element.44.q_ref.k_ref.v_ref, bf16[4096,1280]{1,0:T(8,128)(2,1)} %get-tuple-element.44.q_ref.k_ref.v_ref, bf16[4096,1280]{1,0:T(8,128)(2,1)} %get-tuple-element.44.q_ref.k_ref.v_ref, bf16[4096,768]{1,0:T(8,128)(2,1)} %d_o.3.do_ref, ...), custom_call_target="tpu_custom_call" | custom-call | flops 64424509440 | bytes 25165824 | tf_op jit(solution)/shard_map/attn_bwd/pallas_call | solution.py:373
  588.5 94.8 %attn_bwd.2.refs_0_.refs_4_ = bf16[4096,640]{1,0:T(8,128)(2,1)} custom-call(bf16[4096,1280]{1,0:T(8,128)(2,1)} %get-tuple-element.44.q_ref.k_ref.v_ref, bf16[4096,1280]{1,0:T(8,128)(2,1)} %get-tuple-element.44.q_ref.k_ref.v_ref, bf16[4096,1280]{1,0:T(8,128)(2,1)} %get-tuple-element.44.q_ref.k_ref.v_ref, bf16[4096,768]{1,0:T(8,128)(2,1)} %d_o.3.do_ref, ...), custom_call_target="tpu_custom_call" | custom-call | flops 64424509440 | bytes 25165824 | tf_op jit(solution)/shard_map/attn_bwd/pallas_call | solution.py:373
  683.4 43.3 %weight_grad.3 = (bf16[3072,3072]{1,0:T(8,128)(2,1)}, bf16[3072,1024]{1,0:T(8,128)(2,1)}, bf16[3072,1024]{1,0:T(8,128)(2,1)}, bf16[3072,1280]{1,0:T(8,128)(2,1)}) custom-call(s32[5]{0:T(128)} %stack.93.idx, bf16[2048,3072]{1,0:T(8,128)(2,1)} %get-tuple-element.50.refs_0_.refs_2_, ...), custom_call_target="tpu_custom_call", output_to_operand_aliasing={{0}: (7, {}), {1}: (8, {}), {2}: (9, {})} | custom-call | flops 32212254720 | bytes 51380224 | tf_op jit(solution)/shard_map/weight_grad/pallas_call | solution.py:620
  726.9 1.7 collective-permute-start.12
  728.7 0.6 stack.92.idx
  729.6 27.2 %out_weight_grad.1 = (bf16[3072,3072]{1,0:T(8,128)(2,1)}, bf16[768,3072]{1,0:T(8,128)(2,1)}) custom-call(s32[5]{0:T(128)} %stack.93.idx, bf16[4096,768]{1,0:T(8,128)(2,1)} %get-tuple-element.45.refs_0_.o_ref, bf16[1024,3072]{1,0:T(8,128)(2,1)} %refs_0_.1, bf16[1024,3072]{1,0:T(8,128)(2,1)} %collective-permute-done.9.ga_ref.refs_1_, ...), custom_call_target="tpu_custom_call", output_to_operand_aliasing={{0}: (6, {})} | custom-call | flops 19327352832 | bytes 40894464 | tf_op jit(solution)/shard_map/out_weight_grad/pallas_call | solution.py:652
  756.8 2.1 constant_dynamic-slice_fusion.6
  758.9 1.8 collective-permute-start.6
  760.7 7.7 place.3
  768.4 74.7 %collective-permute-done.12.refs_2_.refs_4_ = bf16[4096,640]{1,0:T(8,128)(2,1)} collective-permute-done((bf16[4096,640]{1,0:T(8,128)(2,1)}, bf16[4096,640]{1,0:T(8,128)(2,1)}, u32[]{:S(2)}, u32[]{:S(2)}) %collective-permute-start.12) | collective-permute-done | bytes 5242912 | tf_op jit(solution)/shard_map/ppermute | solution.py:703
  843.1 28.1 %weight_grad.4 = (bf16[3072,3072]{1,0:T(8,128)(2,1)}, bf16[3072,1024]{1,0:T(8,128)(2,1)}, bf16[3072,1024]{1,0:T(8,128)(2,1)}, bf16[3072,640]{1,0:T(8,128)(2,1)}) custom-call(s32[5]{0:T(128)} %stack.92.idx, bf16[2048,3072]{1,0:T(8,128)(2,1)} %get-tuple-element.50.refs_0_.refs_2_, ...), custom_call_target="tpu_custom_call", output_to_operand_aliasing={{0}: (6, {}), {1}: (7, {}), {2}: (8, {})} | custom-call | flops 16106127360 | bytes 38273024 | tf_op jit(solution)/shard_map/weight_grad/pallas_call | solution.py:620
  871.3 1.8 collective-permute-start.24
  873.0 0.7 stack.44.idx
  873.7 0.6 stack.37.idx
  874.3 2.5 constant_dynamic-slice_fusion.2
  876.9 2.5 constant_dynamic-slice_fusion.3
  879.3 2.7 constant_dynamic-slice_fusion.5
  882.0 140.9 %collective-permute-done.6.refs_1_ = bf16[2048,768]{1,0:T(8,128)(2,1)} collective-permute-done((bf16[2048,768]{1,0:T(8,128)(2,1)S(1)}, bf16[2048,768]{1,0:T(8,128)(2,1)}, u32[]{:S(2)}, u32[]{:S(2)}) %collective-permute-start.6) | collective-permute-done | bytes 3145760 | tf_op jit(solution)/shard_map/ppermute | solution.py:703
  1022.9 1.5 constant_dynamic-slice_fusion.4
  1025.0 4.8 constant_dynamic-update-slice_fusion.2
  1029.8 2.5 constant_dynamic-slice_fusion
  1032.4 2.5 constant_dynamic-slice_fusion.1
  1035.3 5.7 place.4
  1041.0 28.0 %weight_grad.5 = (bf16[3072,3072]{1,0:T(8,128)(2,1)}, bf16[3072,1024]{1,0:T(8,128)(2,1)}, bf16[3072,1024]{1,0:T(8,128)(2,1)}, bf16[3072,640]{1,0:T(8,128)(2,1)}) custom-call(s32[5]{0:T(128)} %stack.44.idx, bf16[2048,3072]{1,0:T(8,128)(2,1)} %get-tuple-element.50.refs_0_.refs_2_, ...), custom_call_target="tpu_custom_call", output_to_operand_aliasing={{0}: (6, {}), {1}: (7, {}), {2}: (8, {})} | custom-call | flops 16106127360 | bytes 38273024 | tf_op jit(solution)/shard_map/weight_grad/pallas_call | solution.py:620
  1069.6 53.8 %collective-permute-done.24 = bf16[768,3072]{1,0:T(8,128)(2,1)} collective-permute-done((bf16[768,3072]{1,0:T(8,128)(2,1)}, bf16[768,3072]{1,0:T(8,128)(2,1)}, u32[]{:S(2)}, u32[]{:S(2)}) %collective-permute-start.24) | collective-permute-done | bytes 4718624 | tf_op jit(solution)/shard_map/ppermute | solution.py:703
  1123.9 55.0 %hidden_grad.1 = (bf16[1024,3072]{1,0:T(8,128)(2,1)}, f32[1,3072]{1,0:T(1,128)}) custom-call(s32[5]{0:T(128)} %stack.37.idx, bf16[4096,640]{1,0:T(8,128)(2,1)} %attn_bwd.2.refs_0_.refs_4_, bf16[4096,640]{1,0:T(8,128)(2,1)} %attn_bwd.3.refs_1_.refs_5_, bf16[4096,640]{1,0:T(8,128)(2,1)} %collective-permute-done.12.refs_2_.refs_4_, ...), custom_call_target="tpu_custom_call" | custom-call | flops 32212254720 | bytes 54525952 | tf_op jit(solution)/shard_map/hidden_grad/pallas_call | solution.py:555
  1178.9 4.8 constant_dynamic-update-slice_fusion.1
  1183.8 1.8 collective-permute-start.19
  1185.6 30.9 %out_proj.1 = bf16[1024,3072]{1,0:T(8,128)(2,1)} custom-call(s32[5]{0:T(128)} %stack.37.idx, bf16[4096,768]{1,0:T(8,128)(2,1)} %get-tuple-element.45.refs_0_.o_ref, bf16[2048,768]{1,0:T(8,128)(2,1)} %collective-permute-done.6.refs_1_, bf16[1024,768]{1,0:T(8,128)(2,1)} %collective-permute-done.7.refs_2_, bf16[1024,768]{1,0:T(8,128)(2,1)} %collective-permute-done.8.refs_3_, ...), custom_call_target="tpu_custom_call" | custom-call | flops 19327352832 | bytes 31457280 | tf_op jit(solution)/shard_map/out_proj/pallas_call | solution.py:462
  1216.4 0.6 convert_reduce_fusion
  1217.1 4.8 constant_dynamic-update-slice_fusion
  1221.9 5.7 place.5
  (54 shorter events, 4.1 us)
Async XLA Ops:
  0.6 140.0 %collective-permute-start = (bf16[1024,3072]{1,0:T(8,128)(2,1)}, bf16[1024,3072]{1,0:T(8,128)(2,1)}, u32[]{:S(2)}, u32[]{:S(2)}) collective-permute-start(bf16[1024,3072]{1,0:T(8,128)(2,1)} %refs_11_.1), channel_id=1, source_target_pairs={{0,2},{1,3},{2,0},{3,1},{4,6},{5,7},{6,4},{7,5}} | collective-permute-start | bytes 18874376 | tf_op jit(solution)/shard_map/ppermute | solution.py:703
  4.0 291.1 %collective-permute-start.9 = (bf16[1024,3072]{1,0:T(8,128)(2,1)}, bf16[1024,3072]{1,0:T(8,128)(2,1)}, u32[]{:S(2)}, u32[]{:S(2)}) collective-permute-start(bf16[1024,3072]{1,0:T(8,128)(2,1)} %refs_0_.1), channel_id=1, source_target_pairs={{0,2},{1,3},{2,0},{3,1},{4,6},{5,7},{6,4},{7,5}} | collective-permute-start | bytes 18874376 | tf_op jit(solution)/shard_map/ppermute | solution.py:703
  4.0 291.5 %collective-permute-start.11 = (bf16[1024,3072]{1,0:T(8,128)(2,1)}, bf16[1024,3072]{1,0:T(8,128)(2,1)}, u32[]{:S(2)}, u32[]{:S(2)}) collective-permute-start(bf16[1024,3072]{1,0:T(8,128)(2,1)} %refs_0_.1), channel_id=1, source_target_pairs={{0,1},{1,0},{2,3},{3,2},{4,5},{5,4},{6,7},{7,6}} | collective-permute-start | bytes 18874376 | tf_op jit(solution)/shard_map/ppermute | solution.py:706
  4.0 308.5 %collective-permute-start.5 = (bf16[1024,3072]{1,0:T(8,128)(2,1)}, bf16[1024,3072]{1,0:T(8,128)(2,1)}, u32[]{:S(2)}, u32[]{:S(2)}) collective-permute-start(bf16[1024,3072]{1,0:T(8,128)(2,1)} %refs_11_.1), channel_id=1, source_target_pairs={{0,1},{1,0},{2,3},{3,2},{4,5},{5,4},{6,7},{7,6}} | collective-permute-start | bytes 18874376 | tf_op jit(solution)/shard_map/ppermute | solution.py:706
  140.6 202.2 %collective-permute-start.1 = (bf16[1024,3072]{1,0:T(8,128)(2,1)}, bf16[1024,3072]{1,0:T(8,128)(2,1)}, u32[]{:S(2)}, u32[]{:S(2)}) collective-permute-start(bf16[1024,3072]{1,0:T(8,128)(2,1)} %collective-permute-done.xa_ref), channel_id=1, source_target_pairs={{0,1},{1,0},{2,3},{3,2},{4,5},{5,4},{6,7},{7,6}} | collective-permute-start | bytes 18874376 | tf_op jit(solution)/shard_map/ppermute | solution.py:706
  140.6 134.0 %collective-permute-start.3 = (s32[1024]{0:T(1024)}, s32[1024]{0:T(1024)S(1)}, u32[]{:S(2)}, u32[]{:S(2)}) collective-permute-start(s32[1024]{0:T(1024)} %param.9), channel_id=1, source_target_pairs={{0,2},{1,3},{2,0},{3,1},{4,6},{5,7},{6,4},{7,5}} | collective-permute-start | bytes 12296 | tf_op jit(solution)/shard_map/ppermute | solution.py:703
  274.7 1.4 collective-permute-start.2
  276.0 9.6 collective-permute-start.4
  279.0 6.6 copy-start.2
  295.1 181.4 %collective-permute-start.10 = (bf16[1024,3072]{1,0:T(8,128)(2,1)}, bf16[1024,3072]{1,0:T(8,128)(2,1)}, u32[]{:S(2)}, u32[]{:S(2)}) collective-permute-start(bf16[1024,3072]{1,0:T(8,128)(2,1)} %collective-permute-done.9.ga_ref.refs_1_), channel_id=1, source_target_pairs={{0,1},{1,0},{2,3},{3,2},{4,5},{5,4},{6,7},{7,6}} | collective-permute-start | bytes 18874376 | tf_op jit(solution)/shard_map/ppermute | solution.py:706
  726.7 34.0 %collective-permute-start.20 = (bf16[3072,1280]{1,0:T(8,128)(2,1)}, bf16[3072,1280]{1,0:T(8,128)(2,1)}, u32[]{:S(2)}, u32[]{:S(2)}) collective-permute-start(bf16[3072,1280]{1,0:T(8,128)(2,1)} %get-tuple-element.55), channel_id=1, source_target_pairs={{0,1},{1,0},{2,3},{3,2},{4,5},{5,4},{6,7},{7,6}} | collective-permute-start | bytes 23592968 | tf_op jit(solution)/shard_map/ppermute | solution.py:706
  726.9 116.2 %collective-permute-start.12 = (bf16[4096,640]{1,0:T(8,128)(2,1)}, bf16[4096,640]{1,0:T(8,128)(2,1)}, u32[]{:S(2)}, u32[]{:S(2)}) collective-permute-start(bf16[4096,640]{1,0:T(8,128)(2,1)} %attn_bwd.2.refs_0_.refs_4_), channel_id=1, source_target_pairs={{0,2},{1,3},{2,0},{3,1},{4,6},{5,7},{6,4},{7,5}} | collective-permute-start | bytes 15728648 | tf_op jit(solution)/shard_map/ppermute | solution.py:703
  729.3 300.5 %collective-permute-start.13 = (bf16[4096,640]{1,0:T(8,128)(2,1)}, bf16[4096,640]{1,0:T(8,128)(2,1)}, u32[]{:S(2)}, u32[]{:S(2)}) collective-permute-start(bf16[4096,640]{1,0:T(8,128)(2,1)} %attn_bwd.3.refs_1_.refs_5_), channel_id=1, source_target_pairs={{0,2},{1,3},{2,0},{3,1},{4,6},{5,7},{6,4},{7,5}} | collective-permute-start | bytes 15728648 | tf_op jit(solution)/shard_map/ppermute | solution.py:703
  756.8 267.6 %collective-permute-start.23 = (bf16[768,3072]{1,0:T(8,128)(2,1)}, bf16[768,3072]{1,0:T(8,128)(2,1)}, u32[]{:S(2)}, u32[]{:S(2)}) collective-permute-start(bf16[768,3072]{1,0:T(8,128)(2,1)} %get-tuple-element.78), channel_id=1, source_target_pairs={{0,1},{1,0},{2,3},{3,2},{4,5},{5,4},{6,7},{7,6}} | collective-permute-start | bytes 14155784 | tf_op jit(solution)/shard_map/ppermute | solution.py:706
  758.9 264.0 %collective-permute-start.6 = (bf16[2048,768]{1,0:T(8,128)(2,1)S(1)}, bf16[2048,768]{1,0:T(8,128)(2,1)}, u32[]{:S(2)}, u32[]{:S(2)}) collective-permute-start(bf16[2048,768]{1,0:T(8,128)(2,1)S(1)} %constant_dynamic-slice_fusion.6), channel_id=1, source_target_pairs={{0,2},{1,3},{2,0},{3,1},{4,6},{5,7},{6,4},{7,5}} | collective-permute-start | bytes 9437192 | tf_op jit(solution)/shard_map/ppermute | solution.py:703
  871.3 163.6 %collective-permute-start.21 = (bf16[3072,640]{1,0:T(8,128)(2,1)}, bf16[3072,640]{1,0:T(8,128)(2,1)}, u32[]{:S(2)}, u32[]{:S(2)}) collective-permute-start(bf16[3072,640]{1,0:T(8,128)(2,1)} %get-tuple-element.62), channel_id=1, source_target_pairs={{0,1},{1,0},{2,3},{3,2},{4,5},{5,4},{6,7},{7,6}} | collective-permute-start | bytes 11796488 | tf_op jit(solution)/shard_map/ppermute | solution.py:706
  871.3 252.1 %collective-permute-start.24 = (bf16[768,3072]{1,0:T(8,128)(2,1)}, bf16[768,3072]{1,0:T(8,128)(2,1)}, u32[]{:S(2)}, u32[]{:S(2)}) collective-permute-start(bf16[768,3072]{1,0:T(8,128)(2,1)} %get-tuple-element.78), channel_id=1, source_target_pairs={{0,2},{1,3},{2,0},{3,1},{4,6},{5,7},{6,4},{7,5}} | collective-permute-start | bytes 14155784 | tf_op jit(solution)/shard_map/ppermute | solution.py:703
  1022.9 46.1 %collective-permute-start.15 = (bf16[1024,640]{1,0:T(8,128)(2,1)}, bf16[1024,640]{1,0:T(8,128)(2,1)}, u32[]{:S(2)}, u32[]{:S(2)}) collective-permute-start(bf16[1024,640]{1,0:T(8,128)(2,1)} %constant_dynamic-slice_fusion.2), channel_id=1, source_target_pairs={{0,1},{1,0},{2,3},{3,2},{4,5},{5,4},{6,7},{7,6}} | collective-permute-start | bytes 3932168 | tf_op jit(solution)/shard_map/ppermute | solution.py:706
  1024.4 44.7 %collective-permute-start.14 = (bf16[1024,640]{1,0:T(8,128)(2,1)}, bf16[1024,640]{1,0:T(8,128)(2,1)}, u32[]{:S(2)}, u32[]{:S(2)}) collective-permute-start(bf16[1024,640]{1,0:T(8,128)(2,1)} %constant_dynamic-slice_fusion.3), channel_id=1, source_target_pairs={{0,1},{1,0},{2,3},{3,2},{4,5},{5,4},{6,7},{7,6}} | collective-permute-start | bytes 3932168 | tf_op jit(solution)/shard_map/ppermute | solution.py:706
  1032.3 91.0 %collective-permute-start.17 = (bf16[1024,640]{1,0:T(8,128)(2,1)}, bf16[1024,640]{1,0:T(8,128)(2,1)}, u32[]{:S(2)}, u32[]{:S(2)}) collective-permute-start(bf16[1024,640]{1,0:T(8,128)(2,1)} %constant_dynamic-slice_fusion), channel_id=1, source_target_pairs={{0,1},{1,0},{2,3},{3,2},{4,5},{5,4},{6,7},{7,6}} | collective-permute-start | bytes 3932168 | tf_op jit(solution)/shard_map/ppermute | solution.py:706
  1034.8 89.0 %collective-permute-start.16 = (bf16[1024,640]{1,0:T(8,128)(2,1)}, bf16[1024,640]{1,0:T(8,128)(2,1)}, u32[]{:S(2)}, u32[]{:S(2)}) collective-permute-start(bf16[1024,640]{1,0:T(8,128)(2,1)} %constant_dynamic-slice_fusion.1), channel_id=1, source_target_pairs={{0,1},{1,0},{2,3},{3,2},{4,5},{5,4},{6,7},{7,6}} | collective-permute-start | bytes 3932168 | tf_op jit(solution)/shard_map/ppermute | solution.py:706
  1041.0 28.0 %copy-start = (bf16[1024,768]{1,0:T(8,128)(2,1)S(1)}, bf16[1024,768]{1,0:T(8,128)(2,1)}, u32[]{:S(2)}) copy-start(bf16[1024,768]{1,0:T(8,128)(2,1)} %constant_dynamic-slice_fusion.5) | copy-start | bytes 4718596
  1069.1 116.5 %collective-permute-start.7 = (bf16[1024,768]{1,0:T(8,128)(2,1)S(1)}, bf16[1024,768]{1,0:T(8,128)(2,1)}, u32[]{:S(2)}, u32[]{:S(2)}) collective-permute-start(bf16[1024,768]{1,0:T(8,128)(2,1)S(1)} %copy-done), channel_id=1, source_target_pairs={{0,1},{1,0},{2,3},{3,2},{4,5},{5,4},{6,7},{7,6}} | collective-permute-start | bytes 4718600 | tf_op jit(solution)/shard_map/ppermute | solution.py:706
  1069.1 116.4 %collective-permute-start.8 = (bf16[1024,768]{1,0:T(8,128)(2,1)S(1)}, bf16[1024,768]{1,0:T(8,128)(2,1)}, u32[]{:S(2)}, u32[]{:S(2)}) collective-permute-start(bf16[1024,768]{1,0:T(8,128)(2,1)S(1)} %constant_dynamic-slice_fusion.4), channel_id=1, source_target_pairs={{0,1},{1,0},{2,3},{3,2},{4,5},{5,4},{6,7},{7,6}} | collective-permute-start | bytes 4718600 | tf_op jit(solution)/shard_map/ppermute | solution.py:706
  1123.4 93.7 %collective-permute-start.25 = (bf16[768,3072]{1,0:T(8,128)(2,1)}, bf16[768,3072]{1,0:T(8,128)(2,1)}, u32[]{:S(2)}, u32[]{:S(2)}) collective-permute-start(bf16[768,3072]{1,0:T(8,128)(2,1)} %collective-permute-done.24), channel_id=1, source_target_pairs={{0,1},{1,0},{2,3},{3,2},{4,5},{5,4},{6,7},{7,6}} | collective-permute-start | bytes 14155784 | tf_op jit(solution)/shard_map/ppermute | solution.py:706
  1123.4 98.6 %collective-permute-start.22 = (bf16[3072,640]{1,0:T(8,128)(2,1)}, bf16[3072,640]{1,0:T(8,128)(2,1)}, u32[]{:S(2)}, u32[]{:S(2)}) collective-permute-start(bf16[3072,640]{1,0:T(8,128)(2,1)} %get-tuple-element.69), channel_id=1, source_target_pairs={{0,1},{1,0},{2,3},{3,2},{4,5},{5,4},{6,7},{7,6}} | collective-permute-start | bytes 11796488 | tf_op jit(solution)/shard_map/ppermute | solution.py:706
  1178.8 4.9 copy-start.1
  1178.9 4.9 collective-permute-start.18
  1183.8 32.6 %collective-permute-start.19 = (f32[1,3072]{1,0:T(1,128)S(1)}, f32[1,3072]{1,0:T(1,128)S(1)}, u32[]{:S(2)}, u32[]{:S(2)}) collective-permute-start(f32[1,3072]{1,0:T(1,128)S(1)} %add.58), channel_id=1, source_target_pairs={{0,2},{1,3},{2,0},{3,1},{4,6},{5,7},{6,4},{7,5}} | collective-permute-start | bytes 36872 | tf_op jit(solution)/shard_map/ppermute | solution.py:703

commit v6 on v5

--- a/solution.py
+++ b/solution.py
@@ -138,8 +138,8 @@
 def do_blocks(idx, gs, wo_t, seq, prev):
     rows, dim = gs[0].shape
     ce = wo_t.shape[1]
-    per = rows // BQ
-    in_specs = pair_specs((BQ, dim), per) + [pl.BlockSpec((dim, ce), lambda p, i, ix: (0, 0))]
+    per = rows // ROWS
+    in_specs = pair_specs((ROWS, dim), per) + [pl.BlockSpec((dim, ce), lambda p, i, ix: (0, 0))]
     args = [idx, *gs, wo_t]
     aliases = {}
     if prev is not None:
@@ -151,8 +151,8 @@
         out_shape=jax.ShapeDtypeStruct((seq, ce), BF16),
         grid_spec=pltpu.PrefetchScalarGridSpec(
             num_scalar_prefetch=1, grid=(2, per), in_specs=in_specs,
-            out_specs=pl.BlockSpec((BQ, ce), lambda p, i, ix: (ix[1 + p] * per + i, 0)),
-            scratch_shapes=[pltpu.VMEM((BQ, dim), BF16)]),
+            out_specs=pl.BlockSpec((ROWS, ce), lambda p, i, ix: (ix[1 + p] * per + i, 0)),
+            scratch_shapes=[pltpu.VMEM((ROWS, dim), BF16)]),
         input_output_aliases=aliases,
         compiler_params=pltpu.CompilerParams(dimension_semantics=("arbitrary", "arbitrary"), vmem_limit_bytes=VMEM_BYTES),
         cost_estimate=cost(4 * rows * dim * ce, 2 * (2 * rows * dim + dim * ce + 2 * rows * ce)),

time: 1240 us -> 1240 us (level)
  no operation moved by 1% of the time
where the time goes in v6:
time: 1240 us; the launch traced here: 1230 us
  Pallas kernels  626 us (50%)
  waiting for transfers between devices  538 us (43%)
  local copies, waits for them, and re-layouts  34.9 us (3%)
  starting transfers between devices  15.9 us (1%)
    ppermute x8, waiting for transfers between devices, over_chip(): return lax.ppermute(val, 'sp', [(i, i ^ 2) for i in range(n_dev)])  538 us
    pallas_call x2, Pallas kernels, attn_backward(): pl.pallas_call(bwd_kernel, grid=(nq,), in_specs=[pl.BlockSpec((BQ, wide),...  190 us
    pallas_call x1, Pallas kernels, attn_forward(): pl.pallas_call(fwd_kernel, grid=(kv_local, nq), in_specs=[pl.BlockSpec((B...  103 us
    pallas_call x3, Pallas kernels, weight_grad(): pl.pallas_call(dw_kernel, out_shape=tuple((jax.ShapeDtypeStruct(b.shape,...  99.4 us
    pallas_call x2, Pallas kernels, qkv_blocks(): pl.pallas_call(qkv_kernel, out_shape=(jax.ShapeDtypeStruct((2 * rows, dim...  61 us
    pallas_call x1, Pallas kernels, hidden_grad(): pl.pallas_call(dh_kernel, out_shape=(jax.ShapeDtypeStruct((rows, dim), BF...  54.9 us
    pallas_call x2, Pallas kernels, do_blocks(): pl.pallas_call(do_kernel, out_shape=jax.ShapeDtypeStruct((seq, ce), BF16)...  34.3 us
    pallas_call x1, Pallas kernels, out_proj(): pl.pallas_call(out_kernel, out_shape=jax.ShapeDtypeStruct((rows, dim), BF...  30.9 us
  transfers between devices with their start and end apart: 26, of which 6 were waited for; matrix products, arithmetic and copies ran while one was open for 4% of the time, Pallas kernels for 30%

profile of v6, /device:TPU:0, one launch (start us, length us, event | category | flops | bytes accessed | tf_op | source)
XLA Modules:
  0.0 1228.2 jit_solution(10550146081988109145)
XLA Ops:
  0.6 3.3 collective-permute-start
  4.5 136.1 %collective-permute-done.xa_ref = bf16[1024,3072]{1,0:T(8,128)(2,1)} collective-permute-done((bf16[1024,3072]{1,0:T(8,128)(2,1)}, bf16[1024,3072]{1,0:T(8,128)(2,1)}, u32[]{:S(2)}, u32[]{:S(2)}) %collective-permute-start) | collective-permute-done | bytes 6291488 | tf_op jit(solution)/shard_map/ppermute | solution.py:703
  140.6 2.0 collective-permute-start.3
  142.7 132.0 %collective-permute-done.3 = s32[1024]{0:T(1024)S(1)} collective-permute-done((s32[1024]{0:T(1024)}, s32[1024]{0:T(1024)S(1)}, u32[]{:S(2)}, u32[]{:S(2)}) %collective-permute-start.3) | collective-permute-done | bytes 4128 | tf_op jit(solution)/shard_map/ppermute | solution.py:703
  274.7 0.7 pad_add_fusion.1.idx
  275.3 0.7 collective-permute-done.2
  276.2 0.7 pad_add_fusion.idx
  276.9 0.7 stack.93.idx
  277.7 1.3 reshape.68.lnw_ref.refs_12_
  279.0 6.6 wo_t.1.wo_ref
  285.7 9.4 fusion
  295.5 17.2 %d_o.2.rest_0_ = bf16[4096,768]{1,0:T(8,128)(2,1)} custom-call(s32[3]{0:T(128)} %pad_add_fusion.1.idx, bf16[1024,3072]{1,0:T(8,128)(2,1)} %refs_0_.1, bf16[1024,3072]{1,0:T(8,128)(2,1)} %collective-permute-done.11.gb_ref.refs_2_, bf16[3072,768]{1,0:T(8,128)(2,1)} %wo_t.1.wo_ref), custom_call_target="tpu_custom_call" | custom-call | flops 9663676416 | bytes 20447232 | tf_op jit(solution)/shard_map/d_o/pallas_call | solution.py:149
  312.6 30.4 %ln_qkv.2 = (bf16[2048,3072]{1,0:T(8,128)(2,1)}, bf16[4096,1280]{1,0:T(8,128)(2,1)}) custom-call(s32[3]{0:T(128)} %pad_add_fusion.1.idx, bf16[1024,3072]{1,0:T(8,128)(2,1)} %refs_11_.1, bf16[1024,3072]{1,0:T(8,128)(2,1)} %collective-permute-done.5.xb_ref, bf16[1,3072]{1,0:T(2,128)(2,1)} %reshape.68.lnw_ref.refs_12_, bf16[3072,3072]{1,0:T(8,128)(2,1)} %refs_8_.1, ...), custom_call_target="tpu_custom_call" | custom-call | flops 16106127360 | bytes 38273024 | tf_op jit(solution)/shard_map/ln_qkv/pallas_call | solution.py:98
  343.0 30.6 %ln_qkv.3 = (bf16[2048,3072]{1,0:T(8,128)(2,1)}, bf16[4096,1280]{1,0:T(8,128)(2,1)}) custom-call(s32[3]{0:T(128)} %pad_add_fusion.idx, bf16[1024,3072]{1,0:T(8,128)(2,1)} %collective-permute-done.xa_ref, bf16[1024,3072]{1,0:T(8,128)(2,1)} %collective-permute-done.1.xb_ref, ...), custom_call_target="tpu_custom_call", output_to_operand_aliasing={{1}: (9, {})} | custom-call | flops 16106127360 | bytes 38273024 | tf_op jit(solution)/shard_map/ln_qkv/pallas_call | solution.py:98
  373.7 102.9 %attn_fwd.1 = (bf16[4096,768]{1,0:T(8,128)(2,1)}, f32[2,16,128,768]{3,2,1,0:T(8,128)}, f32[2,16,1,768]{3,2,1,0:T(1,128)}) custom-call(bf16[4096,1280]{1,0:T(8,128)(2,1)} %get-tuple-element.44.q_ref.k_ref.v_ref, bf16[4096,1280]{1,0:T(8,128)(2,1)} %get-tuple-element.44.q_ref.k_ref.v_ref, bf16[4096,1280]{1,0:T(8,128)(2,1)} %get-tuple-element.44.q_ref.k_ref.v_ref), custom_call_target="tpu_custom_call" | custom-call | flops 51539607552 | bytes 25165824 | tf_op jit(solution)/shard_map/attn_fwd/pallas_call | solution.py:259
  476.5 17.2 %d_o.3.do_ref = bf16[4096,768]{1,0:T(8,128)(2,1)} custom-call(s32[3]{0:T(128)} %pad_add_fusion.idx, bf16[1024,3072]{1,0:T(8,128)(2,1)} %collective-permute-done.9.ga_ref.refs_1_, bf16[1024,3072]{1,0:T(8,128)(2,1)} %collective-permute-done.10.gb_ref.refs_3_, bf16[3072,768]{1,0:T(8,128)(2,1)} %wo_t.1.wo_ref, ...), custom_call_target="tpu_custom_call", output_to_operand_aliasing={{}: (4, {})} | custom-call | flops 9663676416 | bytes 20447232 | tf_op jit(solution)/shard_map/d_o/pallas_call | solution.py:149
  493.7 95.2 %attn_bwd.3.refs_1_.refs_5_ = bf16[4096,640]{1,0:T(8,128)(2,1)} custom-call(bf16[4096,1280]{1,0:T(8,128)(2,1)} %get-tuple-element.44.q_ref.k_ref.v_ref, bf16[4096,1280]{1,0:T(8,128)(2,1)} %get-tuple-element.44.q_ref.k_ref.v_ref, bf16[4096,1280]{1,0:T(8,128)(2,1)} %get-tuple-element.44.q_ref.k_ref.v_ref, bf16[4096,768]{1,0:T(8,128)(2,1)} %d_o.3.do_ref, ...), custom_call_target="tpu_custom_call" | custom-call | flops 64424509440 | bytes 25165824 | tf_op jit(solution)/shard_map/attn_bwd/pallas_call | solution.py:373
  588.9 94.8 %attn_bwd.2.refs_0_.refs_4_ = bf16[4096,640]{1,0:T(8,128)(2,1)} custom-call(bf16[4096,1280]{1,0:T(8,128)(2,1)} %get-tuple-element.44.q_ref.k_ref.v_ref, bf16[4096,1280]{1,0:T(8,128)(2,1)} %get-tuple-element.44.q_ref.k_ref.v_ref, bf16[4096,1280]{1,0:T(8,128)(2,1)} %get-tuple-element.44.q_ref.k_ref.v_ref, bf16[4096,768]{1,0:T(8,128)(2,1)} %d_o.3.do_ref, ...), custom_call_target="tpu_custom_call" | custom-call | flops 64424509440 | bytes 25165824 | tf_op jit(solution)/shard_map/attn_bwd/pallas_call | solution.py:373
  683.7 43.3 %weight_grad.3 = (bf16[3072,3072]{1,0:T(8,128)(2,1)}, bf16[3072,1024]{1,0:T(8,128)(2,1)}, bf16[3072,1024]{1,0:T(8,128)(2,1)}, bf16[3072,1280]{1,0:T(8,128)(2,1)}) custom-call(s32[5]{0:T(128)} %stack.93.idx, bf16[2048,3072]{1,0:T(8,128)(2,1)} %get-tuple-element.50.refs_0_.refs_2_, ...), custom_call_target="tpu_custom_call", output_to_operand_aliasing={{0}: (7, {}), {1}: (8, {}), {2}: (9, {})} | custom-call | flops 32212254720 | bytes 51380224 | tf_op jit(solution)/shard_map/weight_grad/pallas_call | solution.py:620
  727.1 1.8 collective-permute-start.12
  728.9 0.6 stack.92.idx
  729.7 27.3 %out_weight_grad.1 = (bf16[3072,3072]{1,0:T(8,128)(2,1)}, bf16[768,3072]{1,0:T(8,128)(2,1)}) custom-call(s32[5]{0:T(128)} %stack.93.idx, bf16[4096,768]{1,0:T(8,128)(2,1)} %get-tuple-element.45.refs_0_.o_ref, bf16[1024,3072]{1,0:T(8,128)(2,1)} %refs_0_.1, bf16[1024,3072]{1,0:T(8,128)(2,1)} %collective-permute-done.9.ga_ref.refs_1_, ...), custom_call_target="tpu_custom_call", output_to_operand_aliasing={{0}: (6, {})} | custom-call | flops 19327352832 | bytes 40894464 | tf_op jit(solution)/shard_map/out_weight_grad/pallas_call | solution.py:652
  757.0 2.1 constant_dynamic-slice_fusion.6
  759.1 1.8 collective-permute-start.6
  760.9 7.7 place.3
  768.6 74.7 %collective-permute-done.12.refs_2_.refs_4_ = bf16[4096,640]{1,0:T(8,128)(2,1)} collective-permute-done((bf16[4096,640]{1,0:T(8,128)(2,1)}, bf16[4096,640]{1,0:T(8,128)(2,1)}, u32[]{:S(2)}, u32[]{:S(2)}) %collective-permute-start.12) | collective-permute-done | bytes 5242912 | tf_op jit(solution)/shard_map/ppermute | solution.py:703
  843.3 28.1 %weight_grad.4 = (bf16[3072,3072]{1,0:T(8,128)(2,1)}, bf16[3072,1024]{1,0:T(8,128)(2,1)}, bf16[3072,1024]{1,0:T(8,128)(2,1)}, bf16[3072,640]{1,0:T(8,128)(2,1)}) custom-call(s32[5]{0:T(128)} %stack.92.idx, bf16[2048,3072]{1,0:T(8,128)(2,1)} %get-tuple-element.50.refs_0_.refs_2_, ...), custom_call_target="tpu_custom_call", output_to_operand_aliasing={{0}: (6, {}), {1}: (7, {}), {2}: (8, {})} | custom-call | flops 16106127360 | bytes 38273024 | tf_op jit(solution)/shard_map/weight_grad/pallas_call | solution.py:620
  871.4 1.8 collective-permute-start.24
  873.2 0.7 stack.44.idx
  873.9 0.6 stack.37.idx
  874.5 2.5 constant_dynamic-slice_fusion.2
  877.0 2.5 constant_dynamic-slice_fusion.3
  879.5 2.7 constant_dynamic-slice_fusion.5
  882.2 140.9 %collective-permute-done.6.refs_1_ = bf16[2048,768]{1,0:T(8,128)(2,1)} collective-permute-done((bf16[2048,768]{1,0:T(8,128)(2,1)S(1)}, bf16[2048,768]{1,0:T(8,128)(2,1)}, u32[]{:S(2)}, u32[]{:S(2)}) %collective-permute-start.6) | collective-permute-done | bytes 3145760 | tf_op jit(solution)/shard_map/ppermute | solution.py:703
  1023.1 1.5 constant_dynamic-slice_fusion.4
  1025.2 4.8 constant_dynamic-update-slice_fusion.2
  1030.0 2.5 constant_dynamic-slice_fusion
  1032.5 2.5 constant_dynamic-slice_fusion.1
  1035.5 5.7 place.4
  1041.2 28.0 %weight_grad.5 = (bf16[3072,3072]{1,0:T(8,128)(2,1)}, bf16[3072,1024]{1,0:T(8,128)(2,1)}, bf16[3072,1024]{1,0:T(8,128)(2,1)}, bf16[3072,640]{1,0:T(8,128)(2,1)}) custom-call(s32[5]{0:T(128)} %stack.44.idx, bf16[2048,3072]{1,0:T(8,128)(2,1)} %get-tuple-element.50.refs_0_.refs_2_, ...), custom_call_target="tpu_custom_call", output_to_operand_aliasing={{0}: (6, {}), {1}: (7, {}), {2}: (8, {})} | custom-call | flops 16106127360 | bytes 38273024 | tf_op jit(solution)/shard_map/weight_grad/pallas_call | solution.py:620
  1069.8 53.9 %collective-permute-done.24 = bf16[768,3072]{1,0:T(8,128)(2,1)} collective-permute-done((bf16[768,3072]{1,0:T(8,128)(2,1)}, bf16[768,3072]{1,0:T(8,128)(2,1)}, u32[]{:S(2)}, u32[]{:S(2)}) %collective-permute-start.24) | collective-permute-done | bytes 4718624 | tf_op jit(solution)/shard_map/ppermute | solution.py:703
  1124.2 54.9 %hidden_grad.1 = (bf16[1024,3072]{1,0:T(8,128)(2,1)}, f32[1,3072]{1,0:T(1,128)}) custom-call(s32[5]{0:T(128)} %stack.37.idx, bf16[4096,640]{1,0:T(8,128)(2,1)} %attn_bwd.2.refs_0_.refs_4_, bf16[4096,640]{1,0:T(8,128)(2,1)} %attn_bwd.3.refs_1_.refs_5_, bf16[4096,640]{1,0:T(8,128)(2,1)} %collective-permute-done.12.refs_2_.refs_4_, ...), custom_call_target="tpu_custom_call" | custom-call | flops 32212254720 | bytes 54525952 | tf_op jit(solution)/shard_map/hidden_grad/pallas_call | solution.py:555
  1179.2 4.8 constant_dynamic-update-slice_fusion.1
  1184.0 1.7 collective-permute-start.19
  1185.7 30.9 %out_proj.1 = bf16[1024,3072]{1,0:T(8,128)(2,1)} custom-call(s32[5]{0:T(128)} %stack.37.idx, bf16[4096,768]{1,0:T(8,128)(2,1)} %get-tuple-element.45.refs_0_.o_ref, bf16[2048,768]{1,0:T(8,128)(2,1)} %collective-permute-done.6.refs_1_, bf16[1024,768]{1,0:T(8,128)(2,1)} %collective-permute-done.7.refs_2_, bf16[1024,768]{1,0:T(8,128)(2,1)} %collective-permute-done.8.refs_3_, ...), custom_call_target="tpu_custom_call" | custom-call | flops 19327352832 | bytes 31457280 | tf_op jit(solution)/shard_map/out_proj/pallas_call | solution.py:462
  1216.6 0.6 convert_reduce_fusion
  1217.2 4.8 constant_dynamic-update-slice_fusion
  1222.1 5.7 place.5
  (54 shorter events, 3.9 us)
Async XLA Ops:
  0.6 140.0 %collective-permute-start = (bf16[1024,3072]{1,0:T(8,128)(2,1)}, bf16[1024,3072]{1,0:T(8,128)(2,1)}, u32[]{:S(2)}, u32[]{:S(2)}) collective-permute-start(bf16[1024,3072]{1,0:T(8,128)(2,1)} %refs_11_.1), channel_id=1, source_target_pairs={{0,2},{1,3},{2,0},{3,1},{4,6},{5,7},{6,4},{7,5}} | collective-permute-start | bytes 18874376 | tf_op jit(solution)/shard_map/ppermute | solution.py:703
  4.0 291.1 %collective-permute-start.9 = (bf16[1024,3072]{1,0:T(8,128)(2,1)}, bf16[1024,3072]{1,0:T(8,128)(2,1)}, u32[]{:S(2)}, u32[]{:S(2)}) collective-permute-start(bf16[1024,3072]{1,0:T(8,128)(2,1)} %refs_0_.1), channel_id=1, source_target_pairs={{0,2},{1,3},{2,0},{3,1},{4,6},{5,7},{6,4},{7,5}} | collective-permute-start | bytes 18874376 | tf_op jit(solution)/shard_map/ppermute | solution.py:703
  4.0 291.5 %collective-permute-start.11 = (bf16[1024,3072]{1,0:T(8,128)(2,1)}, bf16[1024,3072]{1,0:T(8,128)(2,1)}, u32[]{:S(2)}, u32[]{:S(2)}) collective-permute-start(bf16[1024,3072]{1,0:T(8,128)(2,1)} %refs_0_.1), channel_id=1, source_target_pairs={{0,1},{1,0},{2,3},{3,2},{4,5},{5,4},{6,7},{7,6}} | collective-permute-start | bytes 18874376 | tf_op jit(solution)/shard_map/ppermute | solution.py:706
  4.0 308.6 %collective-permute-start.5 = (bf16[1024,3072]{1,0:T(8,128)(2,1)}, bf16[1024,3072]{1,0:T(8,128)(2,1)}, u32[]{:S(2)}, u32[]{:S(2)}) collective-permute-start(bf16[1024,3072]{1,0:T(8,128)(2,1)} %refs_11_.1), channel_id=1, source_target_pairs={{0,1},{1,0},{2,3},{3,2},{4,5},{5,4},{6,7},{7,6}} | collective-permute-start | bytes 18874376 | tf_op jit(solution)/shard_map/ppermute | solution.py:706
  140.6 202.4 %collective-permute-start.1 = (bf16[1024,3072]{1,0:T(8,128)(2,1)}, bf16[1024,3072]{1,0:T(8,128)(2,1)}, u32[]{:S(2)}, u32[]{:S(2)}) collective-permute-start(bf16[1024,3072]{1,0:T(8,128)(2,1)} %collective-permute-done.xa_ref), channel_id=1, source_target_pairs={{0,1},{1,0},{2,3},{3,2},{4,5},{5,4},{6,7},{7,6}} | collective-permute-start | bytes 18874376 | tf_op jit(solution)/shard_map/ppermute | solution.py:706
  140.6 134.0 %collective-permute-start.3 = (s32[1024]{0:T(1024)}, s32[1024]{0:T(1024)S(1)}, u32[]{:S(2)}, u32[]{:S(2)}) collective-permute-start(s32[1024]{0:T(1024)} %param.9), channel_id=1, source_target_pairs={{0,2},{1,3},{2,0},{3,1},{4,6},{5,7},{6,4},{7,5}} | collective-permute-start | bytes 12296 | tf_op jit(solution)/shard_map/ppermute | solution.py:703
  274.7 1.4 collective-permute-start.2
  276.0 9.6 collective-permute-start.4
  279.0 6.6 copy-start.2
  295.1 181.4 %collective-permute-start.10 = (bf16[1024,3072]{1,0:T(8,128)(2,1)}, bf16[1024,3072]{1,0:T(8,128)(2,1)}, u32[]{:S(2)}, u32[]{:S(2)}) collective-permute-start(bf16[1024,3072]{1,0:T(8,128)(2,1)} %collective-permute-done.9.ga_ref.refs_1_), channel_id=1, source_target_pairs={{0,1},{1,0},{2,3},{3,2},{4,5},{5,4},{6,7},{7,6}} | collective-permute-start | bytes 18874376 | tf_op jit(solution)/shard_map/ppermute | solution.py:706
  727.0 33.9 %collective-permute-start.20 = (bf16[3072,1280]{1,0:T(8,128)(2,1)}, bf16[3072,1280]{1,0:T(8,128)(2,1)}, u32[]{:S(2)}, u32[]{:S(2)}) collective-permute-start(bf16[3072,1280]{1,0:T(8,128)(2,1)} %get-tuple-element.55), channel_id=1, source_target_pairs={{0,1},{1,0},{2,3},{3,2},{4,5},{5,4},{6,7},{7,6}} | collective-permute-start | bytes 23592968 | tf_op jit(solution)/shard_map/ppermute | solution.py:706
  727.1 116.2 %collective-permute-start.12 = (bf16[4096,640]{1,0:T(8,128)(2,1)}, bf16[4096,640]{1,0:T(8,128)(2,1)}, u32[]{:S(2)}, u32[]{:S(2)}) collective-permute-start(bf16[4096,640]{1,0:T(8,128)(2,1)} %attn_bwd.2.refs_0_.refs_4_), channel_id=1, source_target_pairs={{0,2},{1,3},{2,0},{3,1},{4,6},{5,7},{6,4},{7,5}} | collective-permute-start | bytes 15728648 | tf_op jit(solution)/shard_map/ppermute | solution.py:703
  729.5 300.5 %collective-permute-start.13 = (bf16[4096,640]{1,0:T(8,128)(2,1)}, bf16[4096,640]{1,0:T(8,128)(2,1)}, u32[]{:S(2)}, u32[]{:S(2)}) collective-permute-start(bf16[4096,640]{1,0:T(8,128)(2,1)} %attn_bwd.3.refs_1_.refs_5_), channel_id=1, source_target_pairs={{0,2},{1,3},{2,0},{3,1},{4,6},{5,7},{6,4},{7,5}} | collective-permute-start | bytes 15728648 | tf_op jit(solution)/shard_map/ppermute | solution.py:703
  757.0 267.6 %collective-permute-start.23 = (bf16[768,3072]{1,0:T(8,128)(2,1)}, bf16[768,3072]{1,0:T(8,128)(2,1)}, u32[]{:S(2)}, u32[]{:S(2)}) collective-permute-start(bf16[768,3072]{1,0:T(8,128)(2,1)} %get-tuple-element.78), channel_id=1, source_target_pairs={{0,1},{1,0},{2,3},{3,2},{4,5},{5,4},{6,7},{7,6}} | collective-permute-start | bytes 14155784 | tf_op jit(solution)/shard_map/ppermute | solution.py:706
  759.1 264.0 %collective-permute-start.6 = (bf16[2048,768]{1,0:T(8,128)(2,1)S(1)}, bf16[2048,768]{1,0:T(8,128)(2,1)}, u32[]{:S(2)}, u32[]{:S(2)}) collective-permute-start(bf16[2048,768]{1,0:T(8,128)(2,1)S(1)} %constant_dynamic-slice_fusion.6), channel_id=1, source_target_pairs={{0,2},{1,3},{2,0},{3,1},{4,6},{5,7},{6,4},{7,5}} | collective-permute-start | bytes 9437192 | tf_op jit(solution)/shard_map/ppermute | solution.py:703
  871.4 163.6 %collective-permute-start.21 = (bf16[3072,640]{1,0:T(8,128)(2,1)}, bf16[3072,640]{1,0:T(8,128)(2,1)}, u32[]{:S(2)}, u32[]{:S(2)}) collective-permute-start(bf16[3072,640]{1,0:T(8,128)(2,1)} %get-tuple-element.62), channel_id=1, source_target_pairs={{0,1},{1,0},{2,3},{3,2},{4,5},{5,4},{6,7},{7,6}} | collective-permute-start | bytes 11796488 | tf_op jit(solution)/shard_map/ppermute | solution.py:706
  871.4 252.2 %collective-permute-start.24 = (bf16[768,3072]{1,0:T(8,128)(2,1)}, bf16[768,3072]{1,0:T(8,128)(2,1)}, u32[]{:S(2)}, u32[]{:S(2)}) collective-permute-start(bf16[768,3072]{1,0:T(8,128)(2,1)} %get-tuple-element.78), channel_id=1, source_target_pairs={{0,2},{1,3},{2,0},{3,1},{4,6},{5,7},{6,4},{7,5}} | collective-permute-start | bytes 14155784 | tf_op jit(solution)/shard_map/ppermute | solution.py:703
  1023.1 46.1 %collective-permute-start.15 = (bf16[1024,640]{1,0:T(8,128)(2,1)}, bf16[1024,640]{1,0:T(8,128)(2,1)}, u32[]{:S(2)}, u32[]{:S(2)}) collective-permute-start(bf16[1024,640]{1,0:T(8,128)(2,1)} %constant_dynamic-slice_fusion.2), channel_id=1, source_target_pairs={{0,1},{1,0},{2,3},{3,2},{4,5},{5,4},{6,7},{7,6}} | collective-permute-start | bytes 3932168 | tf_op jit(solution)/shard_map/ppermute | solution.py:706
  1024.6 44.7 %collective-permute-start.14 = (bf16[1024,640]{1,0:T(8,128)(2,1)}, bf16[1024,640]{1,0:T(8,128)(2,1)}, u32[]{:S(2)}, u32[]{:S(2)}) collective-permute-start(bf16[1024,640]{1,0:T(8,128)(2,1)} %constant_dynamic-slice_fusion.3), channel_id=1, source_target_pairs={{0,1},{1,0},{2,3},{3,2},{4,5},{5,4},{6,7},{7,6}} | collective-permute-start | bytes 3932168 | tf_op jit(solution)/shard_map/ppermute | solution.py:706
  1032.5 91.1 %collective-permute-start.17 = (bf16[1024,640]{1,0:T(8,128)(2,1)}, bf16[1024,640]{1,0:T(8,128)(2,1)}, u32[]{:S(2)}, u32[]{:S(2)}) collective-permute-start(bf16[1024,640]{1,0:T(8,128)(2,1)} %constant_dynamic-slice_fusion), channel_id=1, source_target_pairs={{0,1},{1,0},{2,3},{3,2},{4,5},{5,4},{6,7},{7,6}} | collective-permute-start | bytes 3932168 | tf_op jit(solution)/shard_map/ppermute | solution.py:706
  1035.0 89.1 %collective-permute-start.16 = (bf16[1024,640]{1,0:T(8,128)(2,1)}, bf16[1024,640]{1,0:T(8,128)(2,1)}, u32[]{:S(2)}, u32[]{:S(2)}) collective-permute-start(bf16[1024,640]{1,0:T(8,128)(2,1)} %constant_dynamic-slice_fusion.1), channel_id=1, source_target_pairs={{0,1},{1,0},{2,3},{3,2},{4,5},{5,4},{6,7},{7,6}} | collective-permute-start | bytes 3932168 | tf_op jit(solution)/shard_map/ppermute | solution.py:706
  1041.2 28.0 %copy-start = (bf16[1024,768]{1,0:T(8,128)(2,1)S(1)}, bf16[1024,768]{1,0:T(8,128)(2,1)}, u32[]{:S(2)}) copy-start(bf16[1024,768]{1,0:T(8,128)(2,1)} %constant_dynamic-slice_fusion.5) | copy-start | bytes 4718596
  1069.3 116.5 %collective-permute-start.7 = (bf16[1024,768]{1,0:T(8,128)(2,1)S(1)}, bf16[1024,768]{1,0:T(8,128)(2,1)}, u32[]{:S(2)}, u32[]{:S(2)}) collective-permute-start(bf16[1024,768]{1,0:T(8,128)(2,1)S(1)} %copy-done), channel_id=1, source_target_pairs={{0,1},{1,0},{2,3},{3,2},{4,5},{5,4},{6,7},{7,6}} | collective-permute-start | bytes 4718600 | tf_op jit(solution)/shard_map/ppermute | solution.py:706
  1069.3 116.4 %collective-permute-start.8 = (bf16[1024,768]{1,0:T(8,128)(2,1)S(1)}, bf16[1024,768]{1,0:T(8,128)(2,1)}, u32[]{:S(2)}, u32[]{:S(2)}) collective-permute-start(bf16[1024,768]{1,0:T(8,128)(2,1)S(1)} %constant_dynamic-slice_fusion.4), channel_id=1, source_target_pairs={{0,1},{1,0},{2,3},{3,2},{4,5},{5,4},{6,7},{7,6}} | collective-permute-start | bytes 4718600 | tf_op jit(solution)/shard_map/ppermute | solution.py:706
  1123.7 93.6 %collective-permute-start.25 = (bf16[768,3072]{1,0:T(8,128)(2,1)}, bf16[768,3072]{1,0:T(8,128)(2,1)}, u32[]{:S(2)}, u32[]{:S(2)}) collective-permute-start(bf16[768,3072]{1,0:T(8,128)(2,1)} %collective-permute-done.24), channel_id=1, source_target_pairs={{0,1},{1,0},{2,3},{3,2},{4,5},{5,4},{6,7},{7,6}} | collective-permute-start | bytes 14155784 | tf_op jit(solution)/shard_map/ppermute | solution.py:706
  1123.7 98.4 %collective-permute-start.22 = (bf16[3072,640]{1,0:T(8,128)(2,1)}, bf16[3072,640]{1,0:T(8,128)(2,1)}, u32[]{:S(2)}, u32[]{:S(2)}) collective-permute-start(bf16[3072,640]{1,0:T(8,128)(2,1)} %get-tuple-element.69), channel_id=1, source_target_pairs={{0,1},{1,0},{2,3},{3,2},{4,5},{5,4},{6,7},{7,6}} | collective-permute-start | bytes 11796488 | tf_op jit(solution)/shard_map/ppermute | solution.py:706
  1179.1 4.9 copy-start.1
  1179.1 4.9 collective-permute-start.18
  1184.0 32.6 %collective-permute-start.19 = (f32[1,3072]{1,0:T(1,128)S(1)}, f32[1,3072]{1,0:T(1,128)S(1)}, u32[]{:S(2)}, u32[]{:S(2)}) collective-permute-start(f32[1,3072]{1,0:T(1,128)S(1)} %add.58), channel_id=1, source_target_pairs={{0,2},{1,3},{2,0},{3,1},{4,6},{5,7},{6,4},{7,5}} | collective-permute-start | bytes 36872 | tf_op jit(solution)/shard_map/ppermute | solution.py:703
